TPU v7x, 32 devices: a whole 2x2x4 slice. The times are simulated.
32 devices in a mesh: row: 8 (over y, x, core), col: 4 (over z).
Axes of the slice: x: 2, y: 2, z: 4, core: 2. Of those that a mesh axis runs over, the one named last changes fastest.
Arguments:
- jacobian: float32 [2, 4096, 256], P(None, ('row', 'col')), may hold values from -0.25 to 0.25
Outputs:
- normal_tiles: float32 [8, 2, 4, 512, 512], P('row', None, 'col')
All inputs are finite; a program needn't handle non-finite values.
Results may differ from a plain program's by a relative error of at most 0.0003.
Values sent between devices are 32-bit elements; how exact they have to be, the bound alone decides.
No kernel may reach another device: no remote copies, remote signals or barrier semaphores. Data moves between devices by JAX's collectives and lax.ppermute only.
A program may use at most 64 MiB of HBM per device.

v0:
```python
import jax
import jax.numpy as jnp
from jax import lax
from jax.sharding import PartitionSpec as P


def from_partner(block, axis, distance):
    count = lax.axis_size(axis)
    route = []
    for low in range(count):
        high = low | 1 << distance
        if high != low and high < count:
            route += [(low, high), (high, low)]
    return lax.ppermute(block, axis, route)


def partner_rows(block, bit_number):
    return from_partner(block, ("row", "col"), bit_number)


def body(jacobian):
    row_index = lax.axis_index("row")
    col_index = lax.axis_index("col")
    col_count = lax.axis_size("col")
    cycles = lax.axis_size("row") // col_count
    panel_count = jacobian.shape[0]
    width = jacobian.shape[2]
    own_tile = lax.all_gather(jacobian, "col", axis=1, tiled=True)
    tile_size = own_tile.shape[1]
    col_bits = col_count.bit_length() - 1
    low_row = row_index % col_count
    moved = jacobian
    for bit_number in range(col_bits):
        first = partner_rows(moved, bit_number)
        second = partner_rows(first, bit_number + col_bits)
        differ = low_row >> bit_number & 1 != col_index >> bit_number & 1
        moved = jnp.where(differ, second, moved)
    gathered = lax.all_gather(moved, "row", axis=1, tiled=True)
    gathered = gathered.reshape(panel_count, cycles, tile_size, width)
    partners = [gathered[:, turn_index] for turn_index in range(cycles)]

    def product(partner):
        return jnp.einsum("pak,pbk->ab", own_tile, partner, precision=lax.Precision.HIGHEST)

    def empty_tile(partner):
        return jnp.zeros((tile_size, tile_size), jnp.float32)

    results = []
    for turn_index in range(cycles):
        column_tile = col_index + col_count * turn_index
        results.append(
            lax.cond(column_tile <= row_index, product, empty_tile, partners[turn_index])
        )
    blocks = jnp.stack(results, 0)
    return blocks[None, :, None]


def solution(mesh):
    in_specs = (P(None, ("row", "col"), None),)
    out_specs = P("row", None, "col", None, None)
    return jax.shard_map(body, mesh=mesh, in_specs=in_specs, out_specs=out_specs, check_vma=False)
```

profile of v0, /device:TPU:4, one launch (start us, length us, event | category | flops | bytes accessed | tf_op | source)
XLA Modules:
  0.0 115.7 jit_solution(6772489944896085306)
XLA Ops:
  6.5 0.0 all-gather.3.cloned.1.call-start
  6.5 1.6 %collective-permute-start = (f32[2,128,256]{2,1,0:T(8,128)}, f32[2,128,256]{2,1,0:T(8,128)S(1)}, u32[]{:S(2)}, u32[]{:S(2)}) collective-permute-start(f32[2,128,256]{2,1,0:T(8,128)} %param.5), channel_id=1, source_target_pairs={{0,1},{1,0},{2,3},{3,2},{4,5},{5,4},{6,7},{7,6},{8,9},{9,8},{10,11... | collective-permute-start | bytes 786440 | tf_op jit(solution)/shard_map/ppermute | solution.py:14
  8.1 6.7 %collective-permute-done = f32[2,128,256]{2,1,0:T(8,128)S(1)} collective-permute-done((f32[2,128,256]{2,1,0:T(8,128)}, f32[2,128,256]{2,1,0:T(8,128)S(1)}, u32[]{:S(2)}, u32[]{:S(2)}) %collective-permute-start) | collective-permute-done | bytes 262176 | tf_op jit(solution)/shard_map/ppermute | solution.py:14
  14.8 0.0 collective-permute-start.1
  14.8 1.5 %collective-permute-done.1 = f32[2,128,256]{2,1,0:T(8,128)S(1)} collective-permute-done((f32[2,128,256]{2,1,0:T(8,128)S(1)}, f32[2,128,256]{2,1,0:T(8,128)S(1)}, u32[]{:S(2)}, u32[]{:S(2)}) %collective-permute-start.1) | collective-permute-done | bytes 262176 | tf_op jit(solution)/shard_map/ppermute | solution.py:14
  16.3 1.0 broadcast_select_fusion
  17.3 2.7 %collective-permute-start.2 = (f32[2,128,256]{2,1,0:T(8,128)S(1)}, f32[2,128,256]{2,1,0:T(8,128)S(1)}, u32[]{:S(2)}, u32[]{:S(2)}) collective-permute-start(f32[2,128,256]{2,1,0:T(8,128)S(1)} %broadcast_select_fusion), channel_id=1, source_target_pairs={{0,2},{2,0},{1,3},{3,1},{4,6},{6,4},{5,7},{7,5},{8,10},{10,8},{9,1... | collective-permute-start | bytes 786440 | tf_op jit(solution)/shard_map/ppermute | solution.py:14
  20.0 11.3 %collective-permute-done.2 = f32[2,128,256]{2,1,0:T(8,128)S(1)} collective-permute-done((f32[2,128,256]{2,1,0:T(8,128)S(1)}, f32[2,128,256]{2,1,0:T(8,128)S(1)}, u32[]{:S(2)}, u32[]{:S(2)}) %collective-permute-start.2) | collective-permute-done | bytes 262176 | tf_op jit(solution)/shard_map/ppermute | solution.py:14
  31.3 1.5 %collective-permute-start.3 = (f32[2,128,256]{2,1,0:T(8,128)S(1)}, f32[2,128,256]{2,1,0:T(8,128)S(1)}, u32[]{:S(2)}, u32[]{:S(2)}) collective-permute-start(f32[2,128,256]{2,1,0:T(8,128)S(1)} %collective-permute-done.2), channel_id=1, source_target_pairs={{0,8},{8,0},{1,9},{9,1},{2,10},{10,2},{3,11},{11,3},{4,12},{12,4},... | collective-permute-start | bytes 786440 | tf_op jit(solution)/shard_map/ppermute | solution.py:14
  32.8 5.1 %collective-permute-done.3 = f32[2,128,256]{2,1,0:T(8,128)S(1)} collective-permute-done((f32[2,128,256]{2,1,0:T(8,128)S(1)}, f32[2,128,256]{2,1,0:T(8,128)S(1)}, u32[]{:S(2)}, u32[]{:S(2)}) %collective-permute-start.3) | collective-permute-done | bytes 262176 | tf_op jit(solution)/shard_map/ppermute | solution.py:14
  37.8 0.7 broadcast_select_fusion.1
  38.6 0.0 all-gather.3.cloned.1.call-update
  38.6 0.0 all-gather.5.cloned.1.call-start
  38.7 0.7 all-gather.5.cloned.1.call-update
  39.4 30.0 %all-gather.3.cloned.1.call-done = f32[2,1024,256]{2,1,0:T(8,128)} async-done(((f32[2,128,256]{2,1,0:T(8,128)}), f32[2,1024,256]{2,1,0:T(8,128)}) %all-gather.3.cloned.1.call-update) | async-done | bytes 2097168 | tf_op jit(solution)/shard_map/all_gather | solution.py:38
  69.3 1.7 %copy.2 = f32[2,2,512,256]{3,2,0,1:T(8,128)S(1)} copy(f32[2,2,512,256]{3,2,1,0:T(8,128)} %bitcast.17) | data formatting | bytes 4194304 | tf_op jit(solution)/shard_map/cond | solution.py:52
  71.1 27.9 %all-gather.5.cloned.1.call-done = f32[2,512,256]{2,1,0:T(8,128)} async-done(((f32[2,128,256]{2,1,0:T(8,128)}), f32[2,512,256]{2,1,0:T(8,128)}) %all-gather.5.cloned.1.call-update) | async-done | bytes 1048592 | tf_op jit(solution)/shard_map/all_gather | solution.py:28
  99.0 3.1 %conditional.3 = (f32[1,512,512]{2,1,0:T(8,128)S(1)}) conditional(s32[]{:T(128)} %convert_element_type.7, () %tuple.23, (f32[2,2,512,256]{3,2,0,1:T(8,128)S(1)}, f32[2,512,256]{2,1,0:T(8,128)}) %tuple.24), branch_computations={%region_2.3_spmd, %region_3.4_spmd} | conditional | flops 1610612736 | bytes 3145736 | solution.py:52
  99.0 3.1 %convolution_bitcast_fusion.1 = f32[1,512,512]{2,1,0:T(8,128)S(1)} fusion(f32[2,512,256]{2,1,0:T(8,128)} %get-tuple-element.27, f32[2,2,512,256]{3,2,0,1:T(8,128)S(1)} %get-tuple-element.28), kind=kOutput, calls=%fused_computation.3 | convolution fusion | flops 1610612736 | bytes 3145728 | tf_op jit(solution)/shard_map/cond/branch_1_fun/pak,pbk->ab/dot_general | solution.py:43
  102.1 4.1 %conditional.2 = (f32[1,512,512]{2,1,0:T(8,128)}) conditional(s32[]{:T(128)} %convert_element_type.6, () %tuple.21, (f32[2,2,512,256]{3,2,0,1:T(8,128)S(1)}, f32[2,512,256]{2,1,0:T(8,128)}) %tuple.24), branch_computations={%region_0.1_spmd, %region_1.2_spmd} | conditional | flops 1610612736 | bytes 3145736 | solution.py:52
  102.1 4.1 %convolution_bitcast_fusion = f32[1,512,512]{2,1,0:T(8,128)} fusion(f32[2,512,256]{2,1,0:T(8,128)} %get-tuple-element.25, f32[2,2,512,256]{3,2,0,1:T(8,128)S(1)} %get-tuple-element.26), kind=kOutput, calls=%fused_computation | convolution fusion | flops 1610612736 | bytes 3145728 | tf_op jit(solution)/shard_map/cond/branch_1_fun/pak,pbk->ab/dot_general | solution.py:43
  106.2 2.7 %maximum_bitcast_fusion = f32[1,2,1,512,512]{4,3,2,1,0:T(8,128)} fusion(f32[1,512,512]{2,1,0:T(8,128)S(1)} %get-tuple-element.34, f32[1,512,512]{2,1,0:T(8,128)} %get-tuple-element.33), kind=kLoop, calls=%fused_computation.6 | loop fusion | flops 524288 | bytes 4194304 | tf_op jit(solution)/shard_map/broadcast_in_dim | solution.py:55
Async XLA Ops:
  6.5 62.8 %all-gather.3.cloned.1.call-start = ((), (), s32[]{:S(2)}) async-start(), calls=%async_computation | async-start | bytes 2359296 | tf_op jit(solution)/shard_map/all_gather | solution.py:38
  6.5 8.3 %collective-permute-start = (f32[2,128,256]{2,1,0:T(8,128)}, f32[2,128,256]{2,1,0:T(8,128)S(1)}, u32[]{:S(2)}, u32[]{:S(2)}) collective-permute-start(f32[2,128,256]{2,1,0:T(8,128)} %param.5), channel_id=1, source_target_pairs={{0,1},{1,0},{2,3},{3,2},{4,5},{5,4},{6,7},{7,6},{8,9},{9,8},{10,11... | collective-permute-start | bytes 786440 | tf_op jit(solution)/shard_map/ppermute | solution.py:14
  14.8 1.5 %collective-permute-start.1 = (f32[2,128,256]{2,1,0:T(8,128)S(1)}, f32[2,128,256]{2,1,0:T(8,128)S(1)}, u32[]{:S(2)}, u32[]{:S(2)}) collective-permute-start(f32[2,128,256]{2,1,0:T(8,128)S(1)} %collective-permute-done), channel_id=1, source_target_pairs={{0,4},{4,0},{1,5},{5,1},{2,6},{6,2},{3,7},{7,3},{8,12},{12,8},{9,1... | collective-permute-start | bytes 786440 | tf_op jit(solution)/shard_map/ppermute | solution.py:14
  17.3 14.0 %collective-permute-start.2 = (f32[2,128,256]{2,1,0:T(8,128)S(1)}, f32[2,128,256]{2,1,0:T(8,128)S(1)}, u32[]{:S(2)}, u32[]{:S(2)}) collective-permute-start(f32[2,128,256]{2,1,0:T(8,128)S(1)} %broadcast_select_fusion), channel_id=1, source_target_pairs={{0,2},{2,0},{1,3},{3,1},{4,6},{6,4},{5,7},{7,5},{8,10},{10,8},{9,1... | collective-permute-start | bytes 786440 | tf_op jit(solution)/shard_map/ppermute | solution.py:14
  31.3 6.5 %collective-permute-start.3 = (f32[2,128,256]{2,1,0:T(8,128)S(1)}, f32[2,128,256]{2,1,0:T(8,128)S(1)}, u32[]{:S(2)}, u32[]{:S(2)}) collective-permute-start(f32[2,128,256]{2,1,0:T(8,128)S(1)} %collective-permute-done.2), channel_id=1, source_target_pairs={{0,8},{8,0},{1,9},{9,1},{2,10},{10,2},{3,11},{11,3},{4,12},{12,4},... | collective-permute-start | bytes 786440 | tf_op jit(solution)/shard_map/ppermute | solution.py:14
  38.6 60.4 %all-gather.5.cloned.1.call-start = ((), (), s32[]{:S(2)}) async-start(), calls=%async_computation.1 | async-start | bytes 1310720 | tf_op jit(solution)/shard_map/all_gather | solution.py:28
Sparse Core Ops, SparseCore 0:
  38.7 30.5 all-gather.2
  70.9 28.0 all-gather.4
where the time goes:
time: 116 us
  waiting for transfers between devices  83.2 us (72%)
  between operations  13.4 us (12%)
  matrix products  7.14 us (6%)
  starting transfers between devices  5.77 us (5%)
  other arithmetic  4.43 us (4%)
  local copies, waits for them, and re-layouts  1.73 us (1%)
    all_gather x1, waiting for transfers between devices, body(): gathered = lax.all_gather(moved, 'row', axis=1, tiled=True)  30 us
    all_gather x1, waiting for transfers between devices, body(): own_tile = lax.all_gather(jacobian, 'col', axis=1, tiled=True)  27.9 us
    ppermute x4, waiting for transfers between devices, from_partner(): return lax.ppermute(block, axis, route)  24.6 us
    dot_general x2, matrix products, product(): jnp.einsum('pak,pbk->ab', own_tile, partner, precision=lax.Precision.HIGH...  7.14 us
    ppermute x4, starting transfers between devices, from_partner(): return lax.ppermute(block, axis, route)  5.72 us
    broadcast_in_dim x1, other arithmetic, body(): return blocks[None, :, None]  2.71 us
  transfers between devices with their start and end apart: 6, of which 6 were waited for; matrix products, arithmetic and copies ran while one was open for 1% of the time, Pallas kernels for 0%

commit v1 on v0

v1 whole, which is shorter than its diff:
```python
import jax
import jax.numpy as jnp
from jax import lax
from jax.experimental import pallas as pl
from jax.experimental.pallas import tpu as pltpu
from jax.sharding import PartitionSpec as P


def swap(block, bits):
    count = lax.axis_size("row")
    return lax.ppermute(block, "row", [(low, low ^ bits) for low in range(count)])


def shift(block, distance):
    count = lax.axis_size("col")
    return lax.ppermute(block, "col", [(low, (low + distance) % count) for low in range(count)])


def transposed(block, skew):
    rows, cols = lax.axis_size("row"), lax.axis_size("col")
    route = []
    for row in range(rows):
        for col in range(cols):
            target = row // cols * cols + (col + skew) % cols
            route.append((row * cols + col, target * cols + row % cols))
    return lax.ppermute(block, ("row", "col"), route)


def body(jacobian):
    rows, cols = lax.axis_size("row"), lax.axis_size("col")
    cycles = rows // cols
    panels, depth, width = jacobian.shape
    tile = depth * cols
    half = panels // 2
    skew = cols // 2
    moved = [transposed(jacobian[:half], 0), transposed(jacobian[half:], skew)]
    near = [shift(jacobian, distance) for distance in range(1, cols)]
    bits = [1 << number for number in range(rows.bit_length() - 1)]
    first, second = bits[1], bits[2]
    low, high = moved
    low_first, high_first = swap(low, first), swap(high, first)
    low_second, high_second = swap(low, second), swap(high, second)
    low_far, high_far = swap(low_first, second), swap(high_second, first)
    held = [
        (0, 0, low), (0, 1, high),
        (first, 0, low_first), (first, 1, high_first),
        (second, 0, low_second), (second, 1, high_second),
        (first | second, 0, low_far), (first | second, 1, high_far),
    ]
    for bit in bits[:1] + bits[3:]:
        held += [(distance ^ bit, part, swap(block, bit)) for distance, part, block in held]
    pieces = [block for _, _, block in held]
    kinds = [(distance, part) for distance, part, _ in held]

    def kernel(position, own, *refs):
        shifted = refs[: cols - 1]
        columns = refs[cols - 1 : cols - 1 + len(pieces)]
        out, row_hi, row_lo, col_hi, col_lo = refs[cols - 1 + len(pieces) :]
        row_index, col_index = position[0], position[1]

        def split(value, hi, lo, lead, start, lane):
            top = value.astype(jnp.bfloat16)
            rest = (value - top.astype(jnp.float32)).astype(jnp.bfloat16)
            where = pl.ds(pl.multiple_of(start, depth), depth)
            hi[lead, where, lane * width : (lane + 1) * width] = top
            lo[lead, where, lane * width : (lane + 1) * width] = rest

        for distance, source in enumerate((own,) + tuple(shifted)):
            start = lax.rem(col_index - distance + cols, cols) * depth
            for panel in range(panels):
                split(source[panel], row_hi, row_lo, 0, start, panel)
        for (distance, part), source in zip(kinds, columns):
            holder = row_index ^ distance
            turn = holder // cols
            slot = lax.rem(holder - turn * cols - part * skew + cols, cols)
            for panel in range(half):
                split(source[panel], col_hi, col_lo, turn, slot * depth, part * half + panel)

        def dot(left, right):
            return lax.dot_general(
                left, right, (((1,), (1,)), ((), ())), preferred_element_type=jnp.float32
            )

        for turn in range(cycles):
            wanted = turn * cols + col_index <= row_index

            @pl.when(wanted)
            def _():
                out[0, turn, 0] = (
                    dot(row_hi[0], col_lo[turn]) + dot(row_lo[0], col_hi[turn])
                ) + dot(row_hi[0], col_hi[turn])

            @pl.when(jnp.logical_not(wanted))
            def _():
                out[0, turn, 0] = jnp.zeros((tile, tile), jnp.float32)

    position = jnp.stack([lax.axis_index("row"), lax.axis_index("col")]).astype(jnp.int32)
    vmem = pl.BlockSpec(memory_space=pltpu.VMEM)
    return pl.pallas_call(
        kernel,
        out_shape=jax.ShapeDtypeStruct((1, cycles, 1, tile, tile), jnp.float32),
        in_specs=[pl.BlockSpec(memory_space=pltpu.SMEM)] + [vmem] * (cols + len(pieces)),
        out_specs=vmem,
        scratch_shapes=[
            pltpu.VMEM((1, tile, panels * width), jnp.bfloat16),
            pltpu.VMEM((1, tile, panels * width), jnp.bfloat16),
            pltpu.VMEM((cycles, tile, panels * width), jnp.bfloat16),
            pltpu.VMEM((cycles, tile, panels * width), jnp.bfloat16),
        ],
        compiler_params=pltpu.CompilerParams(vmem_limit_bytes=24 << 20),
        cost_estimate=pl.CostEstimate(
            flops=6 * cycles * tile * tile * panels * width,
            bytes_accessed=4 * cycles * tile * tile * 2,
            transcendentals=0,
        ),
    )(position, jacobian, *near, *pieces)


def solution(mesh):
    in_specs = (P(None, ("row", "col"), None),)
    out_specs = P("row", None, "col", None, None)
    return jax.shard_map(body, mesh=mesh, in_specs=in_specs, out_specs=out_specs, check_vma=False)
```

time: 116 us -> 50.3 us (0.43)
  waiting for transfers between devices: 83.2 us -> 29.9 us
  between operations: 13.4 us -> 0.04 us
  starting transfers between devices: 5.77 us -> 13.1 us
  matrix products: 7.14 us -> 0 us
  other arithmetic: 4.43 us -> 0.07 us
  Pallas kernels: 0 us -> 4.31 us
    all_gather x2 -> x0, waiting for transfers between devices: 57.9 us -> none  [the longest x1 30 us: body(): gathered = lax.all_gather(moved, 'row', axis=1, tiled=True)]
    ppermute x4 -> x19, starting transfers between devices: 5.72 us -> 13.1 us  [the longest x3 7.12 us: shift(): lax.ppermute(block, 'col', [(low, (low + distance) % count) for low in ra...]
    dot_general x2 -> x0, matrix products: 7.14 us -> none  [product(): jnp.einsum('pak,pbk->ab', own_tile, partner, precision=lax.Precision.HIGH...]
    ppermute x4 -> x19, waiting for transfers between devices: 24.6 us -> 29.9 us  [the longest x3 14.8 us: shift(): lax.ppermute(block, 'col', [(low, (low + distance) % count) for low in ra...]
    pallas_call x0 -> x1, Pallas kernels: none -> 4.31 us  [body(): pl.pallas_call(kernel, out_shape=jax.ShapeDtypeStruct((1, cycles, 1, tile...]
    broadcast_in_dim x1 -> x0, other arithmetic: 2.71 us -> none  [body(): return blocks[None, :, None]]
    cond x1 -> x0, local copies, waits for them, and re-layouts: 1.73 us -> none  [body(): lax.cond(column_tile <= row_index, product, empty_tile, partners[turn_ind...]
    select_n x2 -> x0, other arithmetic: 1.72 us -> none  [body(): moved = jnp.where(differ, second, moved)]
  transfers between devices with their start and end apart: 6 -> 19, of which waited for: 6 -> 9; matrix products, arithmetic and copies ran while one was open for 1% -> 0% of each run, Pallas kernels for 0% -> 0%
where the time goes in v1:
time: 50.3 us; the launch traced here: 49.4 us
  waiting for transfers between devices  29.9 us (59%)
  starting transfers between devices  13.1 us (26%)
  Pallas kernels  4.31 us (9%)
  local copies, waits for them, and re-layouts  1.94 us (4%)
    ppermute x3, waiting for transfers between devices, shift(): lax.ppermute(block, 'col', [(low, (low + distance) % count) for low in ra...  14.8 us
    ppermute x2, waiting for transfers between devices, transposed(): return lax.ppermute(block, ('row', 'col'), route)  9.3 us
    ppermute x3, starting transfers between devices, shift(): lax.ppermute(block, 'col', [(low, (low + distance) % count) for low in ra...  7.12 us
    ppermute x14, waiting for transfers between devices, swap(): lax.ppermute(block, 'row', [(low, low ^ bits) for low in range(count)])  5.81 us
    pallas_call x1, Pallas kernels, body(): pl.pallas_call(kernel, out_shape=jax.ShapeDtypeStruct((1, cycles, 1, tile...  4.31 us
    ppermute x14, starting transfers between devices, swap(): lax.ppermute(block, 'row', [(low, low ^ bits) for low in range(count)])  3.82 us
    ppermute x2, starting transfers between devices, transposed(): return lax.ppermute(block, ('row', 'col'), route)  2.2 us
  transfers between devices with their start and end apart: 19, of which 9 were waited for; matrix products, arithmetic and copies ran while one was open for 0% of the time, Pallas kernels for 0%

profile of v1, /device:TPU:4, one launch (start us, length us, event | category | flops | bytes accessed | tf_op | source)
XLA Modules:
  0.0 49.4 jit_solution(17321693221134987056)
XLA Ops:
  0.0 1.0 %fusion = (f32[1,128,256]{2,1,0:T(8,128)S(1)}, f32[1,128,256]{2,1,0:T(8,128)S(1)}) fusion(f32[2,128,256]{2,1,0:T(8,128)} %own.1), kind=kLoop, calls=%fused_computation.1 | loop fusion | bytes 524288 | tf_op jit(solution)/shard_map/slice | solution.py:36
  1.0 1.5 %collective-permute-start.4 = (f32[1,128,256]{2,1,0:T(8,128)S(1)}, f32[1,128,256]{2,1,0:T(8,128)S(1)}, u32[]{:S(2)}, u32[]{:S(2)}) collective-permute-start(f32[1,128,256]{2,1,0:T(8,128)S(1)} %get-tuple-element.5), channel_id=1, source_target_pairs={{0,8},{1,12},{2,0},{3,4},{4,9},{5,13},{6,1},{7,5},{8,10},{9,14},{1... | collective-permute-start | bytes 393224 | tf_op jit(solution)/shard_map/ppermute | solution.py:26
  2.5 0.7 %collective-permute-start.3 = (f32[1,128,256]{2,1,0:T(8,128)S(1)}, f32[1,128,256]{2,1,0:T(8,128)S(1)}, u32[]{:S(2)}, u32[]{:S(2)}) collective-permute-start(f32[1,128,256]{2,1,0:T(8,128)S(1)} %get-tuple-element.6), channel_id=1, source_target_pairs={{0,0},{1,4},{2,8},{3,12},{4,1},{5,5},{6,9},{7,13},{8,2},{9,6},{10,... | collective-permute-start | bytes 393224 | tf_op jit(solution)/shard_map/ppermute | solution.py:26
  3.2 9.3 %collective-permute-done.4.refs_4_ = f32[1,128,256]{2,1,0:T(8,128)S(1)} collective-permute-done((f32[1,128,256]{2,1,0:T(8,128)S(1)}, f32[1,128,256]{2,1,0:T(8,128)S(1)}, u32[]{:S(2)}, u32[]{:S(2)}) %collective-permute-start.4) | collective-permute-done | bytes 131104 | tf_op jit(solution)/shard_map/ppermute | solution.py:26
  12.5 0.2 collective-permute-start.8
  12.7 0.0 collective-permute-done.3.refs_3_
  12.7 0.4 collective-permute-start.11
  13.1 6.5 %collective-permute-start.2 = (f32[2,128,256]{2,1,0:T(8,128)}, f32[2,128,256]{2,1,0:T(8,128)S(1)}, u32[]{:S(2)}, u32[]{:S(2)}) collective-permute-start(f32[2,128,256]{2,1,0:T(8,128)} %own.1), channel_id=1, source_target_pairs={{0,3},{1,0},{2,1},{3,2},{4,7},{5,4},{6,5},{7,6},{8,11},{9,8},{10,9... | collective-permute-start | bytes 786440 | tf_op jit(solution)/shard_map/ppermute | solution.py:16
  19.6 0.6 %collective-permute-start = (f32[2,128,256]{2,1,0:T(8,128)}, f32[2,128,256]{2,1,0:T(8,128)S(1)}, u32[]{:S(2)}, u32[]{:S(2)}) collective-permute-start(f32[2,128,256]{2,1,0:T(8,128)} %own.1), channel_id=1, source_target_pairs={{0,1},{1,2},{2,3},{3,0},{4,5},{5,6},{6,7},{7,4},{8,9},{9,10},{10,1... | collective-permute-start | bytes 786440 | tf_op jit(solution)/shard_map/ppermute | solution.py:16
  20.2 0.0 collective-permute-done.6.refs_6_
  20.2 0.5 %collective-permute-start.7 = (f32[1,128,256]{2,1,0:T(8,128)S(1)}, f32[1,128,256]{2,1,0:T(8,128)S(1)}, u32[]{:S(2)}, u32[]{:S(2)}) collective-permute-start(f32[1,128,256]{2,1,0:T(8,128)S(1)} %collective-permute-done.3.refs_3_), channel_id=1, source_target_pairs={{0,16},{4,20},{8,24},{12,28},{16,0},{20,4},{24,8},{28,12},{1,17},{... | collective-permute-start | bytes 393224 | tf_op jit(solution)/shard_map/ppermute | solution.py:11
  20.7 0.4 collective-permute-start.5
  21.1 4.1 %collective-permute-done.7.refs_7_ = f32[1,128,256]{2,1,0:T(8,128)S(1)} collective-permute-done((f32[1,128,256]{2,1,0:T(8,128)S(1)}, f32[1,128,256]{2,1,0:T(8,128)S(1)}, u32[]{:S(2)}, u32[]{:S(2)}) %collective-permute-start.7) | collective-permute-done | bytes 131104 | tf_op jit(solution)/shard_map/ppermute | solution.py:11
  25.2 0.5 %collective-permute-done.5.refs_5_ = f32[1,128,256]{2,1,0:T(8,128)S(1)} collective-permute-done((f32[1,128,256]{2,1,0:T(8,128)S(1)}, f32[1,128,256]{2,1,0:T(8,128)S(1)}, u32[]{:S(2)}, u32[]{:S(2)}) %collective-permute-start.5) | collective-permute-done | bytes 131104 | tf_op jit(solution)/shard_map/ppermute | solution.py:11
  25.7 0.4 collective-permute-start.10
  26.1 0.6 %collective-permute-done.2.refs_2_ = f32[2,128,256]{2,1,0:T(8,128)S(1)} collective-permute-done((f32[2,128,256]{2,1,0:T(8,128)}, f32[2,128,256]{2,1,0:T(8,128)S(1)}, u32[]{:S(2)}, u32[]{:S(2)}) %collective-permute-start.2) | collective-permute-done | bytes 262176 | tf_op jit(solution)/shard_map/ppermute | solution.py:16
  26.7 0.9 %collective-permute-start.9 = (f32[1,128,256]{2,1,0:T(8,128)S(1)}, f32[1,128,256]{2,1,0:T(8,128)S(1)}, u32[]{:S(2)}, u32[]{:S(2)}) collective-permute-start(f32[1,128,256]{2,1,0:T(8,128)S(1)} %collective-permute-done.5.refs_5_), channel_id=1, source_target_pairs={{0,16},{4,20},{8,24},{12,28},{16,0},{20,4},{24,8},{28,12},{1,17},{... | collective-permute-start | bytes 393224 | tf_op jit(solution)/shard_map/ppermute | solution.py:11
  27.6 14.1 %collective-permute-done.1.refs_1_ = f32[2,128,256]{2,1,0:T(8,128)S(1)} collective-permute-done((f32[2,128,256]{2,1,0:T(8,128)}, f32[2,128,256]{2,1,0:T(8,128)S(1)}, u32[]{:S(2)}, u32[]{:S(2)}) %collective-permute-start.1) | collective-permute-done | bytes 262176 | tf_op jit(solution)/shard_map/ppermute | solution.py:16
  41.7 0.0 collective-permute-start.13
  41.7 0.0 collective-permute-done.refs_0_
  41.7 0.5 %collective-permute-start.14 = (f32[1,128,256]{2,1,0:T(8,128)S(1)}, f32[1,128,256]{2,1,0:T(8,128)S(1)}, u32[]{:S(2)}, u32[]{:S(2)}) collective-permute-start(f32[1,128,256]{2,1,0:T(8,128)S(1)} %collective-permute-done.6.refs_6_), channel_id=1, source_target_pairs={{0,4},{4,0},{8,12},{12,8},{16,20},{20,16},{24,28},{28,24},{1,5},{5... | collective-permute-start | bytes 393224 | tf_op jit(solution)/shard_map/ppermute | solution.py:11
  42.2 0.0 collective-permute-done.16.refs_16_
  42.2 0.1 collective-permute-start.15
  42.3 0.4 collective-permute-start.18
  42.8 0.1 collective-permute-start.17
  42.8 0.1 pad_add_fusion.position
  42.9 0.4 collective-permute-done.14.refs_14_
  43.3 0.3 collective-permute-done.15.refs_15_
  43.6 0.2 collective-permute-done.18.refs_18_
  43.8 0.3 collective-permute-done.17.refs_17_
  44.1 0.9 %copy-done = f32[2,128,256]{2,1,0:T(8,128)S(1)} copy-done((f32[2,128,256]{2,1,0:T(8,128)S(1)}, f32[2,128,256]{2,1,0:T(8,128)}, u32[]{:S(2)}) %copy-start) | copy-done | bytes 262168
  45.1 4.3 %shard_map.17 = f32[1,2,1,512,512]{4,3,2,1,0:T(8,128)} custom-call(s32[2]{0:T(128)S(1)} %pad_add_fusion.position, f32[2,128,256]{2,1,0:T(8,128)S(1)} %copy-done, f32[2,128,256]{2,1,0:T(8,128)S(1)} %collective-permute-done.refs_0_, f32[2,128,256]{2,1,0:T(8,128)S(1)} %collective-permute-done.1.refs_1_, f32[2,128,256]{2,1,0:T(8,128)S(1)} %collective-permute-done.2.refs_2_, ...), custom_call_target="tpu_custom_call" | custom-call | flops 1610612736 | bytes 4194304 | tf_op jit(solution)/shard_map/pallas_call | solution.py:99
  (11 shorter events, 0.0 us)
Async XLA Ops:
  1.0 11.5 %collective-permute-start.4 = (f32[1,128,256]{2,1,0:T(8,128)S(1)}, f32[1,128,256]{2,1,0:T(8,128)S(1)}, u32[]{:S(2)}, u32[]{:S(2)}) collective-permute-start(f32[1,128,256]{2,1,0:T(8,128)S(1)} %get-tuple-element.5), channel_id=1, source_target_pairs={{0,8},{1,12},{2,0},{3,4},{4,9},{5,13},{6,1},{7,5},{8,10},{9,14},{1... | collective-permute-start | bytes 393224 | tf_op jit(solution)/shard_map/ppermute | solution.py:26
  2.5 10.2 %collective-permute-start.3 = (f32[1,128,256]{2,1,0:T(8,128)S(1)}, f32[1,128,256]{2,1,0:T(8,128)S(1)}, u32[]{:S(2)}, u32[]{:S(2)}) collective-permute-start(f32[1,128,256]{2,1,0:T(8,128)S(1)} %get-tuple-element.6), channel_id=1, source_target_pairs={{0,0},{1,4},{2,8},{3,12},{4,1},{5,5},{6,9},{7,13},{8,2},{9,6},{10,... | collective-permute-start | bytes 393224 | tf_op jit(solution)/shard_map/ppermute | solution.py:26
  12.5 7.1 %collective-permute-start.12 = (f32[1,128,256]{2,1,0:T(8,128)S(1)}, f32[1,128,256]{2,1,0:T(8,128)S(1)}, u32[]{:S(2)}, u32[]{:S(2)}) collective-permute-start(f32[1,128,256]{2,1,0:T(8,128)S(1)} %collective-permute-done.4.refs_4_), channel_id=1, source_target_pairs={{0,4},{4,0},{8,12},{12,8},{16,20},{20,16},{24,28},{28,24},{1,5},{5... | collective-permute-start | bytes 393224 | tf_op jit(solution)/shard_map/ppermute | solution.py:11
  12.5 7.1 %collective-permute-start.8 = (f32[1,128,256]{2,1,0:T(8,128)S(1)}, f32[1,128,256]{2,1,0:T(8,128)S(1)}, u32[]{:S(2)}, u32[]{:S(2)}) collective-permute-start(f32[1,128,256]{2,1,0:T(8,128)S(1)} %collective-permute-done.4.refs_4_), channel_id=1, source_target_pairs={{0,16},{4,20},{8,24},{12,28},{16,0},{20,4},{24,8},{28,12},{1,17},{... | collective-permute-start | bytes 393224 | tf_op jit(solution)/shard_map/ppermute | solution.py:11
  12.7 7.5 %collective-permute-start.6 = (f32[1,128,256]{2,1,0:T(8,128)S(1)}, f32[1,128,256]{2,1,0:T(8,128)S(1)}, u32[]{:S(2)}, u32[]{:S(2)}) collective-permute-start(f32[1,128,256]{2,1,0:T(8,128)S(1)} %collective-permute-done.4.refs_4_), channel_id=1, source_target_pairs={{0,8},{4,12},{8,0},{12,4},{16,24},{20,28},{24,16},{28,20},{1,9},{5... | collective-permute-start | bytes 393224 | tf_op jit(solution)/shard_map/ppermute | solution.py:11
  12.7 8.0 %collective-permute-start.11 = (f32[1,128,256]{2,1,0:T(8,128)S(1)}, f32[1,128,256]{2,1,0:T(8,128)S(1)}, u32[]{:S(2)}, u32[]{:S(2)}) collective-permute-start(f32[1,128,256]{2,1,0:T(8,128)S(1)} %collective-permute-done.3.refs_3_), channel_id=1, source_target_pairs={{0,4},{4,0},{8,12},{12,8},{16,20},{20,16},{24,28},{28,24},{1,5},{5... | collective-permute-start | bytes 393224 | tf_op jit(solution)/shard_map/ppermute | solution.py:11
  13.1 13.6 %collective-permute-start.2 = (f32[2,128,256]{2,1,0:T(8,128)}, f32[2,128,256]{2,1,0:T(8,128)S(1)}, u32[]{:S(2)}, u32[]{:S(2)}) collective-permute-start(f32[2,128,256]{2,1,0:T(8,128)} %own.1), channel_id=1, source_target_pairs={{0,3},{1,0},{2,1},{3,2},{4,7},{5,4},{6,5},{7,6},{8,11},{9,8},{10,9... | collective-permute-start | bytes 786440 | tf_op jit(solution)/shard_map/ppermute | solution.py:16
  19.6 22.1 %collective-permute-start.1 = (f32[2,128,256]{2,1,0:T(8,128)}, f32[2,128,256]{2,1,0:T(8,128)S(1)}, u32[]{:S(2)}, u32[]{:S(2)}) collective-permute-start(f32[2,128,256]{2,1,0:T(8,128)} %own.1), channel_id=1, source_target_pairs={{0,2},{1,3},{2,0},{3,1},{4,6},{5,7},{6,4},{7,5},{8,10},{9,11},{10,... | collective-permute-start | bytes 786440 | tf_op jit(solution)/shard_map/ppermute | solution.py:16
  19.6 22.1 %collective-permute-start = (f32[2,128,256]{2,1,0:T(8,128)}, f32[2,128,256]{2,1,0:T(8,128)S(1)}, u32[]{:S(2)}, u32[]{:S(2)}) collective-permute-start(f32[2,128,256]{2,1,0:T(8,128)} %own.1), channel_id=1, source_target_pairs={{0,1},{1,2},{2,3},{3,0},{4,5},{5,6},{6,7},{7,4},{8,9},{9,10},{10,1... | collective-permute-start | bytes 786440 | tf_op jit(solution)/shard_map/ppermute | solution.py:16
  20.2 5.0 %collective-permute-start.7 = (f32[1,128,256]{2,1,0:T(8,128)S(1)}, f32[1,128,256]{2,1,0:T(8,128)S(1)}, u32[]{:S(2)}, u32[]{:S(2)}) collective-permute-start(f32[1,128,256]{2,1,0:T(8,128)S(1)} %collective-permute-done.3.refs_3_), channel_id=1, source_target_pairs={{0,16},{4,20},{8,24},{12,28},{16,0},{20,4},{24,8},{28,12},{1,17},{... | collective-permute-start | bytes 393224 | tf_op jit(solution)/shard_map/ppermute | solution.py:11
  20.7 5.0 %collective-permute-start.5 = (f32[1,128,256]{2,1,0:T(8,128)S(1)}, f32[1,128,256]{2,1,0:T(8,128)S(1)}, u32[]{:S(2)}, u32[]{:S(2)}) collective-permute-start(f32[1,128,256]{2,1,0:T(8,128)S(1)} %collective-permute-done.3.refs_3_), channel_id=1, source_target_pairs={{0,8},{4,12},{8,0},{12,4},{16,24},{20,28},{24,16},{28,20},{1,9},{5... | collective-permute-start | bytes 393224 | tf_op jit(solution)/shard_map/ppermute | solution.py:11
  25.2 17.0 %collective-permute-start.16 = (f32[1,128,256]{2,1,0:T(8,128)S(1)}, f32[1,128,256]{2,1,0:T(8,128)S(1)}, u32[]{:S(2)}, u32[]{:S(2)}) collective-permute-start(f32[1,128,256]{2,1,0:T(8,128)S(1)} %collective-permute-done.8.refs_8_), channel_id=1, source_target_pairs={{0,4},{4,0},{8,12},{12,8},{16,20},{20,16},{24,28},{28,24},{1,5},{5... | collective-permute-start | bytes 393224 | tf_op jit(solution)/shard_map/ppermute | solution.py:11
  25.7 16.6 %collective-permute-start.10 = (f32[1,128,256]{2,1,0:T(8,128)S(1)}, f32[1,128,256]{2,1,0:T(8,128)S(1)}, u32[]{:S(2)}, u32[]{:S(2)}) collective-permute-start(f32[1,128,256]{2,1,0:T(8,128)S(1)} %collective-permute-done.8.refs_8_), channel_id=1, source_target_pairs={{0,8},{4,12},{8,0},{12,4},{16,24},{20,28},{24,16},{28,20},{1,9},{5... | collective-permute-start | bytes 393224 | tf_op jit(solution)/shard_map/ppermute | solution.py:11
  26.7 16.0 %collective-permute-start.9 = (f32[1,128,256]{2,1,0:T(8,128)S(1)}, f32[1,128,256]{2,1,0:T(8,128)S(1)}, u32[]{:S(2)}, u32[]{:S(2)}) collective-permute-start(f32[1,128,256]{2,1,0:T(8,128)S(1)} %collective-permute-done.5.refs_5_), channel_id=1, source_target_pairs={{0,16},{4,20},{8,24},{12,28},{16,0},{20,4},{24,8},{28,12},{1,17},{... | collective-permute-start | bytes 393224 | tf_op jit(solution)/shard_map/ppermute | solution.py:11
  41.7 1.9 %collective-permute-start.13 = (f32[1,128,256]{2,1,0:T(8,128)S(1)}, f32[1,128,256]{2,1,0:T(8,128)S(1)}, u32[]{:S(2)}, u32[]{:S(2)}) collective-permute-start(f32[1,128,256]{2,1,0:T(8,128)S(1)} %collective-permute-done.5.refs_5_), channel_id=1, source_target_pairs={{0,4},{4,0},{8,12},{12,8},{16,20},{20,16},{24,28},{28,24},{1,5},{5... | collective-permute-start | bytes 393224 | tf_op jit(solution)/shard_map/ppermute | solution.py:11
  41.7 1.5 %collective-permute-start.14 = (f32[1,128,256]{2,1,0:T(8,128)S(1)}, f32[1,128,256]{2,1,0:T(8,128)S(1)}, u32[]{:S(2)}, u32[]{:S(2)}) collective-permute-start(f32[1,128,256]{2,1,0:T(8,128)S(1)} %collective-permute-done.6.refs_6_), channel_id=1, source_target_pairs={{0,4},{4,0},{8,12},{12,8},{16,20},{20,16},{24,28},{28,24},{1,5},{5... | collective-permute-start | bytes 393224 | tf_op jit(solution)/shard_map/ppermute | solution.py:11
  42.2 1.3 %collective-permute-start.15 = (f32[1,128,256]{2,1,0:T(8,128)S(1)}, f32[1,128,256]{2,1,0:T(8,128)S(1)}, u32[]{:S(2)}, u32[]{:S(2)}) collective-permute-start(f32[1,128,256]{2,1,0:T(8,128)S(1)} %collective-permute-done.7.refs_7_), channel_id=1, source_target_pairs={{0,4},{4,0},{8,12},{12,8},{16,20},{20,16},{24,28},{28,24},{1,5},{5... | collective-permute-start | bytes 393224 | tf_op jit(solution)/shard_map/ppermute | solution.py:11
  42.3 1.5 %collective-permute-start.18 = (f32[1,128,256]{2,1,0:T(8,128)S(1)}, f32[1,128,256]{2,1,0:T(8,128)S(1)}, u32[]{:S(2)}, u32[]{:S(2)}) collective-permute-start(f32[1,128,256]{2,1,0:T(8,128)S(1)} %collective-permute-done.10.refs_10_), channel_id=1, source_target_pairs={{0,4},{4,0},{8,12},{12,8},{16,20},{20,16},{24,28},{28,24},{1,5},{5... | collective-permute-start | bytes 393224 | tf_op jit(solution)/shard_map/ppermute | solution.py:11
  42.8 1.3 %collective-permute-start.17 = (f32[1,128,256]{2,1,0:T(8,128)S(1)}, f32[1,128,256]{2,1,0:T(8,128)S(1)}, u32[]{:S(2)}, u32[]{:S(2)}) collective-permute-start(f32[1,128,256]{2,1,0:T(8,128)S(1)} %collective-permute-done.9.refs_9_), channel_id=1, source_target_pairs={{0,4},{4,0},{8,12},{12,8},{16,20},{20,16},{24,28},{28,24},{1,5},{5... | collective-permute-start | bytes 393224 | tf_op jit(solution)/shard_map/ppermute | solution.py:11
  44.1 1.0 %copy-start = (f32[2,128,256]{2,1,0:T(8,128)S(1)}, f32[2,128,256]{2,1,0:T(8,128)}, u32[]{:S(2)}) copy-start(f32[2,128,256]{2,1,0:T(8,128)} %own.1) | copy-start | bytes 786436

commit v2 on v1

v2 whole, which is shorter than its diff:
```python
import jax
import jax.numpy as jnp
from jax import lax
from jax.experimental import pallas as pl
from jax.experimental.pallas import tpu as pltpu
from jax.sharding import PartitionSpec as P


def swap(block, bits):
    count = lax.axis_size("row")
    return lax.ppermute(block, "row", [(low, low ^ bits) for low in range(count)])


def shift(block, distance):
    rows, cols = lax.axis_size("row"), lax.axis_size("col")
    route = []
    for row in range(rows):
        for col in range(cols):
            target = (col + distance) % cols
            if target < row and row % cols != target:
                route.append((row * cols + col, row * cols + target))
    return lax.ppermute(block, ("row", "col"), route)


def transpose(block):
    rows, cols = lax.axis_size("row"), lax.axis_size("col")
    route = []
    for row in range(rows):
        for col in range(cols):
            target = row // cols * cols + col
            route.append((row * cols + col, target * cols + row % cols))
    return lax.ppermute(block, ("row", "col"), route)


def tiles(jacobian):
    rows, cols = lax.axis_size("row"), lax.axis_size("col")
    cycles = rows // cols
    panels, depth, width = jacobian.shape
    tile = depth * cols
    half = panels // 2
    moved = transpose(jacobian)
    near = [shift(jacobian, distance) for distance in range(1, cols)]
    bits = [1 << number for number in range(rows.bit_length() - 1)]
    first, second = bits[1], bits[2]
    by_first = swap(moved, first)
    by_second = swap(moved, second)
    low_far = swap(by_first[:half], second)
    high_far = swap(by_second[half:], first)
    held = [
        (0, 0, moved), (first, 0, by_first), (second, 0, by_second),
        (first | second, 0, low_far), (first | second, half, high_far),
    ]
    for bit in bits[:1] + bits[3:]:
        held += [
            (distance ^ bit, panel, swap(block, bit))
            for distance, panel, block in held
        ]
    pieces = [block for _, _, block in held]
    kinds = [(distance, panel) for distance, panel, _ in held]

    spread = panels * width
    vmem = pl.BlockSpec(memory_space=pltpu.VMEM)
    smem = pl.BlockSpec(memory_space=pltpu.SMEM)

    def split(value, hi, lo, lead, start, panel):
        top = value.astype(jnp.bfloat16)
        where = pl.ds(pl.multiple_of(start, depth), depth)
        hi[lead, where, panel * width : (panel + 1) * width] = top
        lo[lead, where, panel * width : (panel + 1) * width] = (
            value - top.astype(jnp.float32)
        ).astype(jnp.bfloat16)

    def split_columns(position, *refs):
        columns, (hi, lo) = refs[: len(pieces)], refs[len(pieces) :]
        for (distance, lead), source in zip(kinds, columns):
            holder = position[0] ^ distance
            turn = holder // cols
            for panel in range(source.shape[0]):
                split(source[panel], hi, lo, turn, (holder - turn * cols) * depth, lead + panel)

    def multiply(position, own, *refs):
        blocks = (own,) + tuple(refs[: cols - 1])
        col_hi, col_lo, out, row_hi, row_lo, stage, sems = refs[cols - 1 :]
        row_index, col_index = position[0], position[1]
        own_turn = row_index // cols
        diagonal = row_index - own_turn * cols == col_index

        @pl.when(diagonal)
        def _():
            row_hi[0] = col_hi[own_turn]
            row_lo[0] = col_lo[own_turn]

        @pl.when(jnp.logical_not(diagonal))
        def _():
            for distance, source in enumerate(blocks):
                start = lax.rem(col_index - distance + cols, cols) * depth
                for panel in range(panels):
                    split(source[panel], row_hi, row_lo, 0, start, panel)

        def dot(left, right):
            return lax.dot_general(
                left, right, (((1,), (1,)), ((), ())), preferred_element_type=jnp.float32
            )

        copies = []
        for turn in range(cycles):
            wanted = turn * cols + col_index <= row_index

            @pl.when(wanted)
            def _():
                stage[turn] = (
                    dot(row_hi[0], col_lo[turn]) + dot(row_lo[0], col_hi[turn])
                ) + dot(row_hi[0], col_hi[turn])

            @pl.when(jnp.logical_not(wanted))
            def _():
                stage[turn] = jnp.zeros((tile, tile), jnp.float32)

            copies.append(pltpu.make_async_copy(stage.at[turn], out.at[0, turn, 0], sems.at[turn]))
            copies[-1].start()
        for copy in copies:
            copy.wait()

    position = jnp.stack([lax.axis_index("row"), lax.axis_index("col")]).astype(jnp.int32)
    halves = jax.ShapeDtypeStruct((cycles, tile, spread), jnp.bfloat16)
    col_hi, col_lo = pl.pallas_call(
        split_columns,
        out_shape=(halves, halves),
        in_specs=[smem] + [vmem] * len(pieces),
        out_specs=(vmem, vmem),
        compiler_params=pltpu.CompilerParams(vmem_limit_bytes=16 << 20),
        cost_estimate=pl.CostEstimate(
            flops=8 * cycles * tile * spread,
            bytes_accessed=8 * cycles * tile * spread,
            transcendentals=0,
        ),
    )(position, *pieces)
    return pl.pallas_call(
        multiply,
        out_shape=jax.ShapeDtypeStruct((1, cycles, 1, tile, tile), jnp.float32),
        in_specs=[smem] + [vmem] * (cols + 2),
        out_specs=pl.BlockSpec(memory_space=pl.ANY),
        scratch_shapes=[
            pltpu.VMEM((1, tile, spread), jnp.bfloat16),
            pltpu.VMEM((1, tile, spread), jnp.bfloat16),
            pltpu.VMEM((cycles, tile, tile), jnp.float32),
            pltpu.SemaphoreType.DMA((cycles,)),
        ],
        compiler_params=pltpu.CompilerParams(vmem_limit_bytes=24 << 20),
        cost_estimate=pl.CostEstimate(
            flops=6 * cycles * tile * tile * spread,
            bytes_accessed=8 * cycles * tile * tile,
            transcendentals=0,
        ),
    )(position, jacobian, *near, col_hi, col_lo)


def solution(mesh):
    in_specs = (P(None, ("row", "col"), None),)
    out_specs = P("row", None, "col", None, None)
    return jax.shard_map(tiles, mesh=mesh, in_specs=in_specs, out_specs=out_specs, check_vma=False)
```

time: 50.3 us -> 59.3 us (1.18)
  the two profiles are of different devices: /device:TPU:4 before, /device:TPU:15 now
where the time goes in v2:
time: 59.3 us; the launch traced here: 59.1 us
  waiting for transfers between devices  33.7 us (57%)
  starting transfers between devices  20.8 us (35%)
  Pallas kernels  4.46 us (8%)
    ppermute x3, waiting for transfers between devices, shift(): return lax.ppermute(block, ('row', 'col'), route)  16.9 us
    ppermute x1, waiting for transfers between devices, transpose(): return lax.ppermute(block, ('row', 'col'), route)  11.6 us
    ppermute x3, starting transfers between devices, shift(): return lax.ppermute(block, ('row', 'col'), route)  8.96 us
    ppermute x9, starting transfers between devices, swap(): lax.ppermute(block, 'row', [(low, low ^ bits) for low in range(count)])  7.48 us
    ppermute x9, waiting for transfers between devices, swap(): lax.ppermute(block, 'row', [(low, low ^ bits) for low in range(count)])  5.22 us
    ppermute x1, starting transfers between devices, transpose(): return lax.ppermute(block, ('row', 'col'), route)  4.31 us
    pallas_call x1, Pallas kernels, tiles(): pl.pallas_call(multiply, out_shape=jax.ShapeDtypeStruct((1, cycles, 1, ti...  3.68 us
  transfers between devices with their start and end apart: 13, of which 6 were waited for; matrix products, arithmetic and copies ran while one was open for 0% of the time, Pallas kernels for 1%

profile of v2, /device:TPU:15, one launch (start us, length us, event | category | flops | bytes accessed | tf_op | source)
XLA Modules:
  0.0 59.1 jit_solution(4924941497996866873)
XLA Ops:
  0.0 0.0 copy-start
  0.0 4.3 %collective-permute-start.3 = (f32[2,128,256]{2,1,0:T(8,128)}, f32[2,128,256]{2,1,0:T(8,128)S(1)}, u32[]{:S(2)}, u32[]{:S(2)}) collective-permute-start(f32[2,128,256]{2,1,0:T(8,128)} %own.1), channel_id=1, source_target_pairs={{0,0},{1,4},{2,8},{3,12},{4,1},{5,5},{6,9},{7,13},{8,2},{9,6},{10,... | collective-permute-start | bytes 786440 | tf_op jit(solution)/shard_map/ppermute | solution.py:32
  4.3 11.6 %collective-permute-done.3.refs_0_ = f32[2,128,256]{2,1,0:T(8,128)S(1)} collective-permute-done((f32[2,128,256]{2,1,0:T(8,128)}, f32[2,128,256]{2,1,0:T(8,128)S(1)}, u32[]{:S(2)}, u32[]{:S(2)}) %collective-permute-start.3) | collective-permute-done | bytes 262176 | tf_op jit(solution)/shard_map/ppermute | solution.py:32
  15.9 0.2 collective-permute-start.5
  16.1 0.0 collective-permute-start.4
  16.2 1.9 %collective-permute-start.8 = (f32[2,128,256]{2,1,0:T(8,128)S(1)}, f32[2,128,256]{2,1,0:T(8,128)S(1)}, u32[]{:S(2)}, u32[]{:S(2)}) collective-permute-start(f32[2,128,256]{2,1,0:T(8,128)S(1)} %collective-permute-done.3.refs_0_), channel_id=1, source_target_pairs={{0,4},{4,0},{8,12},{12,8},{16,20},{20,16},{24,28},{28,24},{1,5},{5... | collective-permute-start | bytes 786440 | tf_op jit(solution)/shard_map/ppermute | solution.py:11
  18.1 4.0 %collective-permute-done.5.refs_2_ = f32[2,128,256]{2,1,0:T(8,128)S(1)} collective-permute-done((f32[2,128,256]{2,1,0:T(8,128)S(1)}, f32[2,128,256]{2,1,0:T(8,128)S(1)}, u32[]{:S(2)}, u32[]{:S(2)}) %collective-permute-start.5) | collective-permute-done | bytes 262176 | tf_op jit(solution)/shard_map/ppermute | solution.py:11
  22.1 2.5 %collective-permute-start.10 = (f32[2,128,256]{2,1,0:T(8,128)S(1)}, f32[2,128,256]{2,1,0:T(8,128)S(1)}, u32[]{:S(2)}, u32[]{:S(2)}) collective-permute-start(f32[2,128,256]{2,1,0:T(8,128)S(1)} %collective-permute-done.5.refs_2_), channel_id=1, source_target_pairs={{0,4},{4,0},{8,12},{12,8},{16,20},{20,16},{24,28},{28,24},{1,5},{5... | collective-permute-start | bytes 786440 | tf_op jit(solution)/shard_map/ppermute | solution.py:11
  24.6 0.0 collective-permute-done.4.refs_1_
  24.6 0.2 collective-permute-start.9
  24.9 1.3 %collective-permute-start.6 = (f32[1,128,256]{2,1,0:T(8,128)S(1)}, f32[1,128,256]{2,1,0:T(8,128)S(1)}, u32[]{:S(2)}, u32[]{:S(2)}) collective-permute-start(f32[1,128,256]{2,1,0:T(8,128)S(1)} %slice.8), channel_id=1, source_target_pairs={{0,16},{4,20},{8,24},{12,28},{16,0},{20,4},{24,8},{28,12},{1,17},{... | collective-permute-start | bytes 393224 | tf_op jit(solution)/shard_map/ppermute | solution.py:11
  26.2 0.1 collective-permute-start.7
  26.3 0.0 collective-permute-done.8.refs_5_
  26.3 4.3 %collective-permute-start = (f32[2,128,256]{2,1,0:T(8,128)}, f32[2,128,256]{2,1,0:T(8,128)S(1)}, u32[]{:S(2)}, u32[]{:S(2)}) collective-permute-start(f32[2,128,256]{2,1,0:T(8,128)} %own.1), channel_id=1, source_target_pairs={{7,4},{8,9},{11,8},{12,13},{13,14},{15,12},{16,17},{17,18},{18,19}... | collective-permute-start | bytes 786440 | tf_op jit(solution)/shard_map/ppermute | solution.py:22
  30.6 0.0 collective-permute-done.6.refs_3_
  30.6 1.3 %collective-permute-start.1 = (f32[2,128,256]{2,1,0:T(8,128)}, f32[2,128,256]{2,1,0:T(8,128)S(1)}, u32[]{:S(2)}, u32[]{:S(2)}) collective-permute-start(f32[2,128,256]{2,1,0:T(8,128)} %own.1), channel_id=1, source_target_pairs={{6,4},{10,8},{11,9},{12,14},{14,12},{15,13},{16,18},{17,19},{19,17... | collective-permute-start | bytes 786440 | tf_op jit(solution)/shard_map/ppermute | solution.py:22
  31.9 0.0 collective-permute-done.7.refs_4_
  32.0 3.3 %collective-permute-start.2 = (f32[2,128,256]{2,1,0:T(8,128)}, f32[2,128,256]{2,1,0:T(8,128)S(1)}, u32[]{:S(2)}, u32[]{:S(2)}) collective-permute-start(f32[2,128,256]{2,1,0:T(8,128)} %own.1), channel_id=1, source_target_pairs={{5,4},{9,8},{10,9},{13,12},{14,13},{15,14},{16,19},{18,17},{19,18}... | collective-permute-start | bytes 786440 | tf_op jit(solution)/shard_map/ppermute | solution.py:22
  35.3 0.0 collective-permute-done.10.refs_7_
  35.3 1.1 %collective-permute-start.11 = (f32[1,128,256]{2,1,0:T(8,128)S(1)}, f32[1,128,256]{2,1,0:T(8,128)S(1)}, u32[]{:S(2)}, u32[]{:S(2)}) collective-permute-start(f32[1,128,256]{2,1,0:T(8,128)S(1)} %collective-permute-done.6.refs_3_), channel_id=1, source_target_pairs={{0,4},{4,0},{8,12},{12,8},{16,20},{20,16},{24,28},{28,24},{1,5},{5... | collective-permute-start | bytes 393224 | tf_op jit(solution)/shard_map/ppermute | solution.py:11
  36.4 0.0 collective-permute-done.9.refs_6_
  36.4 0.1 collective-permute-start.12
  36.5 0.1 pad_add_fusion.position
  36.6 0.8 %collective-permute-done.11.refs_8_ = f32[1,128,256]{2,1,0:T(8,128)S(1)} collective-permute-done((f32[1,128,256]{2,1,0:T(8,128)S(1)}, f32[1,128,256]{2,1,0:T(8,128)S(1)}, u32[]{:S(2)}, u32[]{:S(2)}) %collective-permute-start.11) | collective-permute-done | bytes 131104 | tf_op jit(solution)/shard_map/ppermute | solution.py:11
  37.4 0.4 collective-permute-done.12.refs_9_
  37.8 0.8 %shard_map.17 = (bf16[2,512,512]{2,1,0:T(8,128)(2,1)S(1)}, bf16[2,512,512]{2,1,0:T(8,128)(2,1)S(1)}) custom-call(s32[2]{0:T(128)S(1)} %pad_add_fusion.position, f32[2,128,256]{2,1,0:T(8,128)S(1)} %collective-permute-done.3.refs_0_, f32[2,128,256]{2,1,0:T(8,128)S(1)} %collective-permute-done.4.refs_1_, f32[2,128,256]{2,1,0:T(8,128)S(1)} %collective-permute-done.5.refs_2_, ...), custom_call_target="tpu_custom_call" | custom-call | flops 4194304 | bytes 4194304 | tf_op jit(solution)/shard_map/pallas_call | solution.py:126
  38.5 0.0 collective-permute-done.refs_0_
  38.6 5.0 %collective-permute-done.1.refs_1_ = f32[2,128,256]{2,1,0:T(8,128)S(1)} collective-permute-done((f32[2,128,256]{2,1,0:T(8,128)}, f32[2,128,256]{2,1,0:T(8,128)S(1)}, u32[]{:S(2)}, u32[]{:S(2)}) %collective-permute-start.1) | collective-permute-done | bytes 262176 | tf_op jit(solution)/shard_map/ppermute | solution.py:22
  43.6 11.8 %collective-permute-done.2.refs_2_ = f32[2,128,256]{2,1,0:T(8,128)S(1)} collective-permute-done((f32[2,128,256]{2,1,0:T(8,128)}, f32[2,128,256]{2,1,0:T(8,128)S(1)}, u32[]{:S(2)}, u32[]{:S(2)}) %collective-permute-start.2) | collective-permute-done | bytes 262176 | tf_op jit(solution)/shard_map/ppermute | solution.py:22
  55.4 0.0 copy-done
  55.4 3.7 %shard_map.18 = f32[1,2,1,512,512]{4,3,2,1,0:T(8,128)} custom-call(s32[2]{0:T(128)S(1)} %pad_add_fusion.position, f32[2,128,256]{2,1,0:T(8,128)S(1)} %copy-done, f32[2,128,256]{2,1,0:T(8,128)S(1)} %collective-permute-done.refs_0_, f32[2,128,256]{2,1,0:T(8,128)S(1)} %collective-permute-done.1.refs_1_, f32[2,128,256]{2,1,0:T(8,128)S(1)} %collective-permute-done.2.refs_2_, ...), custom_call_target="tpu_custom_call" | custom-call | flops 1610612736 | bytes 4194304 | tf_op jit(solution)/shard_map/pallas_call | solution.py:138
  (2 shorter events, 0.0 us)
Async XLA Ops:
  0.0 55.4 %copy-start = (f32[2,128,256]{2,1,0:T(8,128)S(1)}, f32[2,128,256]{2,1,0:T(8,128)}, u32[]{:S(2)}) copy-start(f32[2,128,256]{2,1,0:T(8,128)} %own.1) | copy-start | bytes 786436
  0.0 15.9 %collective-permute-start.3 = (f32[2,128,256]{2,1,0:T(8,128)}, f32[2,128,256]{2,1,0:T(8,128)S(1)}, u32[]{:S(2)}, u32[]{:S(2)}) collective-permute-start(f32[2,128,256]{2,1,0:T(8,128)} %own.1), channel_id=1, source_target_pairs={{0,0},{1,4},{2,8},{3,12},{4,1},{5,5},{6,9},{7,13},{8,2},{9,6},{10,... | collective-permute-start | bytes 786440 | tf_op jit(solution)/shard_map/ppermute | solution.py:32
  15.9 6.2 %collective-permute-start.5 = (f32[2,128,256]{2,1,0:T(8,128)S(1)}, f32[2,128,256]{2,1,0:T(8,128)S(1)}, u32[]{:S(2)}, u32[]{:S(2)}) collective-permute-start(f32[2,128,256]{2,1,0:T(8,128)S(1)} %collective-permute-done.3.refs_0_), channel_id=1, source_target_pairs={{0,16},{4,20},{8,24},{12,28},{16,0},{20,4},{24,8},{28,12},{1,17},{... | collective-permute-start | bytes 786440 | tf_op jit(solution)/shard_map/ppermute | solution.py:11
  16.1 8.5 %collective-permute-start.4 = (f32[2,128,256]{2,1,0:T(8,128)S(1)}, f32[2,128,256]{2,1,0:T(8,128)S(1)}, u32[]{:S(2)}, u32[]{:S(2)}) collective-permute-start(f32[2,128,256]{2,1,0:T(8,128)S(1)} %collective-permute-done.3.refs_0_), channel_id=1, source_target_pairs={{0,8},{4,12},{8,0},{12,4},{16,24},{20,28},{24,16},{28,20},{1,9},{5... | collective-permute-start | bytes 786440 | tf_op jit(solution)/shard_map/ppermute | solution.py:11
  16.2 10.1 %collective-permute-start.8 = (f32[2,128,256]{2,1,0:T(8,128)S(1)}, f32[2,128,256]{2,1,0:T(8,128)S(1)}, u32[]{:S(2)}, u32[]{:S(2)}) collective-permute-start(f32[2,128,256]{2,1,0:T(8,128)S(1)} %collective-permute-done.3.refs_0_), channel_id=1, source_target_pairs={{0,4},{4,0},{8,12},{12,8},{16,20},{20,16},{24,28},{28,24},{1,5},{5... | collective-permute-start | bytes 786440 | tf_op jit(solution)/shard_map/ppermute | solution.py:11
  22.1 13.2 %collective-permute-start.10 = (f32[2,128,256]{2,1,0:T(8,128)S(1)}, f32[2,128,256]{2,1,0:T(8,128)S(1)}, u32[]{:S(2)}, u32[]{:S(2)}) collective-permute-start(f32[2,128,256]{2,1,0:T(8,128)S(1)} %collective-permute-done.5.refs_2_), channel_id=1, source_target_pairs={{0,4},{4,0},{8,12},{12,8},{16,20},{20,16},{24,28},{28,24},{1,5},{5... | collective-permute-start | bytes 786440 | tf_op jit(solution)/shard_map/ppermute | solution.py:11
  24.6 11.8 %collective-permute-start.9 = (f32[2,128,256]{2,1,0:T(8,128)S(1)}, f32[2,128,256]{2,1,0:T(8,128)S(1)}, u32[]{:S(2)}, u32[]{:S(2)}) collective-permute-start(f32[2,128,256]{2,1,0:T(8,128)S(1)} %collective-permute-done.4.refs_1_), channel_id=1, source_target_pairs={{0,4},{4,0},{8,12},{12,8},{16,20},{20,16},{24,28},{28,24},{1,5},{5... | collective-permute-start | bytes 786440 | tf_op jit(solution)/shard_map/ppermute | solution.py:11
  24.9 5.8 %collective-permute-start.6 = (f32[1,128,256]{2,1,0:T(8,128)S(1)}, f32[1,128,256]{2,1,0:T(8,128)S(1)}, u32[]{:S(2)}, u32[]{:S(2)}) collective-permute-start(f32[1,128,256]{2,1,0:T(8,128)S(1)} %slice.8), channel_id=1, source_target_pairs={{0,16},{4,20},{8,24},{12,28},{16,0},{20,4},{24,8},{28,12},{1,17},{... | collective-permute-start | bytes 393224 | tf_op jit(solution)/shard_map/ppermute | solution.py:11
  26.2 5.7 %collective-permute-start.7 = (f32[1,128,256]{2,1,0:T(8,128)S(1)}, f32[1,128,256]{2,1,0:T(8,128)S(1)}, u32[]{:S(2)}, u32[]{:S(2)}) collective-permute-start(f32[1,128,256]{2,1,0:T(8,128)S(1)} %slice.9), channel_id=1, source_target_pairs={{0,8},{4,12},{8,0},{12,4},{16,24},{20,28},{24,16},{28,20},{1,9},{5... | collective-permute-start | bytes 393224 | tf_op jit(solution)/shard_map/ppermute | solution.py:11
  26.3 12.3 %collective-permute-start = (f32[2,128,256]{2,1,0:T(8,128)}, f32[2,128,256]{2,1,0:T(8,128)S(1)}, u32[]{:S(2)}, u32[]{:S(2)}) collective-permute-start(f32[2,128,256]{2,1,0:T(8,128)} %own.1), channel_id=1, source_target_pairs={{7,4},{8,9},{11,8},{12,13},{13,14},{15,12},{16,17},{17,18},{18,19}... | collective-permute-start | bytes 786440 | tf_op jit(solution)/shard_map/ppermute | solution.py:22
  30.6 12.9 %collective-permute-start.1 = (f32[2,128,256]{2,1,0:T(8,128)}, f32[2,128,256]{2,1,0:T(8,128)S(1)}, u32[]{:S(2)}, u32[]{:S(2)}) collective-permute-start(f32[2,128,256]{2,1,0:T(8,128)} %own.1), channel_id=1, source_target_pairs={{6,4},{10,8},{11,9},{12,14},{14,12},{15,13},{16,18},{17,19},{19,17... | collective-permute-start | bytes 786440 | tf_op jit(solution)/shard_map/ppermute | solution.py:22
  32.0 23.5 %collective-permute-start.2 = (f32[2,128,256]{2,1,0:T(8,128)}, f32[2,128,256]{2,1,0:T(8,128)S(1)}, u32[]{:S(2)}, u32[]{:S(2)}) collective-permute-start(f32[2,128,256]{2,1,0:T(8,128)} %own.1), channel_id=1, source_target_pairs={{5,4},{9,8},{10,9},{13,12},{14,13},{15,14},{16,19},{18,17},{19,18}... | collective-permute-start | bytes 786440 | tf_op jit(solution)/shard_map/ppermute | solution.py:22
  35.3 2.1 %collective-permute-start.11 = (f32[1,128,256]{2,1,0:T(8,128)S(1)}, f32[1,128,256]{2,1,0:T(8,128)S(1)}, u32[]{:S(2)}, u32[]{:S(2)}) collective-permute-start(f32[1,128,256]{2,1,0:T(8,128)S(1)} %collective-permute-done.6.refs_3_), channel_id=1, source_target_pairs={{0,4},{4,0},{8,12},{12,8},{16,20},{20,16},{24,28},{28,24},{1,5},{5... | collective-permute-start | bytes 393224 | tf_op jit(solution)/shard_map/ppermute | solution.py:11
  36.4 1.3 %collective-permute-start.12 = (f32[1,128,256]{2,1,0:T(8,128)S(1)}, f32[1,128,256]{2,1,0:T(8,128)S(1)}, u32[]{:S(2)}, u32[]{:S(2)}) collective-permute-start(f32[1,128,256]{2,1,0:T(8,128)S(1)} %collective-permute-done.7.refs_4_), channel_id=1, source_target_pairs={{0,4},{4,0},{8,12},{12,8},{16,20},{20,16},{24,28},{28,24},{1,5},{5... | collective-permute-start | bytes 393224 | tf_op jit(solution)/shard_map/ppermute | solution.py:11

commit v3 on v2

v3 whole, which is shorter than its diff:
```python
import jax
import jax.numpy as jnp
from jax import lax
from jax.experimental import pallas as pl
from jax.experimental.pallas import tpu as pltpu
from jax.sharding import PartitionSpec as P


def swap(block, bits):
    count = lax.axis_size("row")
    route = [(low, low ^ bits) for low in range(count)]
    return lax.ppermute(block, "row", route)


def sense(row, cols):
    return 1 if row % cols < cols // 2 else -1


def reads(row, col, cols):
    return col < row and row % cols != col


def shift(block, distance):
    rows, cols = lax.axis_size("row"), lax.axis_size("col")
    route = []
    for row in range(rows):
        for col in range(cols):
            place = col + sense(row, cols) * distance
            if reads(row, place % cols, cols):
                route.append((row * cols + col, row * cols + place % cols))
    return lax.ppermute(block, ("row", "col"), route)


def transpose(block):
    rows, cols = lax.axis_size("row"), lax.axis_size("col")
    route = []
    for row in range(rows):
        for col in range(cols):
            target = row // cols * cols + (col + cols // 2) % cols
            route.append((row * cols + col, target * cols + row % cols))
    return lax.ppermute(block, ("row", "col"), route)


def row_bits(rows):
    bits = [1 << number for number in range(1, rows.bit_length() - 1)]
    distances = [0]
    for bit in bits:
        distances += [distance | bit for distance in distances]
    return distances[1:2] + distances[:1:-1], 1


def tiles(jacobian):
    rows, cols = lax.axis_size("row"), lax.axis_size("col")
    cycles = rows // cols
    panels, depth, width = jacobian.shape
    tile = depth * cols
    half = panels // 2
    first = jacobian[:half]
    parts = (first, lax.optimization_barrier((jacobian, first))[0][half:])
    moved = [transpose(part) for part in parts]
    near = [shift(jacobian, distance) for distance in range(1, cols)]
    far, twin = row_bits(rows)
    held = []
    for part in moved:
        pieces = {0: part}
        for distance in far:
            pieces[distance] = swap(part, distance)
        for distance in [0] + far:
            pieces[distance ^ twin] = swap(pieces[distance], twin)
        held.append(pieces)
    vmem = pl.BlockSpec(memory_space=pltpu.VMEM)
    smem = pl.BlockSpec(memory_space=pltpu.SMEM)
    params = pltpu.CompilerParams(vmem_limit_bytes=16 << 20)
    lanes = half * width
    position = jnp.stack([lax.axis_index("row"), lax.axis_index("col")]).astype(jnp.int32)

    def split(value, hi, lo, lead, start, panel):
        top = value.astype(jnp.bfloat16)
        where = (lead, pl.ds(pl.multiple_of(start, depth), depth), slice(panel * width, (panel + 1) * width))
        hi[where] = top
        lo[where] = (value - top.astype(jnp.float32)).astype(jnp.bfloat16)

    def split_columns(position, *refs):
        pieces, (hi, lo) = refs[:rows], refs[rows:]
        for distance, source in enumerate(pieces):
            holder = position[0] ^ distance
            turn = holder // cols
            slot = lax.rem(holder - turn * cols + cols - cols // 2, cols)
            for panel in range(half):
                split(source[panel], hi, lo, turn, slot * depth, panel)

    def columns(pieces):
        shape = jax.ShapeDtypeStruct((cycles, tile, lanes), jnp.bfloat16)
        return pl.pallas_call(
            split_columns,
            out_shape=(shape, shape),
            in_specs=[smem] + [vmem] * rows,
            out_specs=(vmem, vmem),
            compiler_params=params,
            cost_estimate=pl.CostEstimate(
                flops=4 * cycles * tile * lanes, bytes_accessed=8 * cycles * tile * lanes, transcendentals=0
            ),
        )(position, *[pieces[distance] for distance in range(rows)])

    split_parts = [columns(pieces) for pieces in held]

    chunks = 2
    chunk = tile // chunks

    def dot(left, right):
        return lax.dot_general(
            left, right, (((1,), (1,)), ((), ())), preferred_element_type=jnp.float32
        )

    def multiply(position, *refs):
        own, blocks, refs = refs[:2], refs[2 : cols + 1], refs[cols + 1 :]
        col_hi, col_lo = (refs[0], refs[2]), (refs[1], refs[3])
        out, row_hi, row_lo, stage, sems = refs[4:]
        row, col = position[0], position[1]
        own_turn = row // cols
        diagonal = row - own_turn * cols == col

        def copy(turn, part):
            where = slice(part * chunk, (part + 1) * chunk)
            return pltpu.make_async_copy(
                stage.at[turn, :, where], out.at[0, turn, 0, :, where], sems.at[turn, part]
            )

        wanted = [turn * cols + col <= row for turn in range(cycles)]
        for turn in range(cycles):

            @pl.when(jnp.logical_not(wanted[turn]))
            def _():
                stage[turn] = jnp.zeros((tile, tile), jnp.float32)
                for part in range(chunks):
                    copy(turn, part).start()

        @pl.when(diagonal)
        def _():
            for part in range(2):
                row_hi[part] = col_hi[part][own_turn]
                row_lo[part] = col_lo[part][own_turn]

        @pl.when(jnp.logical_not(diagonal))
        def _():
            ahead = lax.rem(row, cols) < cols // 2
            for distance in range(cols):
                back = jnp.where(ahead, cols - distance, distance)
                start = lax.rem(col + back, cols) * depth
                for panel in range(panels):
                    source = blocks[distance - 1][panel] if distance else own[panel // half][panel % half]
                    split(source, row_hi, row_lo, panel // half, start, panel % half)

        for turn in range(cycles):

            @pl.when(wanted[turn])
            def _():
                for number in range(chunks):
                    where = slice(number * chunk, (number + 1) * chunk)
                    total = None
                    for part in range(2):
                        hi, lo = col_hi[part][turn, where], col_lo[part][turn, where]
                        term = dot(row_hi[part], lo) + dot(row_lo[part], hi) + dot(row_hi[part], hi)
                        total = term if total is None else total + term
                    stage[turn, :, where] = total
                    copy(turn, number).start()

        for turn in range(cycles):
            for part in range(chunks):
                copy(turn, part).wait()

    half_rows = pltpu.VMEM((2, tile, lanes), jnp.bfloat16)
    return pl.pallas_call(
        multiply,
        out_shape=jax.ShapeDtypeStruct((1, cycles, 1, tile, tile), jnp.float32),
        in_specs=[smem] + [vmem] * (cols + 5),
        out_specs=pl.BlockSpec(memory_space=pl.ANY),
        scratch_shapes=[
            half_rows,
            half_rows,
            pltpu.VMEM((cycles, tile, tile), jnp.float32),
            pltpu.SemaphoreType.DMA((cycles, chunks)),
        ],
        compiler_params=params,
        cost_estimate=pl.CostEstimate(
            flops=6 * cycles * tile * tile * panels * width,
            bytes_accessed=8 * cycles * tile * tile,
            transcendentals=0,
        ),
    )(position, *parts, *near, *split_parts[0], *split_parts[1])


def solution(mesh):
    in_specs = (P(None, ("row", "col"), None),)
    out_specs = P("row", None, "col", None, None)
    return jax.shard_map(tiles, mesh=mesh, in_specs=in_specs, out_specs=out_specs, check_vma=False)
```

time: 59.3 us -> 60.2 us (1.015)
  the two profiles are of different devices: /device:TPU:15 before, /device:TPU:6 now
where the time goes in v3:
time: 60.2 us; the launch traced here: 60 us
  waiting for transfers between devices  27.2 us (45%)
  starting transfers between devices  25.8 us (43%)
  Pallas kernels  5.09 us (8%)
  local copies, waits for them, and re-layouts  1.83 us (3%)
    ppermute x3, waiting for transfers between devices, shift(): return lax.ppermute(block, ('row', 'col'), route)  18.4 us
    ppermute x14, starting transfers between devices, swap(): return lax.ppermute(block, 'row', route)  15 us
    ppermute x3, starting transfers between devices, shift(): return lax.ppermute(block, ('row', 'col'), route)  7.63 us
    ppermute x14, waiting for transfers between devices, swap(): return lax.ppermute(block, 'row', route)  5.51 us
    pallas_call x1, Pallas kernels, tiles(): pl.pallas_call(multiply, out_shape=jax.ShapeDtypeStruct((1, cycles, 1, ti...  3.74 us
    ppermute x2, waiting for transfers between devices, transpose(): return lax.ppermute(block, ('row', 'col'), route)  3.25 us
    ppermute x2, starting transfers between devices, transpose(): return lax.ppermute(block, ('row', 'col'), route)  3.18 us
    pallas_call x2, Pallas kernels, columns(): pl.pallas_call(split_columns, out_shape=(shape, shape), in_specs=[smem] +...  1.34 us
  transfers between devices with their start and end apart: 19, of which 9 were waited for; matrix products, arithmetic and copies ran while one was open for 0% of the time, Pallas kernels for 2%

profile of v3, /device:TPU:6, one launch (start us, length us, event | category | flops | bytes accessed | tf_op | source)
XLA Modules:
  0.0 60.0 jit_solution(10618832377669631029)
XLA Ops:
  0.0 0.9 %slice.6.refs_0_ = f32[1,128,256]{2,1,0:T(8,128)S(1)} slice(f32[2,128,256]{2,1,0:T(8,128)} %param.1), slice={[0:1], [0:128], [0:256]} | slice | bytes 262144 | tf_op jit(solution)/shard_map/slice | solution.py:58
  0.9 0.9 %slice.7.refs_1_ = f32[1,128,256]{2,1,0:T(8,128)S(1)} slice(f32[2,128,256]{2,1,0:T(8,128)} %param.1), slice={[1:2], [0:128], [0:256]} | slice | bytes 262144 | tf_op jit(solution)/shard_map/slice | solution.py:59
  1.8 2.6 %collective-permute-start.11 = (f32[1,128,256]{2,1,0:T(8,128)S(1)}, f32[1,128,256]{2,1,0:T(8,128)S(1)}, u32[]{:S(2)}, u32[]{:S(2)}) collective-permute-start(f32[1,128,256]{2,1,0:T(8,128)S(1)} %slice.7.refs_1_), channel_id=1, source_target_pairs={{0,8},{1,12},{2,0},{3,4},{4,9},{5,13},{6,1},{7,5},{8,10},{9,14},{1... | collective-permute-start | bytes 393224 | tf_op jit(solution)/shard_map/ppermute | solution.py:41
  4.5 0.5 collective-permute-start.3
  5.0 3.2 %collective-permute-done.11.refs_0_ = f32[1,128,256]{2,1,0:T(8,128)S(1)} collective-permute-done((f32[1,128,256]{2,1,0:T(8,128)S(1)}, f32[1,128,256]{2,1,0:T(8,128)S(1)}, u32[]{:S(2)}, u32[]{:S(2)}) %collective-permute-start.11) | collective-permute-done | bytes 131104 | tf_op jit(solution)/shard_map/ppermute | solution.py:41
  8.3 6.7 %collective-permute-start.17 = (f32[1,128,256]{2,1,0:T(8,128)S(1)}, f32[1,128,256]{2,1,0:T(8,128)S(1)}, u32[]{:S(2)}, u32[]{:S(2)}) collective-permute-start(f32[1,128,256]{2,1,0:T(8,128)S(1)} %collective-permute-done.11.refs_0_), channel_id=1, source_target_pairs={{0,24},{4,28},{8,16},{12,20},{16,8},{20,12},{24,0},{28,4},{1,25},{... | collective-permute-start | bytes 393224 | tf_op jit(solution)/shard_map/ppermute | solution.py:12
  14.9 1.8 %collective-permute-start.15 = (f32[1,128,256]{2,1,0:T(8,128)S(1)}, f32[1,128,256]{2,1,0:T(8,128)S(1)}, u32[]{:S(2)}, u32[]{:S(2)}) collective-permute-start(f32[1,128,256]{2,1,0:T(8,128)S(1)} %collective-permute-done.11.refs_0_), channel_id=1, source_target_pairs={{0,16},{4,20},{8,24},{12,28},{16,0},{20,4},{24,8},{28,12},{1,17},{... | collective-permute-start | bytes 393224 | tf_op jit(solution)/shard_map/ppermute | solution.py:12
  16.7 0.0 collective-permute-start.13
  16.8 0.0 collective-permute-start.12
  16.8 0.0 collective-permute-done.3.refs_0_
  16.8 1.7 %collective-permute-start.9 = (f32[1,128,256]{2,1,0:T(8,128)S(1)}, f32[1,128,256]{2,1,0:T(8,128)S(1)}, u32[]{:S(2)}, u32[]{:S(2)}) collective-permute-start(f32[1,128,256]{2,1,0:T(8,128)S(1)} %collective-permute-done.3.refs_0_), channel_id=1, source_target_pairs={{0,24},{4,28},{8,16},{12,20},{16,8},{20,12},{24,0},{28,4},{1,25},{... | collective-permute-start | bytes 393224 | tf_op jit(solution)/shard_map/ppermute | solution.py:12
  18.4 1.8 %collective-permute-start.7 = (f32[1,128,256]{2,1,0:T(8,128)S(1)}, f32[1,128,256]{2,1,0:T(8,128)S(1)}, u32[]{:S(2)}, u32[]{:S(2)}) collective-permute-start(f32[1,128,256]{2,1,0:T(8,128)S(1)} %collective-permute-done.3.refs_0_), channel_id=1, source_target_pairs={{0,16},{4,20},{8,24},{12,28},{16,0},{20,4},{24,8},{28,12},{1,17},{... | collective-permute-start | bytes 393224 | tf_op jit(solution)/shard_map/ppermute | solution.py:12
  20.3 1.4 %collective-permute-start.5 = (f32[1,128,256]{2,1,0:T(8,128)S(1)}, f32[1,128,256]{2,1,0:T(8,128)S(1)}, u32[]{:S(2)}, u32[]{:S(2)}) collective-permute-start(f32[1,128,256]{2,1,0:T(8,128)S(1)} %collective-permute-done.3.refs_0_), channel_id=1, source_target_pairs={{0,8},{4,12},{8,0},{12,4},{16,24},{20,28},{24,16},{28,20},{1,9},{5... | collective-permute-start | bytes 393224 | tf_op jit(solution)/shard_map/ppermute | solution.py:12
  21.7 1.4 %collective-permute-done.13.refs_2_ = f32[1,128,256]{2,1,0:T(8,128)S(1)} collective-permute-done((f32[1,128,256]{2,1,0:T(8,128)S(1)}, f32[1,128,256]{2,1,0:T(8,128)S(1)}, u32[]{:S(2)}, u32[]{:S(2)}) %collective-permute-start.13) | collective-permute-done | bytes 131104 | tf_op jit(solution)/shard_map/ppermute | solution.py:12
  23.1 0.5 collective-permute-start.18
  23.6 1.2 %collective-permute-done.9.refs_6_ = f32[1,128,256]{2,1,0:T(8,128)S(1)} collective-permute-done((f32[1,128,256]{2,1,0:T(8,128)S(1)}, f32[1,128,256]{2,1,0:T(8,128)S(1)}, u32[]{:S(2)}, u32[]{:S(2)}) %collective-permute-start.9) | collective-permute-done | bytes 131104 | tf_op jit(solution)/shard_map/ppermute | solution.py:12
  24.8 1.9 %collective-permute-done.7.refs_4_ = f32[1,128,256]{2,1,0:T(8,128)S(1)} collective-permute-done((f32[1,128,256]{2,1,0:T(8,128)S(1)}, f32[1,128,256]{2,1,0:T(8,128)S(1)}, u32[]{:S(2)}, u32[]{:S(2)}) %collective-permute-start.7) | collective-permute-done | bytes 131104 | tf_op jit(solution)/shard_map/ppermute | solution.py:12
  26.7 0.5 collective-permute-done.5.refs_2_
  27.2 0.0 collective-permute-start.10
  27.2 4.2 %collective-permute-start = (f32[2,128,256]{2,1,0:T(8,128)}, f32[2,128,256]{2,1,0:T(8,128)S(1)}, u32[]{:S(2)}, u32[]{:S(2)}) collective-permute-start(f32[2,128,256]{2,1,0:T(8,128)} %param.1), channel_id=1, source_target_pairs={{7,4},{9,8},{10,9},{13,12},{14,13},{15,14},{16,17},{17,18},{18,19}... | collective-permute-start | bytes 786440 | tf_op jit(solution)/shard_map/ppermute | solution.py:31
  31.4 2.2 %collective-permute-start.2 = (f32[2,128,256]{2,1,0:T(8,128)}, f32[2,128,256]{2,1,0:T(8,128)S(1)}, u32[]{:S(2)}, u32[]{:S(2)}) collective-permute-start(f32[2,128,256]{2,1,0:T(8,128)} %param.1), channel_id=1, source_target_pairs={{5,4},{8,9},{11,8},{12,13},{13,14},{15,12},{16,19},{18,17},{19,18}... | collective-permute-start | bytes 786440 | tf_op jit(solution)/shard_map/ppermute | solution.py:31
  33.5 1.3 %collective-permute-start.1 = (f32[2,128,256]{2,1,0:T(8,128)}, f32[2,128,256]{2,1,0:T(8,128)S(1)}, u32[]{:S(2)}, u32[]{:S(2)}) collective-permute-start(f32[2,128,256]{2,1,0:T(8,128)} %param.1), channel_id=1, source_target_pairs={{6,4},{10,8},{11,9},{12,14},{14,12},{15,13},{16,18},{17,19},{19,17... | collective-permute-start | bytes 786440 | tf_op jit(solution)/shard_map/ppermute | solution.py:31
  34.9 1.0 %collective-permute-start.8 = (f32[1,128,256]{2,1,0:T(8,128)S(1)}, f32[1,128,256]{2,1,0:T(8,128)S(1)}, u32[]{:S(2)}, u32[]{:S(2)}) collective-permute-start(f32[1,128,256]{2,1,0:T(8,128)S(1)} %collective-permute-done.7.refs_4_), channel_id=1, source_target_pairs={{0,4},{4,0},{8,12},{12,8},{16,20},{20,16},{24,28},{28,24},{1,5},{5... | collective-permute-start | bytes 393224 | tf_op jit(solution)/shard_map/ppermute | solution.py:12
  35.8 0.1 collective-permute-start.6
  35.9 0.1 pad_add_fusion.position
  36.0 0.7 %shard_map.18 = (bf16[2,512,256]{2,1,0:T(8,128)(2,1)S(1)}, bf16[2,512,256]{2,1,0:T(8,128)(2,1)S(1)}) custom-call(s32[2]{0:T(128)S(1)} %pad_add_fusion.position, f32[1,128,256]{2,1,0:T(8,128)S(1)} %collective-permute-done.11.refs_0_, f32[1,128,256]{2,1,0:T(8,128)S(1)} %collective-permute-done.12.refs_1_, f32[1,128,256]{2,1,0:T(8,128)S(1)} %collective-permute-done.13.refs_2_, ...), custom_call_target="tpu_custom_call" | custom-call | flops 1048576 | bytes 2097152 | tf_op jit(solution)/shard_map/pallas_call | solution.py:94
  36.7 0.1 collective-permute-done.8.refs_5_
  36.8 0.4 collective-permute-done.6.refs_3_
  37.2 0.7 %shard_map.17 = (bf16[2,512,256]{2,1,0:T(8,128)(2,1)S(1)}, bf16[2,512,256]{2,1,0:T(8,128)(2,1)S(1)}) custom-call(s32[2]{0:T(128)S(1)} %pad_add_fusion.position, f32[1,128,256]{2,1,0:T(8,128)S(1)} %collective-permute-done.3.refs_0_, f32[1,128,256]{2,1,0:T(8,128)S(1)} %collective-permute-done.4.refs_1_, f32[1,128,256]{2,1,0:T(8,128)S(1)} %collective-permute-done.5.refs_2_, ...), custom_call_target="tpu_custom_call" | custom-call | flops 1048576 | bytes 2097152 | tf_op jit(solution)/shard_map/pallas_call | solution.py:94
  37.9 6.0 %collective-permute-done.refs_2_ = f32[2,128,256]{2,1,0:T(8,128)S(1)} collective-permute-done((f32[2,128,256]{2,1,0:T(8,128)}, f32[2,128,256]{2,1,0:T(8,128)S(1)}, u32[]{:S(2)}, u32[]{:S(2)}) %collective-permute-start) | collective-permute-done | bytes 262176 | tf_op jit(solution)/shard_map/ppermute | solution.py:31
  43.9 12.4 %collective-permute-done.1.refs_3_ = f32[2,128,256]{2,1,0:T(8,128)S(1)} collective-permute-done((f32[2,128,256]{2,1,0:T(8,128)}, f32[2,128,256]{2,1,0:T(8,128)S(1)}, u32[]{:S(2)}, u32[]{:S(2)}) %collective-permute-start.1) | collective-permute-done | bytes 262176 | tf_op jit(solution)/shard_map/ppermute | solution.py:31
  56.3 3.7 %shard_map.19 = f32[1,2,1,512,512]{4,3,2,1,0:T(8,128)} custom-call(s32[2]{0:T(128)S(1)} %pad_add_fusion.position, f32[1,128,256]{2,1,0:T(8,128)S(1)} %slice.6.refs_0_, f32[1,128,256]{2,1,0:T(8,128)S(1)} %slice.7.refs_1_, f32[2,128,256]{2,1,0:T(8,128)S(1)} %collective-permute-done.refs_2_, f32[2,128,256]{2,1,0:T(8,128)S(1)} %collective-permute-done.1.refs_3_, ...), custom_call_target="tpu_custom_call" | custom-call | flops 1610612736 | bytes 4194304 | tf_op jit(solution)/shard_map/pallas_call | solution.py:173
  (12 shorter events, 0.0 us)
Async XLA Ops:
  1.8 6.4 %collective-permute-start.11 = (f32[1,128,256]{2,1,0:T(8,128)S(1)}, f32[1,128,256]{2,1,0:T(8,128)S(1)}, u32[]{:S(2)}, u32[]{:S(2)}) collective-permute-start(f32[1,128,256]{2,1,0:T(8,128)S(1)} %slice.7.refs_1_), channel_id=1, source_target_pairs={{0,8},{1,12},{2,0},{3,4},{4,9},{5,13},{6,1},{7,5},{8,10},{9,14},{1... | collective-permute-start | bytes 393224 | tf_op jit(solution)/shard_map/ppermute | solution.py:41
  4.5 12.3 %collective-permute-start.3 = (f32[1,128,256]{2,1,0:T(8,128)S(1)}, f32[1,128,256]{2,1,0:T(8,128)S(1)}, u32[]{:S(2)}, u32[]{:S(2)}) collective-permute-start(f32[1,128,256]{2,1,0:T(8,128)S(1)} %slice.6.refs_0_), channel_id=1, source_target_pairs={{0,8},{1,12},{2,0},{3,4},{4,9},{5,13},{6,1},{7,5},{8,10},{9,14},{1... | collective-permute-start | bytes 393224 | tf_op jit(solution)/shard_map/ppermute | solution.py:41
  8.3 10.2 %collective-permute-start.17 = (f32[1,128,256]{2,1,0:T(8,128)S(1)}, f32[1,128,256]{2,1,0:T(8,128)S(1)}, u32[]{:S(2)}, u32[]{:S(2)}) collective-permute-start(f32[1,128,256]{2,1,0:T(8,128)S(1)} %collective-permute-done.11.refs_0_), channel_id=1, source_target_pairs={{0,24},{4,28},{8,16},{12,20},{16,8},{20,12},{24,0},{28,4},{1,25},{... | collective-permute-start | bytes 393224 | tf_op jit(solution)/shard_map/ppermute | solution.py:12
  14.9 5.3 %collective-permute-start.15 = (f32[1,128,256]{2,1,0:T(8,128)S(1)}, f32[1,128,256]{2,1,0:T(8,128)S(1)}, u32[]{:S(2)}, u32[]{:S(2)}) collective-permute-start(f32[1,128,256]{2,1,0:T(8,128)S(1)} %collective-permute-done.11.refs_0_), channel_id=1, source_target_pairs={{0,16},{4,20},{8,24},{12,28},{16,0},{20,4},{24,8},{28,12},{1,17},{... | collective-permute-start | bytes 393224 | tf_op jit(solution)/shard_map/ppermute | solution.py:12
  16.7 6.4 %collective-permute-start.13 = (f32[1,128,256]{2,1,0:T(8,128)S(1)}, f32[1,128,256]{2,1,0:T(8,128)S(1)}, u32[]{:S(2)}, u32[]{:S(2)}) collective-permute-start(f32[1,128,256]{2,1,0:T(8,128)S(1)} %collective-permute-done.11.refs_0_), channel_id=1, source_target_pairs={{0,8},{4,12},{8,0},{12,4},{16,24},{20,28},{24,16},{28,20},{1,9},{5... | collective-permute-start | bytes 393224 | tf_op jit(solution)/shard_map/ppermute | solution.py:12
  16.8 6.4 %collective-permute-start.12 = (f32[1,128,256]{2,1,0:T(8,128)S(1)}, f32[1,128,256]{2,1,0:T(8,128)S(1)}, u32[]{:S(2)}, u32[]{:S(2)}) collective-permute-start(f32[1,128,256]{2,1,0:T(8,128)S(1)} %collective-permute-done.11.refs_0_), channel_id=1, source_target_pairs={{0,4},{4,0},{8,12},{12,8},{16,20},{20,16},{24,28},{28,24},{1,5},{5... | collective-permute-start | bytes 393224 | tf_op jit(solution)/shard_map/ppermute | solution.py:12
  16.8 8.0 %collective-permute-start.9 = (f32[1,128,256]{2,1,0:T(8,128)S(1)}, f32[1,128,256]{2,1,0:T(8,128)S(1)}, u32[]{:S(2)}, u32[]{:S(2)}) collective-permute-start(f32[1,128,256]{2,1,0:T(8,128)S(1)} %collective-permute-done.3.refs_0_), channel_id=1, source_target_pairs={{0,24},{4,28},{8,16},{12,20},{16,8},{20,12},{24,0},{28,4},{1,25},{... | collective-permute-start | bytes 393224 | tf_op jit(solution)/shard_map/ppermute | solution.py:12
  18.4 8.2 %collective-permute-start.7 = (f32[1,128,256]{2,1,0:T(8,128)S(1)}, f32[1,128,256]{2,1,0:T(8,128)S(1)}, u32[]{:S(2)}, u32[]{:S(2)}) collective-permute-start(f32[1,128,256]{2,1,0:T(8,128)S(1)} %collective-permute-done.3.refs_0_), channel_id=1, source_target_pairs={{0,16},{4,20},{8,24},{12,28},{16,0},{20,4},{24,8},{28,12},{1,17},{... | collective-permute-start | bytes 393224 | tf_op jit(solution)/shard_map/ppermute | solution.py:12
  20.3 6.9 %collective-permute-start.5 = (f32[1,128,256]{2,1,0:T(8,128)S(1)}, f32[1,128,256]{2,1,0:T(8,128)S(1)}, u32[]{:S(2)}, u32[]{:S(2)}) collective-permute-start(f32[1,128,256]{2,1,0:T(8,128)S(1)} %collective-permute-done.3.refs_0_), channel_id=1, source_target_pairs={{0,8},{4,12},{8,0},{12,4},{16,24},{20,28},{24,16},{28,20},{1,9},{5... | collective-permute-start | bytes 393224 | tf_op jit(solution)/shard_map/ppermute | solution.py:12
  23.1 4.1 %collective-permute-start.4 = (f32[1,128,256]{2,1,0:T(8,128)S(1)}, f32[1,128,256]{2,1,0:T(8,128)S(1)}, u32[]{:S(2)}, u32[]{:S(2)}) collective-permute-start(f32[1,128,256]{2,1,0:T(8,128)S(1)} %collective-permute-done.3.refs_0_), channel_id=1, source_target_pairs={{0,4},{4,0},{8,12},{12,8},{16,20},{20,16},{24,28},{28,24},{1,5},{5... | collective-permute-start | bytes 393224 | tf_op jit(solution)/shard_map/ppermute | solution.py:12
  23.1 8.3 %collective-permute-start.18 = (f32[1,128,256]{2,1,0:T(8,128)S(1)}, f32[1,128,256]{2,1,0:T(8,128)S(1)}, u32[]{:S(2)}, u32[]{:S(2)}) collective-permute-start(f32[1,128,256]{2,1,0:T(8,128)S(1)} %collective-permute-done.17.refs_6_), channel_id=1, source_target_pairs={{0,4},{4,0},{8,12},{12,8},{16,20},{20,16},{24,28},{28,24},{1,5},{5... | collective-permute-start | bytes 393224 | tf_op jit(solution)/shard_map/ppermute | solution.py:12
  24.8 8.7 %collective-permute-start.16 = (f32[1,128,256]{2,1,0:T(8,128)S(1)}, f32[1,128,256]{2,1,0:T(8,128)S(1)}, u32[]{:S(2)}, u32[]{:S(2)}) collective-permute-start(f32[1,128,256]{2,1,0:T(8,128)S(1)} %collective-permute-done.15.refs_4_), channel_id=1, source_target_pairs={{0,4},{4,0},{8,12},{12,8},{16,20},{20,16},{24,28},{28,24},{1,5},{5... | collective-permute-start | bytes 393224 | tf_op jit(solution)/shard_map/ppermute | solution.py:12
  26.7 8.2 %collective-permute-start.14 = (f32[1,128,256]{2,1,0:T(8,128)S(1)}, f32[1,128,256]{2,1,0:T(8,128)S(1)}, u32[]{:S(2)}, u32[]{:S(2)}) collective-permute-start(f32[1,128,256]{2,1,0:T(8,128)S(1)} %collective-permute-done.13.refs_2_), channel_id=1, source_target_pairs={{0,4},{4,0},{8,12},{12,8},{16,20},{20,16},{24,28},{28,24},{1,5},{5... | collective-permute-start | bytes 393224 | tf_op jit(solution)/shard_map/ppermute | solution.py:12
  27.2 8.7 %collective-permute-start.10 = (f32[1,128,256]{2,1,0:T(8,128)S(1)}, f32[1,128,256]{2,1,0:T(8,128)S(1)}, u32[]{:S(2)}, u32[]{:S(2)}) collective-permute-start(f32[1,128,256]{2,1,0:T(8,128)S(1)} %collective-permute-done.9.refs_6_), channel_id=1, source_target_pairs={{0,4},{4,0},{8,12},{12,8},{16,20},{20,16},{24,28},{28,24},{1,5},{5... | collective-permute-start | bytes 393224 | tf_op jit(solution)/shard_map/ppermute | solution.py:12
  27.2 16.7 %collective-permute-start = (f32[2,128,256]{2,1,0:T(8,128)}, f32[2,128,256]{2,1,0:T(8,128)S(1)}, u32[]{:S(2)}, u32[]{:S(2)}) collective-permute-start(f32[2,128,256]{2,1,0:T(8,128)} %param.1), channel_id=1, source_target_pairs={{7,4},{9,8},{10,9},{13,12},{14,13},{15,14},{16,17},{17,18},{18,19}... | collective-permute-start | bytes 786440 | tf_op jit(solution)/shard_map/ppermute | solution.py:31
  31.4 12.5 %collective-permute-start.2 = (f32[2,128,256]{2,1,0:T(8,128)}, f32[2,128,256]{2,1,0:T(8,128)S(1)}, u32[]{:S(2)}, u32[]{:S(2)}) collective-permute-start(f32[2,128,256]{2,1,0:T(8,128)} %param.1), channel_id=1, source_target_pairs={{5,4},{8,9},{11,8},{12,13},{13,14},{15,12},{16,19},{18,17},{19,18}... | collective-permute-start | bytes 786440 | tf_op jit(solution)/shard_map/ppermute | solution.py:31
  33.5 22.8 %collective-permute-start.1 = (f32[2,128,256]{2,1,0:T(8,128)}, f32[2,128,256]{2,1,0:T(8,128)S(1)}, u32[]{:S(2)}, u32[]{:S(2)}) collective-permute-start(f32[2,128,256]{2,1,0:T(8,128)} %param.1), channel_id=1, source_target_pairs={{6,4},{10,8},{11,9},{12,14},{14,12},{15,13},{16,18},{17,19},{19,17... | collective-permute-start | bytes 786440 | tf_op jit(solution)/shard_map/ppermute | solution.py:31
  34.9 2.0 %collective-permute-start.8 = (f32[1,128,256]{2,1,0:T(8,128)S(1)}, f32[1,128,256]{2,1,0:T(8,128)S(1)}, u32[]{:S(2)}, u32[]{:S(2)}) collective-permute-start(f32[1,128,256]{2,1,0:T(8,128)S(1)} %collective-permute-done.7.refs_4_), channel_id=1, source_target_pairs={{0,4},{4,0},{8,12},{12,8},{16,20},{20,16},{24,28},{28,24},{1,5},{5... | collective-permute-start | bytes 393224 | tf_op jit(solution)/shard_map/ppermute | solution.py:12
  35.8 1.3 %collective-permute-start.6 = (f32[1,128,256]{2,1,0:T(8,128)S(1)}, f32[1,128,256]{2,1,0:T(8,128)S(1)}, u32[]{:S(2)}, u32[]{:S(2)}) collective-permute-start(f32[1,128,256]{2,1,0:T(8,128)S(1)} %collective-permute-done.5.refs_2_), channel_id=1, source_target_pairs={{0,4},{4,0},{8,12},{12,8},{16,20},{20,16},{24,28},{28,24},{1,5},{5... | collective-permute-start | bytes 393224 | tf_op jit(solution)/shard_map/ppermute | solution.py:12

commit v4 on v3

--- a/solution.py
+++ b/solution.py
@@ -6,6 +6,9 @@
 from jax.sharding import PartitionSpec as P
 
 
+ROW_ORDER, COL_ORDER = ("hi", "lo"), ("lo", "hi")
+
+
 def swap(block, bits):
     count = lax.axis_size("row")
     route = [(low, low ^ bits) for low in range(count)]
@@ -20,13 +23,14 @@
     return col < row and row % cols != col
 
 
-def shift(block, distance):
+def shift(block, distance, straight):
     rows, cols = lax.axis_size("row"), lax.axis_size("col")
     route = []
     for row in range(rows):
         for col in range(cols):
             place = col + sense(row, cols) * distance
-            if reads(row, place % cols, cols):
+            inside = 0 <= place < cols
+            if straight in (None, inside) and reads(row, place % cols, cols):
                 route.append((row * cols + col, row * cols + place % cols))
     return lax.ppermute(block, ("row", "col"), route)
 
@@ -46,7 +50,7 @@
     distances = [0]
     for bit in bits:
         distances += [distance | bit for distance in distances]
-    return distances[1:2] + distances[:1:-1], 1
+    return distances[:0:-1], 1
 
 
 def tiles(jacobian):
@@ -58,7 +62,9 @@
     first = jacobian[:half]
     parts = (first, lax.optimization_barrier((jacobian, first))[0][half:])
     moved = [transpose(part) for part in parts]
-    near = [shift(jacobian, distance) for distance in range(1, cols)]
+    halved = range(2, cols - 1)
+    near = [shift(jacobian, distance, True if distance in halved else None) for distance in range(1, cols)]
+    near += [shift(jacobian, distance, False) for distance in halved]
     far, twin = row_bits(rows)
     held = []
     for part in moved:
@@ -74,28 +80,30 @@
     lanes = half * width
     position = jnp.stack([lax.axis_index("row"), lax.axis_index("col")]).astype(jnp.int32)
 
-    def split(value, hi, lo, lead, start, panel):
+    def split(value, parts, order, lead, start, panel):
         top = value.astype(jnp.bfloat16)
-        where = (lead, pl.ds(pl.multiple_of(start, depth), depth), slice(panel * width, (panel + 1) * width))
-        hi[where] = top
-        lo[where] = (value - top.astype(jnp.float32)).astype(jnp.bfloat16)
+        rest = (value - top.astype(jnp.float32)).astype(jnp.bfloat16)
+        where = pl.ds(pl.multiple_of(start, depth), depth)
+        for place, kind in enumerate(order):
+            first = place * lanes + panel * width
+            parts[lead, where, first : first + width] = top if kind == "hi" else rest
 
     def split_columns(position, *refs):
-        pieces, (hi, lo) = refs[:rows], refs[rows:]
+        pieces, whole = refs[:rows], refs[rows]
         for distance, source in enumerate(pieces):
             holder = position[0] ^ distance
             turn = holder // cols
             slot = lax.rem(holder - turn * cols + cols - cols // 2, cols)
             for panel in range(half):
-                split(source[panel], hi, lo, turn, slot * depth, panel)
+                split(source[panel], whole, COL_ORDER, turn, slot * depth, panel)
 
     def columns(pieces):
-        shape = jax.ShapeDtypeStruct((cycles, tile, lanes), jnp.bfloat16)
+        shape = jax.ShapeDtypeStruct((cycles, tile, len(COL_ORDER) * lanes), jnp.bfloat16)
         return pl.pallas_call(
             split_columns,
-            out_shape=(shape, shape),
+            out_shape=shape,
             in_specs=[smem] + [vmem] * rows,
-            out_specs=(vmem, vmem),
+            out_specs=vmem,
             compiler_params=params,
             cost_estimate=pl.CostEstimate(
                 flops=4 * cycles * tile * lanes, bytes_accessed=8 * cycles * tile * lanes, transcendentals=0
@@ -104,7 +112,7 @@
 
     split_parts = [columns(pieces) for pieces in held]
 
-    chunks = 2
+    chunks = 1
     chunk = tile // chunks
 
     def dot(left, right):
@@ -113,9 +121,9 @@
         )
 
     def multiply(position, *refs):
-        own, blocks, refs = refs[:2], refs[2 : cols + 1], refs[cols + 1 :]
-        col_hi, col_lo = (refs[0], refs[2]), (refs[1], refs[3])
-        out, row_hi, row_lo, stage, sems = refs[4:]
+        own, blocks, refs = refs[:2], refs[2 : 2 + len(near)], refs[2 + len(near) :]
+        columns_of = refs[:2]
+        out, rows_of, stage, sems = refs[2:]
         row, col = position[0], position[1]
         own_turn = row // cols
         diagonal = row - own_turn * cols == col
@@ -138,8 +146,11 @@
         @pl.when(diagonal)
         def _():
             for part in range(2):
-                row_hi[part] = col_hi[part][own_turn]
-                row_lo[part] = col_lo[part][own_turn]
+                for place, kind in enumerate(ROW_ORDER):
+                    first = COL_ORDER.index(kind) * lanes
+                    rows_of[part, :, place * lanes : (place + 1) * lanes] = columns_of[part][
+                        own_turn, :, first : first + lanes
+                    ]
 
         @pl.when(jnp.logical_not(diagonal))
         def _():
@@ -149,7 +160,9 @@
                 start = lax.rem(col + back, cols) * depth
                 for panel in range(panels):
                     source = blocks[distance - 1][panel] if distance else own[panel // half][panel % half]
-                    split(source, row_hi, row_lo, panel // half, start, panel % half)
+                    if distance in halved:
+                        source += blocks[cols - 3 + distance][panel]
+                    split(source, rows_of, ROW_ORDER, panel // half, start, panel % half)
 
         for turn in range(cycles):
 
@@ -159,8 +172,8 @@
                     where = slice(number * chunk, (number + 1) * chunk)
                     total = None
                     for part in range(2):
-                        hi, lo = col_hi[part][turn, where], col_lo[part][turn, where]
-                        term = dot(row_hi[part], lo) + dot(row_lo[part], hi) + dot(row_hi[part], hi)
+                        term = dot(rows_of[part], columns_of[part][turn, where])
+                        term += dot(rows_of[part, :, :lanes], columns_of[part][turn, where, lanes:])
                         total = term if total is None else total + term
                     stage[turn, :, where] = total
                     copy(turn, number).start()
@@ -169,14 +182,13 @@
             for part in range(chunks):
                 copy(turn, part).wait()
 
-    half_rows = pltpu.VMEM((2, tile, lanes), jnp.bfloat16)
+    half_rows = pltpu.VMEM((2, tile, len(ROW_ORDER) * lanes), jnp.bfloat16)
     return pl.pallas_call(
         multiply,
         out_shape=jax.ShapeDtypeStruct((1, cycles, 1, tile, tile), jnp.float32),
-        in_specs=[smem] + [vmem] * (cols + 5),
+        in_specs=[smem] + [vmem] * (len(near) + 4),
         out_specs=pl.BlockSpec(memory_space=pl.ANY),
         scratch_shapes=[
-            half_rows,
             half_rows,
             pltpu.VMEM((cycles, tile, tile), jnp.float32),
             pltpu.SemaphoreType.DMA((cycles, chunks)),
@@ -187,7 +199,7 @@
             bytes_accessed=8 * cycles * tile * tile,
             transcendentals=0,
         ),
-    )(position, *parts, *near, *split_parts[0], *split_parts[1])
+    )(position, *parts, *near, *split_parts)
 
 
 def solution(mesh):

time: 60.2 us -> 58.6 us (0.973)
  the two profiles are of different devices: /device:TPU:6 before, /device:TPU:14 now
where the time goes in v4:
time: 58.6 us; the launch traced here: 58.5 us
  waiting for transfers between devices  31.2 us (53%)
  starting transfers between devices  20.1 us (34%)
  Pallas kernels  5.05 us (9%)
  local copies, waits for them, and re-layouts  1.83 us (3%)
    ppermute x4, waiting for transfers between devices, shift(): return lax.ppermute(block, ('row', 'col'), route)  15 us
    ppermute x4, starting transfers between devices, shift(): return lax.ppermute(block, ('row', 'col'), route)  9.34 us
    ppermute x14, waiting for transfers between devices, swap(): return lax.ppermute(block, 'row', route)  8.94 us
    ppermute x14, starting transfers between devices, swap(): return lax.ppermute(block, 'row', route)  7.9 us
    ppermute x2, waiting for transfers between devices, transpose(): return lax.ppermute(block, ('row', 'col'), route)  7.24 us
    pallas_call x1, Pallas kernels, tiles(): pl.pallas_call(multiply, out_shape=jax.ShapeDtypeStruct((1, cycles, 1, ti...  3.71 us
    ppermute x2, starting transfers between devices, transpose(): return lax.ppermute(block, ('row', 'col'), route)  2.9 us
    pallas_call x2, Pallas kernels, columns(): pl.pallas_call(split_columns, out_shape=shape, in_specs=[smem] + [vmem] *...  1.35 us
  transfers between devices with their start and end apart: 20, of which 8 were waited for; matrix products, arithmetic and copies ran while one was open for 0% of the time, Pallas kernels for 2%

profile of v4, /device:TPU:14, one launch (start us, length us, event | category | flops | bytes accessed | tf_op | source)
XLA Modules:
  0.0 58.5 jit_solution(6279107411025228955)
XLA Ops:
  0.0 0.9 %slice.6.refs_0_ = f32[1,128,256]{2,1,0:T(8,128)S(1)} slice(f32[2,128,256]{2,1,0:T(8,128)} %param.1), slice={[0:1], [0:128], [0:256]} | slice | bytes 262144 | tf_op jit(solution)/shard_map/slice | solution.py:62
  0.9 0.9 %slice.7.refs_1_ = f32[1,128,256]{2,1,0:T(8,128)S(1)} slice(f32[2,128,256]{2,1,0:T(8,128)} %param.1), slice={[1:2], [0:128], [0:256]} | slice | bytes 262144 | tf_op jit(solution)/shard_map/slice | solution.py:63
  1.8 1.1 %collective-permute-start.12 = (f32[1,128,256]{2,1,0:T(8,128)S(1)}, f32[1,128,256]{2,1,0:T(8,128)S(1)}, u32[]{:S(2)}, u32[]{:S(2)}) collective-permute-start(f32[1,128,256]{2,1,0:T(8,128)S(1)} %slice.7.refs_1_), channel_id=1, source_target_pairs={{0,8},{1,12},{2,0},{3,4},{4,9},{5,13},{6,1},{7,5},{8,10},{9,14},{1... | collective-permute-start | bytes 393224 | tf_op jit(solution)/shard_map/ppermute | solution.py:45
  2.9 1.8 %collective-permute-start.4 = (f32[1,128,256]{2,1,0:T(8,128)S(1)}, f32[1,128,256]{2,1,0:T(8,128)S(1)}, u32[]{:S(2)}, u32[]{:S(2)}) collective-permute-start(f32[1,128,256]{2,1,0:T(8,128)S(1)} %slice.6.refs_0_), channel_id=1, source_target_pairs={{0,8},{1,12},{2,0},{3,4},{4,9},{5,13},{6,1},{7,5},{8,10},{9,14},{1... | collective-permute-start | bytes 393224 | tf_op jit(solution)/shard_map/ppermute | solution.py:45
  4.7 7.2 %collective-permute-done.12.refs_0_ = f32[1,128,256]{2,1,0:T(8,128)S(1)} collective-permute-done((f32[1,128,256]{2,1,0:T(8,128)S(1)}, f32[1,128,256]{2,1,0:T(8,128)S(1)}, u32[]{:S(2)}, u32[]{:S(2)}) %collective-permute-start.12) | collective-permute-done | bytes 131104 | tf_op jit(solution)/shard_map/ppermute | solution.py:45
  12.0 1.7 %collective-permute-start.18 = (f32[1,128,256]{2,1,0:T(8,128)S(1)}, f32[1,128,256]{2,1,0:T(8,128)S(1)}, u32[]{:S(2)}, u32[]{:S(2)}) collective-permute-start(f32[1,128,256]{2,1,0:T(8,128)S(1)} %collective-permute-done.12.refs_0_), channel_id=1, source_target_pairs={{0,24},{4,28},{8,16},{12,20},{16,8},{20,12},{24,0},{28,4},{1,25},{... | collective-permute-start | bytes 393224 | tf_op jit(solution)/shard_map/ppermute | solution.py:15
  13.7 1.2 %collective-permute-start.16 = (f32[1,128,256]{2,1,0:T(8,128)S(1)}, f32[1,128,256]{2,1,0:T(8,128)S(1)}, u32[]{:S(2)}, u32[]{:S(2)}) collective-permute-start(f32[1,128,256]{2,1,0:T(8,128)S(1)} %collective-permute-done.12.refs_0_), channel_id=1, source_target_pairs={{0,16},{4,20},{8,24},{12,28},{16,0},{20,4},{24,8},{28,12},{1,17},{... | collective-permute-start | bytes 393224 | tf_op jit(solution)/shard_map/ppermute | solution.py:15
  14.9 0.6 %collective-permute-start.14 = (f32[1,128,256]{2,1,0:T(8,128)S(1)}, f32[1,128,256]{2,1,0:T(8,128)S(1)}, u32[]{:S(2)}, u32[]{:S(2)}) collective-permute-start(f32[1,128,256]{2,1,0:T(8,128)S(1)} %collective-permute-done.12.refs_0_), channel_id=1, source_target_pairs={{0,8},{4,12},{8,0},{12,4},{16,24},{20,28},{24,16},{28,20},{1,9},{5... | collective-permute-start | bytes 393224 | tf_op jit(solution)/shard_map/ppermute | solution.py:15
  15.5 0.1 collective-permute-start.13
  15.6 1.5 %collective-permute-start.10 = (f32[1,128,256]{2,1,0:T(8,128)S(1)}, f32[1,128,256]{2,1,0:T(8,128)S(1)}, u32[]{:S(2)}, u32[]{:S(2)}) collective-permute-start(f32[1,128,256]{2,1,0:T(8,128)S(1)} %collective-permute-done.4.refs_0_), channel_id=1, source_target_pairs={{0,24},{4,28},{8,16},{12,20},{16,8},{20,12},{24,0},{28,4},{1,25},{... | collective-permute-start | bytes 393224 | tf_op jit(solution)/shard_map/ppermute | solution.py:15
  17.1 2.2 %collective-permute-done.18.refs_6_ = f32[1,128,256]{2,1,0:T(8,128)S(1)} collective-permute-done((f32[1,128,256]{2,1,0:T(8,128)S(1)}, f32[1,128,256]{2,1,0:T(8,128)S(1)}, u32[]{:S(2)}, u32[]{:S(2)}) %collective-permute-start.18) | collective-permute-done | bytes 131104 | tf_op jit(solution)/shard_map/ppermute | solution.py:15
  19.3 0.5 collective-permute-start.8
  19.8 1.3 %collective-permute-done.16.refs_4_ = f32[1,128,256]{2,1,0:T(8,128)S(1)} collective-permute-done((f32[1,128,256]{2,1,0:T(8,128)S(1)}, f32[1,128,256]{2,1,0:T(8,128)S(1)}, u32[]{:S(2)}, u32[]{:S(2)}) %collective-permute-start.16) | collective-permute-done | bytes 131104 | tf_op jit(solution)/shard_map/ppermute | solution.py:15
  21.2 1.0 %collective-permute-start.6 = (f32[1,128,256]{2,1,0:T(8,128)S(1)}, f32[1,128,256]{2,1,0:T(8,128)S(1)}, u32[]{:S(2)}, u32[]{:S(2)}) collective-permute-start(f32[1,128,256]{2,1,0:T(8,128)S(1)} %collective-permute-done.4.refs_0_), channel_id=1, source_target_pairs={{0,8},{4,12},{8,0},{12,4},{16,24},{20,28},{24,16},{28,20},{1,9},{5... | collective-permute-start | bytes 393224 | tf_op jit(solution)/shard_map/ppermute | solution.py:15
  22.2 0.5 collective-permute-start.19
  22.7 2.3 %collective-permute-done.10.refs_6_ = f32[1,128,256]{2,1,0:T(8,128)S(1)} collective-permute-done((f32[1,128,256]{2,1,0:T(8,128)S(1)}, f32[1,128,256]{2,1,0:T(8,128)S(1)}, u32[]{:S(2)}, u32[]{:S(2)}) %collective-permute-start.10) | collective-permute-done | bytes 131104 | tf_op jit(solution)/shard_map/ppermute | solution.py:15
  25.0 0.1 collective-permute-start.17
  25.0 2.5 %collective-permute-done.8.refs_4_ = f32[1,128,256]{2,1,0:T(8,128)S(1)} collective-permute-done((f32[1,128,256]{2,1,0:T(8,128)S(1)}, f32[1,128,256]{2,1,0:T(8,128)S(1)}, u32[]{:S(2)}, u32[]{:S(2)}) %collective-permute-start.8) | collective-permute-done | bytes 131104 | tf_op jit(solution)/shard_map/ppermute | solution.py:15
  27.6 0.5 collective-permute-start.11
  28.1 0.1 collective-permute-start.9
  28.2 1.3 %collective-permute-start.1 = (f32[2,128,256]{2,1,0:T(8,128)}, f32[2,128,256]{2,1,0:T(8,128)S(1)}, u32[]{:S(2)}, u32[]{:S(2)}) collective-permute-start(f32[2,128,256]{2,1,0:T(8,128)} %param.1), channel_id=1, source_target_pairs={{10,8},{11,9},{14,12},{15,13},{16,18},{17,19},{20,22},{21,23},{26,... | collective-permute-start | bytes 786440 | tf_op jit(solution)/shard_map/ppermute | solution.py:35
  29.5 1.9 %collective-permute-start = (f32[2,128,256]{2,1,0:T(8,128)}, f32[2,128,256]{2,1,0:T(8,128)S(1)}, u32[]{:S(2)}, u32[]{:S(2)}) collective-permute-start(f32[2,128,256]{2,1,0:T(8,128)} %param.1), channel_id=1, source_target_pairs={{7,4},{9,8},{10,9},{13,12},{14,13},{15,14},{16,17},{17,18},{18,19}... | collective-permute-start | bytes 786440 | tf_op jit(solution)/shard_map/ppermute | solution.py:35
  31.4 4.8 %collective-permute-start.3 = (f32[2,128,256]{2,1,0:T(8,128)}, f32[2,128,256]{2,1,0:T(8,128)S(1)}, u32[]{:S(2)}, u32[]{:S(2)}) collective-permute-start(f32[2,128,256]{2,1,0:T(8,128)} %param.1), channel_id=1, source_target_pairs={{6,4},{12,14},{19,17},{22,20},{25,27},{28,30}} | collective-permute-start | bytes 786440 | tf_op jit(solution)/shard_map/ppermute | solution.py:35
  36.3 1.3 %collective-permute-start.2 = (f32[2,128,256]{2,1,0:T(8,128)}, f32[2,128,256]{2,1,0:T(8,128)S(1)}, u32[]{:S(2)}, u32[]{:S(2)}) collective-permute-start(f32[2,128,256]{2,1,0:T(8,128)} %param.1), channel_id=1, source_target_pairs={{5,4},{8,9},{11,8},{12,13},{13,14},{15,12},{16,19},{18,17},{19,18}... | collective-permute-start | bytes 786440 | tf_op jit(solution)/shard_map/ppermute | solution.py:35
  37.6 0.1 collective-permute-start.7
  37.7 0.1 pad_add_fusion.position
  37.8 0.7 %shard_map.18.refs_7_ = bf16[2,512,512]{2,1,0:T(8,128)(2,1)S(1)} custom-call(s32[2]{0:T(128)S(1)} %pad_add_fusion.position, f32[1,128,256]{2,1,0:T(8,128)S(1)} %collective-permute-done.12.refs_0_, f32[1,128,256]{2,1,0:T(8,128)S(1)} %collective-permute-done.13.refs_1_, f32[1,128,256]{2,1,0:T(8,128)S(1)} %collective-permute-done.14.refs_2_, ...), custom_call_target="tpu_custom_call" | custom-call | flops 1048576 | bytes 2097152 | tf_op jit(solution)/shard_map/pallas_call | solution.py:102
  38.4 0.6 collective-permute-done.7.refs_3_
  39.0 0.7 %shard_map.17.refs_6_ = bf16[2,512,512]{2,1,0:T(8,128)(2,1)S(1)} custom-call(s32[2]{0:T(128)S(1)} %pad_add_fusion.position, f32[1,128,256]{2,1,0:T(8,128)S(1)} %collective-permute-done.4.refs_0_, f32[1,128,256]{2,1,0:T(8,128)S(1)} %collective-permute-done.5.refs_1_, f32[1,128,256]{2,1,0:T(8,128)S(1)} %collective-permute-done.6.refs_2_, ...), custom_call_target="tpu_custom_call" | custom-call | flops 1048576 | bytes 2097152 | tf_op jit(solution)/shard_map/pallas_call | solution.py:102
  39.7 0.7 %collective-permute-done.1.refs_3_ = f32[2,128,256]{2,1,0:T(8,128)S(1)} collective-permute-done((f32[2,128,256]{2,1,0:T(8,128)}, f32[2,128,256]{2,1,0:T(8,128)S(1)}, u32[]{:S(2)}, u32[]{:S(2)}) %collective-permute-start.1) | collective-permute-done | bytes 262176 | tf_op jit(solution)/shard_map/ppermute | solution.py:35
  40.4 14.3 %collective-permute-done.refs_2_ = f32[2,128,256]{2,1,0:T(8,128)S(1)} collective-permute-done((f32[2,128,256]{2,1,0:T(8,128)}, f32[2,128,256]{2,1,0:T(8,128)S(1)}, u32[]{:S(2)}, u32[]{:S(2)}) %collective-permute-start) | collective-permute-done | bytes 262176 | tf_op jit(solution)/shard_map/ppermute | solution.py:35
  54.7 3.7 %shard_map.19 = f32[1,2,1,512,512]{4,3,2,1,0:T(8,128)} custom-call(s32[2]{0:T(128)S(1)} %pad_add_fusion.position, f32[1,128,256]{2,1,0:T(8,128)S(1)} %slice.6.refs_0_, f32[1,128,256]{2,1,0:T(8,128)S(1)} %slice.7.refs_1_, f32[2,128,256]{2,1,0:T(8,128)S(1)} %collective-permute-done.refs_2_, f32[2,128,256]{2,1,0:T(8,128)S(1)} %collective-permute-done.1.refs_3_, ...), custom_call_target="tpu_custom_call" | custom-call | flops 1610612736 | bytes 4194304 | tf_op jit(solution)/shard_map/pallas_call | solution.py:186
  (14 shorter events, 0.0 us)
Async XLA Ops:
  1.8 10.1 %collective-permute-start.12 = (f32[1,128,256]{2,1,0:T(8,128)S(1)}, f32[1,128,256]{2,1,0:T(8,128)S(1)}, u32[]{:S(2)}, u32[]{:S(2)}) collective-permute-start(f32[1,128,256]{2,1,0:T(8,128)S(1)} %slice.7.refs_1_), channel_id=1, source_target_pairs={{0,8},{1,12},{2,0},{3,4},{4,9},{5,13},{6,1},{7,5},{8,10},{9,14},{1... | collective-permute-start | bytes 393224 | tf_op jit(solution)/shard_map/ppermute | solution.py:45
  2.9 12.7 %collective-permute-start.4 = (f32[1,128,256]{2,1,0:T(8,128)S(1)}, f32[1,128,256]{2,1,0:T(8,128)S(1)}, u32[]{:S(2)}, u32[]{:S(2)}) collective-permute-start(f32[1,128,256]{2,1,0:T(8,128)S(1)} %slice.6.refs_0_), channel_id=1, source_target_pairs={{0,8},{1,12},{2,0},{3,4},{4,9},{5,13},{6,1},{7,5},{8,10},{9,14},{1... | collective-permute-start | bytes 393224 | tf_op jit(solution)/shard_map/ppermute | solution.py:45
  12.0 7.3 %collective-permute-start.18 = (f32[1,128,256]{2,1,0:T(8,128)S(1)}, f32[1,128,256]{2,1,0:T(8,128)S(1)}, u32[]{:S(2)}, u32[]{:S(2)}) collective-permute-start(f32[1,128,256]{2,1,0:T(8,128)S(1)} %collective-permute-done.12.refs_0_), channel_id=1, source_target_pairs={{0,24},{4,28},{8,16},{12,20},{16,8},{20,12},{24,0},{28,4},{1,25},{... | collective-permute-start | bytes 393224 | tf_op jit(solution)/shard_map/ppermute | solution.py:15
  13.7 7.5 %collective-permute-start.16 = (f32[1,128,256]{2,1,0:T(8,128)S(1)}, f32[1,128,256]{2,1,0:T(8,128)S(1)}, u32[]{:S(2)}, u32[]{:S(2)}) collective-permute-start(f32[1,128,256]{2,1,0:T(8,128)S(1)} %collective-permute-done.12.refs_0_), channel_id=1, source_target_pairs={{0,16},{4,20},{8,24},{12,28},{16,0},{20,4},{24,8},{28,12},{1,17},{... | collective-permute-start | bytes 393224 | tf_op jit(solution)/shard_map/ppermute | solution.py:15
  14.9 7.3 %collective-permute-start.14 = (f32[1,128,256]{2,1,0:T(8,128)S(1)}, f32[1,128,256]{2,1,0:T(8,128)S(1)}, u32[]{:S(2)}, u32[]{:S(2)}) collective-permute-start(f32[1,128,256]{2,1,0:T(8,128)S(1)} %collective-permute-done.12.refs_0_), channel_id=1, source_target_pairs={{0,8},{4,12},{8,0},{12,4},{16,24},{20,28},{24,16},{28,20},{1,9},{5... | collective-permute-start | bytes 393224 | tf_op jit(solution)/shard_map/ppermute | solution.py:15
  15.5 6.7 %collective-permute-start.13 = (f32[1,128,256]{2,1,0:T(8,128)S(1)}, f32[1,128,256]{2,1,0:T(8,128)S(1)}, u32[]{:S(2)}, u32[]{:S(2)}) collective-permute-start(f32[1,128,256]{2,1,0:T(8,128)S(1)} %collective-permute-done.12.refs_0_), channel_id=1, source_target_pairs={{0,4},{4,0},{8,12},{12,8},{16,20},{20,16},{24,28},{28,24},{1,5},{5... | collective-permute-start | bytes 393224 | tf_op jit(solution)/shard_map/ppermute | solution.py:15
  15.6 9.4 %collective-permute-start.10 = (f32[1,128,256]{2,1,0:T(8,128)S(1)}, f32[1,128,256]{2,1,0:T(8,128)S(1)}, u32[]{:S(2)}, u32[]{:S(2)}) collective-permute-start(f32[1,128,256]{2,1,0:T(8,128)S(1)} %collective-permute-done.4.refs_0_), channel_id=1, source_target_pairs={{0,24},{4,28},{8,16},{12,20},{16,8},{20,12},{24,0},{28,4},{1,25},{... | collective-permute-start | bytes 393224 | tf_op jit(solution)/shard_map/ppermute | solution.py:15
  19.3 8.3 %collective-permute-start.8 = (f32[1,128,256]{2,1,0:T(8,128)S(1)}, f32[1,128,256]{2,1,0:T(8,128)S(1)}, u32[]{:S(2)}, u32[]{:S(2)}) collective-permute-start(f32[1,128,256]{2,1,0:T(8,128)S(1)} %collective-permute-done.4.refs_0_), channel_id=1, source_target_pairs={{0,16},{4,20},{8,24},{12,28},{16,0},{20,4},{24,8},{28,12},{1,17},{... | collective-permute-start | bytes 393224 | tf_op jit(solution)/shard_map/ppermute | solution.py:15
  21.2 6.4 %collective-permute-start.6 = (f32[1,128,256]{2,1,0:T(8,128)S(1)}, f32[1,128,256]{2,1,0:T(8,128)S(1)}, u32[]{:S(2)}, u32[]{:S(2)}) collective-permute-start(f32[1,128,256]{2,1,0:T(8,128)S(1)} %collective-permute-done.4.refs_0_), channel_id=1, source_target_pairs={{0,8},{4,12},{8,0},{12,4},{16,24},{20,28},{24,16},{28,20},{1,9},{5... | collective-permute-start | bytes 393224 | tf_op jit(solution)/shard_map/ppermute | solution.py:15
  22.2 5.9 %collective-permute-start.5 = (f32[1,128,256]{2,1,0:T(8,128)S(1)}, f32[1,128,256]{2,1,0:T(8,128)S(1)}, u32[]{:S(2)}, u32[]{:S(2)}) collective-permute-start(f32[1,128,256]{2,1,0:T(8,128)S(1)} %collective-permute-done.4.refs_0_), channel_id=1, source_target_pairs={{0,4},{4,0},{8,12},{12,8},{16,20},{20,16},{24,28},{28,24},{1,5},{5... | collective-permute-start | bytes 393224 | tf_op jit(solution)/shard_map/ppermute | solution.py:15
  22.2 6.0 %collective-permute-start.19 = (f32[1,128,256]{2,1,0:T(8,128)S(1)}, f32[1,128,256]{2,1,0:T(8,128)S(1)}, u32[]{:S(2)}, u32[]{:S(2)}) collective-permute-start(f32[1,128,256]{2,1,0:T(8,128)S(1)} %collective-permute-done.18.refs_6_), channel_id=1, source_target_pairs={{0,4},{4,0},{8,12},{12,8},{16,20},{20,16},{24,28},{28,24},{1,5},{5... | collective-permute-start | bytes 393224 | tf_op jit(solution)/shard_map/ppermute | solution.py:15
  25.0 4.5 %collective-permute-start.17 = (f32[1,128,256]{2,1,0:T(8,128)S(1)}, f32[1,128,256]{2,1,0:T(8,128)S(1)}, u32[]{:S(2)}, u32[]{:S(2)}) collective-permute-start(f32[1,128,256]{2,1,0:T(8,128)S(1)} %collective-permute-done.16.refs_4_), channel_id=1, source_target_pairs={{0,4},{4,0},{8,12},{12,8},{16,20},{20,16},{24,28},{28,24},{1,5},{5... | collective-permute-start | bytes 393224 | tf_op jit(solution)/shard_map/ppermute | solution.py:15
  27.6 3.8 %collective-permute-start.15 = (f32[1,128,256]{2,1,0:T(8,128)S(1)}, f32[1,128,256]{2,1,0:T(8,128)S(1)}, u32[]{:S(2)}, u32[]{:S(2)}) collective-permute-start(f32[1,128,256]{2,1,0:T(8,128)S(1)} %collective-permute-done.14.refs_2_), channel_id=1, source_target_pairs={{0,4},{4,0},{8,12},{12,8},{16,20},{20,16},{24,28},{28,24},{1,5},{5... | collective-permute-start | bytes 393224 | tf_op jit(solution)/shard_map/ppermute | solution.py:15
  27.6 8.7 %collective-permute-start.11 = (f32[1,128,256]{2,1,0:T(8,128)S(1)}, f32[1,128,256]{2,1,0:T(8,128)S(1)}, u32[]{:S(2)}, u32[]{:S(2)}) collective-permute-start(f32[1,128,256]{2,1,0:T(8,128)S(1)} %collective-permute-done.10.refs_6_), channel_id=1, source_target_pairs={{0,4},{4,0},{8,12},{12,8},{16,20},{20,16},{24,28},{28,24},{1,5},{5... | collective-permute-start | bytes 393224 | tf_op jit(solution)/shard_map/ppermute | solution.py:15
  28.1 9.5 %collective-permute-start.9 = (f32[1,128,256]{2,1,0:T(8,128)S(1)}, f32[1,128,256]{2,1,0:T(8,128)S(1)}, u32[]{:S(2)}, u32[]{:S(2)}) collective-permute-start(f32[1,128,256]{2,1,0:T(8,128)S(1)} %collective-permute-done.8.refs_4_), channel_id=1, source_target_pairs={{0,4},{4,0},{8,12},{12,8},{16,20},{20,16},{24,28},{28,24},{1,5},{5... | collective-permute-start | bytes 393224 | tf_op jit(solution)/shard_map/ppermute | solution.py:15
  28.2 12.2 %collective-permute-start.1 = (f32[2,128,256]{2,1,0:T(8,128)}, f32[2,128,256]{2,1,0:T(8,128)S(1)}, u32[]{:S(2)}, u32[]{:S(2)}) collective-permute-start(f32[2,128,256]{2,1,0:T(8,128)} %param.1), channel_id=1, source_target_pairs={{10,8},{11,9},{14,12},{15,13},{16,18},{17,19},{20,22},{21,23},{26,... | collective-permute-start | bytes 786440 | tf_op jit(solution)/shard_map/ppermute | solution.py:35
  29.5 25.3 %collective-permute-start = (f32[2,128,256]{2,1,0:T(8,128)}, f32[2,128,256]{2,1,0:T(8,128)S(1)}, u32[]{:S(2)}, u32[]{:S(2)}) collective-permute-start(f32[2,128,256]{2,1,0:T(8,128)} %param.1), channel_id=1, source_target_pairs={{7,4},{9,8},{10,9},{13,12},{14,13},{15,14},{16,17},{17,18},{18,19}... | collective-permute-start | bytes 786440 | tf_op jit(solution)/shard_map/ppermute | solution.py:35
  31.4 23.3 %collective-permute-start.3 = (f32[2,128,256]{2,1,0:T(8,128)}, f32[2,128,256]{2,1,0:T(8,128)S(1)}, u32[]{:S(2)}, u32[]{:S(2)}) collective-permute-start(f32[2,128,256]{2,1,0:T(8,128)} %param.1), channel_id=1, source_target_pairs={{6,4},{12,14},{19,17},{22,20},{25,27},{28,30}} | collective-permute-start | bytes 786440 | tf_op jit(solution)/shard_map/ppermute | solution.py:35
  36.3 18.5 %collective-permute-start.2 = (f32[2,128,256]{2,1,0:T(8,128)}, f32[2,128,256]{2,1,0:T(8,128)S(1)}, u32[]{:S(2)}, u32[]{:S(2)}) collective-permute-start(f32[2,128,256]{2,1,0:T(8,128)} %param.1), channel_id=1, source_target_pairs={{5,4},{8,9},{11,8},{12,13},{13,14},{15,12},{16,19},{18,17},{19,18}... | collective-permute-start | bytes 786440 | tf_op jit(solution)/shard_map/ppermute | solution.py:35
  37.6 1.4 %collective-permute-start.7 = (f32[1,128,256]{2,1,0:T(8,128)S(1)}, f32[1,128,256]{2,1,0:T(8,128)S(1)}, u32[]{:S(2)}, u32[]{:S(2)}) collective-permute-start(f32[1,128,256]{2,1,0:T(8,128)S(1)} %collective-permute-done.6.refs_2_), channel_id=1, source_target_pairs={{0,4},{4,0},{8,12},{12,8},{16,20},{20,16},{24,28},{28,24},{1,5},{5... | collective-permute-start | bytes 393224 | tf_op jit(solution)/shard_map/ppermute | solution.py:15

commit v5 on v4

--- a/solution.py
+++ b/solution.py
@@ -30,7 +30,7 @@
         for col in range(cols):
             place = col + sense(row, cols) * distance
             inside = 0 <= place < cols
-            if straight in (None, inside) and reads(row, place % cols, cols):
+            if straight in (None, inside) and (straight or reads(row, place % cols, cols)):
                 route.append((row * cols + col, row * cols + place % cols))
     return lax.ppermute(block, ("row", "col"), route)
 
@@ -59,8 +59,7 @@
     panels, depth, width = jacobian.shape
     tile = depth * cols
     half = panels // 2
-    first = jacobian[:half]
-    parts = (first, lax.optimization_barrier((jacobian, first))[0][half:])
+    parts = (jacobian[:half], jacobian[half:])
     moved = [transpose(part) for part in parts]
     halved = range(2, cols - 1)
     near = [shift(jacobian, distance, True if distance in halved else None) for distance in range(1, cols)]

time: 58.6 us -> 59.9 us (1.022)
  the two profiles are of different devices: /device:TPU:14 before, /device:TPU:6 now
where the time goes in v5:
time: 59.9 us; the launch traced here: 59.7 us
  starting transfers between devices  30.3 us (51%)
  waiting for transfers between devices  23.1 us (39%)
  Pallas kernels  5.06 us (8%)
  local copies, waits for them, and re-layouts  0.99 us (2%)
    ppermute x14, starting transfers between devices, swap(): return lax.ppermute(block, 'row', route)  14.5 us
    ppermute x4, waiting for transfers between devices, shift(): return lax.ppermute(block, ('row', 'col'), route)  14.3 us
    ppermute x4, starting transfers between devices, shift(): return lax.ppermute(block, ('row', 'col'), route)  12.7 us
    ppermute x14, waiting for transfers between devices, swap(): return lax.ppermute(block, 'row', route)  5.58 us
    pallas_call x1, Pallas kernels, tiles(): pl.pallas_call(multiply, out_shape=jax.ShapeDtypeStruct((1, cycles, 1, ti...  3.71 us
    ppermute x2, waiting for transfers between devices, transpose(): return lax.ppermute(block, ('row', 'col'), route)  3.25 us
    ppermute x2, starting transfers between devices, transpose(): return lax.ppermute(block, ('row', 'col'), route)  3.18 us
    pallas_call x2, Pallas kernels, columns(): pl.pallas_call(split_columns, out_shape=shape, in_specs=[smem] + [vmem] *...  1.35 us
  transfers between devices with their start and end apart: 20, of which 7 were waited for; matrix products, arithmetic and copies ran while one was open for 0% of the time, Pallas kernels for 2%

profile of v5, /device:TPU:6, one launch (start us, length us, event | category | flops | bytes accessed | tf_op | source)
XLA Modules:
  0.0 59.7 jit_solution(14202523306720613636)
XLA Ops:
  0.0 1.0 %fusion = (f32[1,128,256]{2,1,0:T(8,128)S(1)}, f32[1,128,256]{2,1,0:T(8,128)S(1)}) fusion(f32[2,128,256]{2,1,0:T(8,128)} %param.1), kind=kLoop, calls=%fused_computation.1 | loop fusion | bytes 524288 | tf_op jit(solution)/shard_map/slice | solution.py:62
  1.0 2.6 %collective-permute-start.12 = (f32[1,128,256]{2,1,0:T(8,128)S(1)}, f32[1,128,256]{2,1,0:T(8,128)S(1)}, u32[]{:S(2)}, u32[]{:S(2)}) collective-permute-start(f32[1,128,256]{2,1,0:T(8,128)S(1)} %get-tuple-element.5.refs_1_), channel_id=1, source_target_pairs={{0,8},{1,12},{2,0},{3,4},{4,9},{5,13},{6,1},{7,5},{8,10},{9,14},{1... | collective-permute-start | bytes 393224 | tf_op jit(solution)/shard_map/ppermute | solution.py:45
  3.6 0.5 collective-permute-start.4
  4.2 3.2 %collective-permute-done.12.refs_0_ = f32[1,128,256]{2,1,0:T(8,128)S(1)} collective-permute-done((f32[1,128,256]{2,1,0:T(8,128)S(1)}, f32[1,128,256]{2,1,0:T(8,128)S(1)}, u32[]{:S(2)}, u32[]{:S(2)}) %collective-permute-start.12) | collective-permute-done | bytes 131104 | tf_op jit(solution)/shard_map/ppermute | solution.py:45
  7.4 6.7 %collective-permute-start.18 = (f32[1,128,256]{2,1,0:T(8,128)S(1)}, f32[1,128,256]{2,1,0:T(8,128)S(1)}, u32[]{:S(2)}, u32[]{:S(2)}) collective-permute-start(f32[1,128,256]{2,1,0:T(8,128)S(1)} %collective-permute-done.12.refs_0_), channel_id=1, source_target_pairs={{0,24},{4,28},{8,16},{12,20},{16,8},{20,12},{24,0},{28,4},{1,25},{... | collective-permute-start | bytes 393224 | tf_op jit(solution)/shard_map/ppermute | solution.py:15
  14.1 1.8 %collective-permute-start.16 = (f32[1,128,256]{2,1,0:T(8,128)S(1)}, f32[1,128,256]{2,1,0:T(8,128)S(1)}, u32[]{:S(2)}, u32[]{:S(2)}) collective-permute-start(f32[1,128,256]{2,1,0:T(8,128)S(1)} %collective-permute-done.12.refs_0_), channel_id=1, source_target_pairs={{0,16},{4,20},{8,24},{12,28},{16,0},{20,4},{24,8},{28,12},{1,17},{... | collective-permute-start | bytes 393224 | tf_op jit(solution)/shard_map/ppermute | solution.py:15
  15.9 1.7 %collective-permute-start.10 = (f32[1,128,256]{2,1,0:T(8,128)S(1)}, f32[1,128,256]{2,1,0:T(8,128)S(1)}, u32[]{:S(2)}, u32[]{:S(2)}) collective-permute-start(f32[1,128,256]{2,1,0:T(8,128)S(1)} %collective-permute-done.4.refs_0_), channel_id=1, source_target_pairs={{0,24},{4,28},{8,16},{12,20},{16,8},{20,12},{24,0},{28,4},{1,25},{... | collective-permute-start | bytes 393224 | tf_op jit(solution)/shard_map/ppermute | solution.py:15
  17.6 0.0 collective-permute-done.18.refs_6_
  17.6 1.8 %collective-permute-start.8 = (f32[1,128,256]{2,1,0:T(8,128)S(1)}, f32[1,128,256]{2,1,0:T(8,128)S(1)}, u32[]{:S(2)}, u32[]{:S(2)}) collective-permute-start(f32[1,128,256]{2,1,0:T(8,128)S(1)} %collective-permute-done.4.refs_0_), channel_id=1, source_target_pairs={{0,16},{4,20},{8,24},{12,28},{16,0},{20,4},{24,8},{28,12},{1,17},{... | collective-permute-start | bytes 393224 | tf_op jit(solution)/shard_map/ppermute | solution.py:15
  19.4 0.0 collective-permute-done.16.refs_4_
  19.4 1.4 %collective-permute-start.6 = (f32[1,128,256]{2,1,0:T(8,128)S(1)}, f32[1,128,256]{2,1,0:T(8,128)S(1)}, u32[]{:S(2)}, u32[]{:S(2)}) collective-permute-start(f32[1,128,256]{2,1,0:T(8,128)S(1)} %collective-permute-done.4.refs_0_), channel_id=1, source_target_pairs={{0,8},{4,12},{8,0},{12,4},{16,24},{20,28},{24,16},{28,20},{1,9},{5... | collective-permute-start | bytes 393224 | tf_op jit(solution)/shard_map/ppermute | solution.py:15
  20.8 1.4 %collective-permute-done.14.refs_2_ = f32[1,128,256]{2,1,0:T(8,128)S(1)} collective-permute-done((f32[1,128,256]{2,1,0:T(8,128)S(1)}, f32[1,128,256]{2,1,0:T(8,128)S(1)}, u32[]{:S(2)}, u32[]{:S(2)}) %collective-permute-start.14) | collective-permute-done | bytes 131104 | tf_op jit(solution)/shard_map/ppermute | solution.py:15
  22.3 0.0 collective-permute-start.5
  22.3 0.0 collective-permute-done.13.refs_1_
  22.3 0.5 collective-permute-start.19
  22.8 1.2 %collective-permute-done.10.refs_6_ = f32[1,128,256]{2,1,0:T(8,128)S(1)} collective-permute-done((f32[1,128,256]{2,1,0:T(8,128)S(1)}, f32[1,128,256]{2,1,0:T(8,128)S(1)}, u32[]{:S(2)}, u32[]{:S(2)}) %collective-permute-start.10) | collective-permute-done | bytes 131104 | tf_op jit(solution)/shard_map/ppermute | solution.py:15
  24.0 1.9 %collective-permute-done.8.refs_4_ = f32[1,128,256]{2,1,0:T(8,128)S(1)} collective-permute-done((f32[1,128,256]{2,1,0:T(8,128)S(1)}, f32[1,128,256]{2,1,0:T(8,128)S(1)}, u32[]{:S(2)}, u32[]{:S(2)}) %collective-permute-start.8) | collective-permute-done | bytes 131104 | tf_op jit(solution)/shard_map/ppermute | solution.py:15
  25.8 0.0 collective-permute-start.15
  25.8 0.5 collective-permute-done.6.refs_2_
  26.3 0.0 collective-permute-start.11
  26.3 0.5 collective-permute-start.9
  26.8 3.8 %collective-permute-start = (f32[2,128,256]{2,1,0:T(8,128)}, f32[2,128,256]{2,1,0:T(8,128)S(1)}, u32[]{:S(2)}, u32[]{:S(2)}) collective-permute-start(f32[2,128,256]{2,1,0:T(8,128)} %param.1), channel_id=1, source_target_pairs={{7,4},{9,8},{10,9},{13,12},{14,13},{15,14},{16,17},{17,18},{18,19}... | collective-permute-start | bytes 786440 | tf_op jit(solution)/shard_map/ppermute | solution.py:35
  30.6 1.3 %collective-permute-start.1 = (f32[2,128,256]{2,1,0:T(8,128)}, f32[2,128,256]{2,1,0:T(8,128)S(1)}, u32[]{:S(2)}, u32[]{:S(2)}) collective-permute-start(f32[2,128,256]{2,1,0:T(8,128)} %param.1), channel_id=1, source_target_pairs={{0,2},{1,3},{4,6},{5,7},{10,8},{11,9},{14,12},{15,13},{16,18},{17,... | collective-permute-start | bytes 786440 | tf_op jit(solution)/shard_map/ppermute | solution.py:35
  32.0 0.7 %collective-permute-start.3 = (f32[2,128,256]{2,1,0:T(8,128)}, f32[2,128,256]{2,1,0:T(8,128)S(1)}, u32[]{:S(2)}, u32[]{:S(2)}) collective-permute-start(f32[2,128,256]{2,1,0:T(8,128)} %param.1), channel_id=1, source_target_pairs={{6,4},{12,14},{19,17},{22,20},{25,27},{28,30}} | collective-permute-start | bytes 786440 | tf_op jit(solution)/shard_map/ppermute | solution.py:35
  32.7 6.9 %collective-permute-start.2 = (f32[2,128,256]{2,1,0:T(8,128)}, f32[2,128,256]{2,1,0:T(8,128)S(1)}, u32[]{:S(2)}, u32[]{:S(2)}) collective-permute-start(f32[2,128,256]{2,1,0:T(8,128)} %param.1), channel_id=1, source_target_pairs={{5,4},{8,9},{11,8},{12,13},{13,14},{15,12},{16,19},{18,17},{19,18}... | collective-permute-start | bytes 786440 | tf_op jit(solution)/shard_map/ppermute | solution.py:35
  39.6 0.1 collective-permute-start.7
  39.7 0.1 pad_add_fusion.position
  39.7 0.7 %shard_map.18.refs_7_ = bf16[2,512,512]{2,1,0:T(8,128)(2,1)S(1)} custom-call(s32[2]{0:T(128)S(1)} %pad_add_fusion.position, f32[1,128,256]{2,1,0:T(8,128)S(1)} %collective-permute-done.12.refs_0_, f32[1,128,256]{2,1,0:T(8,128)S(1)} %collective-permute-done.13.refs_1_, f32[1,128,256]{2,1,0:T(8,128)S(1)} %collective-permute-done.14.refs_2_, ...), custom_call_target="tpu_custom_call" | custom-call | flops 1048576 | bytes 2097152 | tf_op jit(solution)/shard_map/pallas_call | solution.py:101
  40.4 0.6 collective-permute-done.7.refs_3_
  41.0 0.7 %shard_map.17.refs_6_ = bf16[2,512,512]{2,1,0:T(8,128)(2,1)S(1)} custom-call(s32[2]{0:T(128)S(1)} %pad_add_fusion.position, f32[1,128,256]{2,1,0:T(8,128)S(1)} %collective-permute-done.4.refs_0_, f32[1,128,256]{2,1,0:T(8,128)S(1)} %collective-permute-done.5.refs_1_, f32[1,128,256]{2,1,0:T(8,128)S(1)} %collective-permute-done.6.refs_2_, ...), custom_call_target="tpu_custom_call" | custom-call | flops 1048576 | bytes 2097152 | tf_op jit(solution)/shard_map/pallas_call | solution.py:101
  41.7 14.3 %collective-permute-done.1.refs_3_ = f32[2,128,256]{2,1,0:T(8,128)S(1)} collective-permute-done((f32[2,128,256]{2,1,0:T(8,128)}, f32[2,128,256]{2,1,0:T(8,128)S(1)}, u32[]{:S(2)}, u32[]{:S(2)}) %collective-permute-start.1) | collective-permute-done | bytes 262176 | tf_op jit(solution)/shard_map/ppermute | solution.py:35
  56.0 3.7 %shard_map.19 = f32[1,2,1,512,512]{4,3,2,1,0:T(8,128)} custom-call(s32[2]{0:T(128)S(1)} %pad_add_fusion.position, f32[1,128,256]{2,1,0:T(8,128)S(1)} %get-tuple-element.6.refs_0_, f32[1,128,256]{2,1,0:T(8,128)S(1)} %get-tuple-element.5.refs_1_, f32[2,128,256]{2,1,0:T(8,128)S(1)} %collective-permute-done.refs_2_, ...), custom_call_target="tpu_custom_call" | custom-call | flops 1610612736 | bytes 4194304 | tf_op jit(solution)/shard_map/pallas_call | solution.py:185
  (13 shorter events, 0.0 us)
Async XLA Ops:
  1.0 6.4 %collective-permute-start.12 = (f32[1,128,256]{2,1,0:T(8,128)S(1)}, f32[1,128,256]{2,1,0:T(8,128)S(1)}, u32[]{:S(2)}, u32[]{:S(2)}) collective-permute-start(f32[1,128,256]{2,1,0:T(8,128)S(1)} %get-tuple-element.5.refs_1_), channel_id=1, source_target_pairs={{0,8},{1,12},{2,0},{3,4},{4,9},{5,13},{6,1},{7,5},{8,10},{9,14},{1... | collective-permute-start | bytes 393224 | tf_op jit(solution)/shard_map/ppermute | solution.py:45
  3.6 12.3 %collective-permute-start.4 = (f32[1,128,256]{2,1,0:T(8,128)S(1)}, f32[1,128,256]{2,1,0:T(8,128)S(1)}, u32[]{:S(2)}, u32[]{:S(2)}) collective-permute-start(f32[1,128,256]{2,1,0:T(8,128)S(1)} %get-tuple-element.6.refs_0_), channel_id=1, source_target_pairs={{0,8},{1,12},{2,0},{3,4},{4,9},{5,13},{6,1},{7,5},{8,10},{9,14},{1... | collective-permute-start | bytes 393224 | tf_op jit(solution)/shard_map/ppermute | solution.py:45
  7.4 10.2 %collective-permute-start.18 = (f32[1,128,256]{2,1,0:T(8,128)S(1)}, f32[1,128,256]{2,1,0:T(8,128)S(1)}, u32[]{:S(2)}, u32[]{:S(2)}) collective-permute-start(f32[1,128,256]{2,1,0:T(8,128)S(1)} %collective-permute-done.12.refs_0_), channel_id=1, source_target_pairs={{0,24},{4,28},{8,16},{12,20},{16,8},{20,12},{24,0},{28,4},{1,25},{... | collective-permute-start | bytes 393224 | tf_op jit(solution)/shard_map/ppermute | solution.py:15
  14.1 5.3 %collective-permute-start.16 = (f32[1,128,256]{2,1,0:T(8,128)S(1)}, f32[1,128,256]{2,1,0:T(8,128)S(1)}, u32[]{:S(2)}, u32[]{:S(2)}) collective-permute-start(f32[1,128,256]{2,1,0:T(8,128)S(1)} %collective-permute-done.12.refs_0_), channel_id=1, source_target_pairs={{0,16},{4,20},{8,24},{12,28},{16,0},{20,4},{24,8},{28,12},{1,17},{... | collective-permute-start | bytes 393224 | tf_op jit(solution)/shard_map/ppermute | solution.py:15
  15.9 6.4 %collective-permute-start.14 = (f32[1,128,256]{2,1,0:T(8,128)S(1)}, f32[1,128,256]{2,1,0:T(8,128)S(1)}, u32[]{:S(2)}, u32[]{:S(2)}) collective-permute-start(f32[1,128,256]{2,1,0:T(8,128)S(1)} %collective-permute-done.12.refs_0_), channel_id=1, source_target_pairs={{0,8},{4,12},{8,0},{12,4},{16,24},{20,28},{24,16},{28,20},{1,9},{5... | collective-permute-start | bytes 393224 | tf_op jit(solution)/shard_map/ppermute | solution.py:15
  15.9 6.4 %collective-permute-start.13 = (f32[1,128,256]{2,1,0:T(8,128)S(1)}, f32[1,128,256]{2,1,0:T(8,128)S(1)}, u32[]{:S(2)}, u32[]{:S(2)}) collective-permute-start(f32[1,128,256]{2,1,0:T(8,128)S(1)} %collective-permute-done.12.refs_0_), channel_id=1, source_target_pairs={{0,4},{4,0},{8,12},{12,8},{16,20},{20,16},{24,28},{28,24},{1,5},{5... | collective-permute-start | bytes 393224 | tf_op jit(solution)/shard_map/ppermute | solution.py:15
  15.9 8.0 %collective-permute-start.10 = (f32[1,128,256]{2,1,0:T(8,128)S(1)}, f32[1,128,256]{2,1,0:T(8,128)S(1)}, u32[]{:S(2)}, u32[]{:S(2)}) collective-permute-start(f32[1,128,256]{2,1,0:T(8,128)S(1)} %collective-permute-done.4.refs_0_), channel_id=1, source_target_pairs={{0,24},{4,28},{8,16},{12,20},{16,8},{20,12},{24,0},{28,4},{1,25},{... | collective-permute-start | bytes 393224 | tf_op jit(solution)/shard_map/ppermute | solution.py:15
  17.6 8.2 %collective-permute-start.8 = (f32[1,128,256]{2,1,0:T(8,128)S(1)}, f32[1,128,256]{2,1,0:T(8,128)S(1)}, u32[]{:S(2)}, u32[]{:S(2)}) collective-permute-start(f32[1,128,256]{2,1,0:T(8,128)S(1)} %collective-permute-done.4.refs_0_), channel_id=1, source_target_pairs={{0,16},{4,20},{8,24},{12,28},{16,0},{20,4},{24,8},{28,12},{1,17},{... | collective-permute-start | bytes 393224 | tf_op jit(solution)/shard_map/ppermute | solution.py:15
  19.4 6.9 %collective-permute-start.6 = (f32[1,128,256]{2,1,0:T(8,128)S(1)}, f32[1,128,256]{2,1,0:T(8,128)S(1)}, u32[]{:S(2)}, u32[]{:S(2)}) collective-permute-start(f32[1,128,256]{2,1,0:T(8,128)S(1)} %collective-permute-done.4.refs_0_), channel_id=1, source_target_pairs={{0,8},{4,12},{8,0},{12,4},{16,24},{20,28},{24,16},{28,20},{1,9},{5... | collective-permute-start | bytes 393224 | tf_op jit(solution)/shard_map/ppermute | solution.py:15
  22.3 4.1 %collective-permute-start.5 = (f32[1,128,256]{2,1,0:T(8,128)S(1)}, f32[1,128,256]{2,1,0:T(8,128)S(1)}, u32[]{:S(2)}, u32[]{:S(2)}) collective-permute-start(f32[1,128,256]{2,1,0:T(8,128)S(1)} %collective-permute-done.4.refs_0_), channel_id=1, source_target_pairs={{0,4},{4,0},{8,12},{12,8},{16,20},{20,16},{24,28},{28,24},{1,5},{5... | collective-permute-start | bytes 393224 | tf_op jit(solution)/shard_map/ppermute | solution.py:15
  22.3 4.6 %collective-permute-start.19 = (f32[1,128,256]{2,1,0:T(8,128)S(1)}, f32[1,128,256]{2,1,0:T(8,128)S(1)}, u32[]{:S(2)}, u32[]{:S(2)}) collective-permute-start(f32[1,128,256]{2,1,0:T(8,128)S(1)} %collective-permute-done.18.refs_6_), channel_id=1, source_target_pairs={{0,4},{4,0},{8,12},{12,8},{16,20},{20,16},{24,28},{28,24},{1,5},{5... | collective-permute-start | bytes 393224 | tf_op jit(solution)/shard_map/ppermute | solution.py:15
  24.0 6.7 %collective-permute-start.17 = (f32[1,128,256]{2,1,0:T(8,128)S(1)}, f32[1,128,256]{2,1,0:T(8,128)S(1)}, u32[]{:S(2)}, u32[]{:S(2)}) collective-permute-start(f32[1,128,256]{2,1,0:T(8,128)S(1)} %collective-permute-done.16.refs_4_), channel_id=1, source_target_pairs={{0,4},{4,0},{8,12},{12,8},{16,20},{20,16},{24,28},{28,24},{1,5},{5... | collective-permute-start | bytes 393224 | tf_op jit(solution)/shard_map/ppermute | solution.py:15
  25.8 6.1 %collective-permute-start.15 = (f32[1,128,256]{2,1,0:T(8,128)S(1)}, f32[1,128,256]{2,1,0:T(8,128)S(1)}, u32[]{:S(2)}, u32[]{:S(2)}) collective-permute-start(f32[1,128,256]{2,1,0:T(8,128)S(1)} %collective-permute-done.14.refs_2_), channel_id=1, source_target_pairs={{0,4},{4,0},{8,12},{12,8},{16,20},{20,16},{24,28},{28,24},{1,5},{5... | collective-permute-start | bytes 393224 | tf_op jit(solution)/shard_map/ppermute | solution.py:15
  26.3 6.3 %collective-permute-start.11 = (f32[1,128,256]{2,1,0:T(8,128)S(1)}, f32[1,128,256]{2,1,0:T(8,128)S(1)}, u32[]{:S(2)}, u32[]{:S(2)}) collective-permute-start(f32[1,128,256]{2,1,0:T(8,128)S(1)} %collective-permute-done.10.refs_6_), channel_id=1, source_target_pairs={{0,4},{4,0},{8,12},{12,8},{16,20},{20,16},{24,28},{28,24},{1,5},{5... | collective-permute-start | bytes 393224 | tf_op jit(solution)/shard_map/ppermute | solution.py:15
  26.3 13.2 %collective-permute-start.9 = (f32[1,128,256]{2,1,0:T(8,128)S(1)}, f32[1,128,256]{2,1,0:T(8,128)S(1)}, u32[]{:S(2)}, u32[]{:S(2)}) collective-permute-start(f32[1,128,256]{2,1,0:T(8,128)S(1)} %collective-permute-done.8.refs_4_), channel_id=1, source_target_pairs={{0,4},{4,0},{8,12},{12,8},{16,20},{20,16},{24,28},{28,24},{1,5},{5... | collective-permute-start | bytes 393224 | tf_op jit(solution)/shard_map/ppermute | solution.py:15
  26.8 14.8 %collective-permute-start = (f32[2,128,256]{2,1,0:T(8,128)}, f32[2,128,256]{2,1,0:T(8,128)S(1)}, u32[]{:S(2)}, u32[]{:S(2)}) collective-permute-start(f32[2,128,256]{2,1,0:T(8,128)} %param.1), channel_id=1, source_target_pairs={{7,4},{9,8},{10,9},{13,12},{14,13},{15,14},{16,17},{17,18},{18,19}... | collective-permute-start | bytes 786440 | tf_op jit(solution)/shard_map/ppermute | solution.py:35
  30.6 25.3 %collective-permute-start.1 = (f32[2,128,256]{2,1,0:T(8,128)}, f32[2,128,256]{2,1,0:T(8,128)S(1)}, u32[]{:S(2)}, u32[]{:S(2)}) collective-permute-start(f32[2,128,256]{2,1,0:T(8,128)} %param.1), channel_id=1, source_target_pairs={{0,2},{1,3},{4,6},{5,7},{10,8},{11,9},{14,12},{15,13},{16,18},{17,... | collective-permute-start | bytes 786440 | tf_op jit(solution)/shard_map/ppermute | solution.py:35
  32.0 24.0 %collective-permute-start.3 = (f32[2,128,256]{2,1,0:T(8,128)}, f32[2,128,256]{2,1,0:T(8,128)S(1)}, u32[]{:S(2)}, u32[]{:S(2)}) collective-permute-start(f32[2,128,256]{2,1,0:T(8,128)} %param.1), channel_id=1, source_target_pairs={{6,4},{12,14},{19,17},{22,20},{25,27},{28,30}} | collective-permute-start | bytes 786440 | tf_op jit(solution)/shard_map/ppermute | solution.py:35
  32.7 23.3 %collective-permute-start.2 = (f32[2,128,256]{2,1,0:T(8,128)}, f32[2,128,256]{2,1,0:T(8,128)S(1)}, u32[]{:S(2)}, u32[]{:S(2)}) collective-permute-start(f32[2,128,256]{2,1,0:T(8,128)} %param.1), channel_id=1, source_target_pairs={{5,4},{8,9},{11,8},{12,13},{13,14},{15,12},{16,19},{18,17},{19,18}... | collective-permute-start | bytes 786440 | tf_op jit(solution)/shard_map/ppermute | solution.py:35
  39.6 1.4 %collective-permute-start.7 = (f32[1,128,256]{2,1,0:T(8,128)S(1)}, f32[1,128,256]{2,1,0:T(8,128)S(1)}, u32[]{:S(2)}, u32[]{:S(2)}) collective-permute-start(f32[1,128,256]{2,1,0:T(8,128)S(1)} %collective-permute-done.6.refs_2_), channel_id=1, source_target_pairs={{0,4},{4,0},{8,12},{12,8},{16,20},{20,16},{24,28},{28,24},{1,5},{5... | collective-permute-start | bytes 393224 | tf_op jit(solution)/shard_map/ppermute | solution.py:15

commit v6 on v5

--- a/solution.py
+++ b/solution.py
@@ -50,7 +50,7 @@
     distances = [0]
     for bit in bits:
         distances += [distance | bit for distance in distances]
-    return distances[:0:-1], 1
+    return distances[len(distances) // 2 :] + distances[1 : len(distances) // 2], 1
 
 
 def tiles(jacobian):
@@ -111,7 +111,7 @@
 
     split_parts = [columns(pieces) for pieces in held]
 
-    chunks = 1
+    chunks = 2
     chunk = tile // chunks
 
     def dot(left, right):
@@ -130,7 +130,7 @@
         def copy(turn, part):
             where = slice(part * chunk, (part + 1) * chunk)
             return pltpu.make_async_copy(
-                stage.at[turn, :, where], out.at[0, turn, 0, :, where], sems.at[turn, part]
+                stage.at[turn, where], out.at[0, turn, 0, where], sems.at[turn, part]
             )
 
         wanted = [turn * cols + col <= row for turn in range(cycles)]
@@ -171,10 +171,10 @@
                     where = slice(number * chunk, (number + 1) * chunk)
                     total = None
                     for part in range(2):
-                        term = dot(rows_of[part], columns_of[part][turn, where])
-                        term += dot(rows_of[part, :, :lanes], columns_of[part][turn, where, lanes:])
+                        term = dot(rows_of[part, where], columns_of[part][turn])
+                        term += dot(rows_of[part, where, :lanes], columns_of[part][turn, :, lanes:])
                         total = term if total is None else total + term
-                    stage[turn, :, where] = total
+                    stage[turn, where] = total
                     copy(turn, number).start()
 
         for turn in range(cycles):

time: 59.9 us -> 59.7 us (level)
  no operation moved by 1% of the time
where the time goes in v6:
time: 59.7 us; the launch traced here: 59.5 us
  starting transfers between devices  30.3 us (51%)
  waiting for transfers between devices  23.1 us (39%)
  Pallas kernels  4.9 us (8%)
  local copies, waits for them, and re-layouts  0.99 us (2%)
    ppermute x14, starting transfers between devices, swap(): return lax.ppermute(block, 'row', route)  14.5 us
    ppermute x4, waiting for transfers between devices, shift(): return lax.ppermute(block, ('row', 'col'), route)  14.3 us
    ppermute x4, starting transfers between devices, shift(): return lax.ppermute(block, ('row', 'col'), route)  12.7 us
    ppermute x14, waiting for transfers between devices, swap(): return lax.ppermute(block, 'row', route)  5.58 us
    pallas_call x1, Pallas kernels, tiles(): pl.pallas_call(multiply, out_shape=jax.ShapeDtypeStruct((1, cycles, 1, ti...  3.55 us
    ppermute x2, waiting for transfers between devices, transpose(): return lax.ppermute(block, ('row', 'col'), route)  3.25 us
    ppermute x2, starting transfers between devices, transpose(): return lax.ppermute(block, ('row', 'col'), route)  3.18 us
    pallas_call x2, Pallas kernels, columns(): pl.pallas_call(split_columns, out_shape=shape, in_specs=[smem] + [vmem] *...  1.35 us
  transfers between devices with their start and end apart: 20, of which 7 were waited for; matrix products, arithmetic and copies ran while one was open for 0% of the time, Pallas kernels for 2%

profile of v6, /device:TPU:6, one launch (start us, length us, event | category | flops | bytes accessed | tf_op | source)
XLA Modules:
  0.0 59.5 jit_solution(13945494379473719735)
XLA Ops:
  0.0 1.0 %fusion = (f32[1,128,256]{2,1,0:T(8,128)S(1)}, f32[1,128,256]{2,1,0:T(8,128)S(1)}) fusion(f32[2,128,256]{2,1,0:T(8,128)} %param.1), kind=kLoop, calls=%fused_computation.1 | loop fusion | bytes 524288 | tf_op jit(solution)/shard_map/slice | solution.py:62
  1.0 2.6 %collective-permute-start.12 = (f32[1,128,256]{2,1,0:T(8,128)S(1)}, f32[1,128,256]{2,1,0:T(8,128)S(1)}, u32[]{:S(2)}, u32[]{:S(2)}) collective-permute-start(f32[1,128,256]{2,1,0:T(8,128)S(1)} %get-tuple-element.5.refs_1_), channel_id=1, source_target_pairs={{0,8},{1,12},{2,0},{3,4},{4,9},{5,13},{6,1},{7,5},{8,10},{9,14},{1... | collective-permute-start | bytes 393224 | tf_op jit(solution)/shard_map/ppermute | solution.py:45
  3.6 0.5 collective-permute-start.4
  4.2 3.2 %collective-permute-done.12.refs_0_ = f32[1,128,256]{2,1,0:T(8,128)S(1)} collective-permute-done((f32[1,128,256]{2,1,0:T(8,128)S(1)}, f32[1,128,256]{2,1,0:T(8,128)S(1)}, u32[]{:S(2)}, u32[]{:S(2)}) %collective-permute-start.12) | collective-permute-done | bytes 131104 | tf_op jit(solution)/shard_map/ppermute | solution.py:45
  7.4 6.7 %collective-permute-start.18 = (f32[1,128,256]{2,1,0:T(8,128)S(1)}, f32[1,128,256]{2,1,0:T(8,128)S(1)}, u32[]{:S(2)}, u32[]{:S(2)}) collective-permute-start(f32[1,128,256]{2,1,0:T(8,128)S(1)} %collective-permute-done.12.refs_0_), channel_id=1, source_target_pairs={{0,24},{4,28},{8,16},{12,20},{16,8},{20,12},{24,0},{28,4},{1,25},{... | collective-permute-start | bytes 393224 | tf_op jit(solution)/shard_map/ppermute | solution.py:15
  14.1 1.8 %collective-permute-start.16 = (f32[1,128,256]{2,1,0:T(8,128)S(1)}, f32[1,128,256]{2,1,0:T(8,128)S(1)}, u32[]{:S(2)}, u32[]{:S(2)}) collective-permute-start(f32[1,128,256]{2,1,0:T(8,128)S(1)} %collective-permute-done.12.refs_0_), channel_id=1, source_target_pairs={{0,16},{4,20},{8,24},{12,28},{16,0},{20,4},{24,8},{28,12},{1,17},{... | collective-permute-start | bytes 393224 | tf_op jit(solution)/shard_map/ppermute | solution.py:15
  15.9 1.7 %collective-permute-start.10 = (f32[1,128,256]{2,1,0:T(8,128)S(1)}, f32[1,128,256]{2,1,0:T(8,128)S(1)}, u32[]{:S(2)}, u32[]{:S(2)}) collective-permute-start(f32[1,128,256]{2,1,0:T(8,128)S(1)} %collective-permute-done.4.refs_0_), channel_id=1, source_target_pairs={{0,24},{4,28},{8,16},{12,20},{16,8},{20,12},{24,0},{28,4},{1,25},{... | collective-permute-start | bytes 393224 | tf_op jit(solution)/shard_map/ppermute | solution.py:15
  17.6 0.0 collective-permute-done.18.refs_6_
  17.6 1.8 %collective-permute-start.8 = (f32[1,128,256]{2,1,0:T(8,128)S(1)}, f32[1,128,256]{2,1,0:T(8,128)S(1)}, u32[]{:S(2)}, u32[]{:S(2)}) collective-permute-start(f32[1,128,256]{2,1,0:T(8,128)S(1)} %collective-permute-done.4.refs_0_), channel_id=1, source_target_pairs={{0,16},{4,20},{8,24},{12,28},{16,0},{20,4},{24,8},{28,12},{1,17},{... | collective-permute-start | bytes 393224 | tf_op jit(solution)/shard_map/ppermute | solution.py:15
  19.4 0.0 collective-permute-done.16.refs_4_
  19.4 1.4 %collective-permute-start.6 = (f32[1,128,256]{2,1,0:T(8,128)S(1)}, f32[1,128,256]{2,1,0:T(8,128)S(1)}, u32[]{:S(2)}, u32[]{:S(2)}) collective-permute-start(f32[1,128,256]{2,1,0:T(8,128)S(1)} %collective-permute-done.4.refs_0_), channel_id=1, source_target_pairs={{0,8},{4,12},{8,0},{12,4},{16,24},{20,28},{24,16},{28,20},{1,9},{5... | collective-permute-start | bytes 393224 | tf_op jit(solution)/shard_map/ppermute | solution.py:15
  20.8 1.4 %collective-permute-done.14.refs_2_ = f32[1,128,256]{2,1,0:T(8,128)S(1)} collective-permute-done((f32[1,128,256]{2,1,0:T(8,128)S(1)}, f32[1,128,256]{2,1,0:T(8,128)S(1)}, u32[]{:S(2)}, u32[]{:S(2)}) %collective-permute-start.14) | collective-permute-done | bytes 131104 | tf_op jit(solution)/shard_map/ppermute | solution.py:15
  22.3 0.0 collective-permute-start.5
  22.3 0.0 collective-permute-done.13.refs_1_
  22.3 0.5 collective-permute-start.19
  22.8 1.2 %collective-permute-done.10.refs_6_ = f32[1,128,256]{2,1,0:T(8,128)S(1)} collective-permute-done((f32[1,128,256]{2,1,0:T(8,128)S(1)}, f32[1,128,256]{2,1,0:T(8,128)S(1)}, u32[]{:S(2)}, u32[]{:S(2)}) %collective-permute-start.10) | collective-permute-done | bytes 131104 | tf_op jit(solution)/shard_map/ppermute | solution.py:15
  24.0 1.9 %collective-permute-done.8.refs_4_ = f32[1,128,256]{2,1,0:T(8,128)S(1)} collective-permute-done((f32[1,128,256]{2,1,0:T(8,128)S(1)}, f32[1,128,256]{2,1,0:T(8,128)S(1)}, u32[]{:S(2)}, u32[]{:S(2)}) %collective-permute-start.8) | collective-permute-done | bytes 131104 | tf_op jit(solution)/shard_map/ppermute | solution.py:15
  25.8 0.0 collective-permute-start.15
  25.8 0.5 collective-permute-done.6.refs_2_
  26.3 0.0 collective-permute-start.11
  26.3 0.5 collective-permute-start.9
  26.8 3.8 %collective-permute-start = (f32[2,128,256]{2,1,0:T(8,128)}, f32[2,128,256]{2,1,0:T(8,128)S(1)}, u32[]{:S(2)}, u32[]{:S(2)}) collective-permute-start(f32[2,128,256]{2,1,0:T(8,128)} %param.1), channel_id=1, source_target_pairs={{7,4},{9,8},{10,9},{13,12},{14,13},{15,14},{16,17},{17,18},{18,19}... | collective-permute-start | bytes 786440 | tf_op jit(solution)/shard_map/ppermute | solution.py:35
  30.6 1.3 %collective-permute-start.1 = (f32[2,128,256]{2,1,0:T(8,128)}, f32[2,128,256]{2,1,0:T(8,128)S(1)}, u32[]{:S(2)}, u32[]{:S(2)}) collective-permute-start(f32[2,128,256]{2,1,0:T(8,128)} %param.1), channel_id=1, source_target_pairs={{0,2},{1,3},{4,6},{5,7},{10,8},{11,9},{14,12},{15,13},{16,18},{17,... | collective-permute-start | bytes 786440 | tf_op jit(solution)/shard_map/ppermute | solution.py:35
  32.0 0.7 %collective-permute-start.3 = (f32[2,128,256]{2,1,0:T(8,128)}, f32[2,128,256]{2,1,0:T(8,128)S(1)}, u32[]{:S(2)}, u32[]{:S(2)}) collective-permute-start(f32[2,128,256]{2,1,0:T(8,128)} %param.1), channel_id=1, source_target_pairs={{6,4},{12,14},{19,17},{22,20},{25,27},{28,30}} | collective-permute-start | bytes 786440 | tf_op jit(solution)/shard_map/ppermute | solution.py:35
  32.7 6.9 %collective-permute-start.2 = (f32[2,128,256]{2,1,0:T(8,128)}, f32[2,128,256]{2,1,0:T(8,128)S(1)}, u32[]{:S(2)}, u32[]{:S(2)}) collective-permute-start(f32[2,128,256]{2,1,0:T(8,128)} %param.1), channel_id=1, source_target_pairs={{5,4},{8,9},{11,8},{12,13},{13,14},{15,12},{16,19},{18,17},{19,18}... | collective-permute-start | bytes 786440 | tf_op jit(solution)/shard_map/ppermute | solution.py:35
  39.6 0.1 collective-permute-start.7
  39.7 0.1 pad_add_fusion.position
  39.7 0.7 %shard_map.18.refs_7_ = bf16[2,512,512]{2,1,0:T(8,128)(2,1)S(1)} custom-call(s32[2]{0:T(128)S(1)} %pad_add_fusion.position, f32[1,128,256]{2,1,0:T(8,128)S(1)} %collective-permute-done.12.refs_0_, f32[1,128,256]{2,1,0:T(8,128)S(1)} %collective-permute-done.13.refs_1_, f32[1,128,256]{2,1,0:T(8,128)S(1)} %collective-permute-done.14.refs_2_, ...), custom_call_target="tpu_custom_call" | custom-call | flops 1048576 | bytes 2097152 | tf_op jit(solution)/shard_map/pallas_call | solution.py:101
  40.4 0.6 collective-permute-done.7.refs_3_
  41.0 0.7 %shard_map.17.refs_6_ = bf16[2,512,512]{2,1,0:T(8,128)(2,1)S(1)} custom-call(s32[2]{0:T(128)S(1)} %pad_add_fusion.position, f32[1,128,256]{2,1,0:T(8,128)S(1)} %collective-permute-done.4.refs_0_, f32[1,128,256]{2,1,0:T(8,128)S(1)} %collective-permute-done.5.refs_1_, f32[1,128,256]{2,1,0:T(8,128)S(1)} %collective-permute-done.6.refs_2_, ...), custom_call_target="tpu_custom_call" | custom-call | flops 1048576 | bytes 2097152 | tf_op jit(solution)/shard_map/pallas_call | solution.py:101
  41.7 14.3 %collective-permute-done.1.refs_3_ = f32[2,128,256]{2,1,0:T(8,128)S(1)} collective-permute-done((f32[2,128,256]{2,1,0:T(8,128)}, f32[2,128,256]{2,1,0:T(8,128)S(1)}, u32[]{:S(2)}, u32[]{:S(2)}) %collective-permute-start.1) | collective-permute-done | bytes 262176 | tf_op jit(solution)/shard_map/ppermute | solution.py:35
  56.0 3.6 %shard_map.19 = f32[1,2,1,512,512]{4,3,2,1,0:T(8,128)} custom-call(s32[2]{0:T(128)S(1)} %pad_add_fusion.position, f32[1,128,256]{2,1,0:T(8,128)S(1)} %get-tuple-element.6.refs_0_, f32[1,128,256]{2,1,0:T(8,128)S(1)} %get-tuple-element.5.refs_1_, f32[2,128,256]{2,1,0:T(8,128)S(1)} %collective-permute-done.refs_2_, ...), custom_call_target="tpu_custom_call" | custom-call | flops 1610612736 | bytes 4194304 | tf_op jit(solution)/shard_map/pallas_call | solution.py:185
  (13 shorter events, 0.0 us)
Async XLA Ops:
  1.0 6.4 %collective-permute-start.12 = (f32[1,128,256]{2,1,0:T(8,128)S(1)}, f32[1,128,256]{2,1,0:T(8,128)S(1)}, u32[]{:S(2)}, u32[]{:S(2)}) collective-permute-start(f32[1,128,256]{2,1,0:T(8,128)S(1)} %get-tuple-element.5.refs_1_), channel_id=1, source_target_pairs={{0,8},{1,12},{2,0},{3,4},{4,9},{5,13},{6,1},{7,5},{8,10},{9,14},{1... | collective-permute-start | bytes 393224 | tf_op jit(solution)/shard_map/ppermute | solution.py:45
  3.6 12.3 %collective-permute-start.4 = (f32[1,128,256]{2,1,0:T(8,128)S(1)}, f32[1,128,256]{2,1,0:T(8,128)S(1)}, u32[]{:S(2)}, u32[]{:S(2)}) collective-permute-start(f32[1,128,256]{2,1,0:T(8,128)S(1)} %get-tuple-element.6.refs_0_), channel_id=1, source_target_pairs={{0,8},{1,12},{2,0},{3,4},{4,9},{5,13},{6,1},{7,5},{8,10},{9,14},{1... | collective-permute-start | bytes 393224 | tf_op jit(solution)/shard_map/ppermute | solution.py:45
  7.4 10.2 %collective-permute-start.18 = (f32[1,128,256]{2,1,0:T(8,128)S(1)}, f32[1,128,256]{2,1,0:T(8,128)S(1)}, u32[]{:S(2)}, u32[]{:S(2)}) collective-permute-start(f32[1,128,256]{2,1,0:T(8,128)S(1)} %collective-permute-done.12.refs_0_), channel_id=1, source_target_pairs={{0,24},{4,28},{8,16},{12,20},{16,8},{20,12},{24,0},{28,4},{1,25},{... | collective-permute-start | bytes 393224 | tf_op jit(solution)/shard_map/ppermute | solution.py:15
  14.1 5.3 %collective-permute-start.16 = (f32[1,128,256]{2,1,0:T(8,128)S(1)}, f32[1,128,256]{2,1,0:T(8,128)S(1)}, u32[]{:S(2)}, u32[]{:S(2)}) collective-permute-start(f32[1,128,256]{2,1,0:T(8,128)S(1)} %collective-permute-done.12.refs_0_), channel_id=1, source_target_pairs={{0,16},{4,20},{8,24},{12,28},{16,0},{20,4},{24,8},{28,12},{1,17},{... | collective-permute-start | bytes 393224 | tf_op jit(solution)/shard_map/ppermute | solution.py:15
  15.9 6.4 %collective-permute-start.14 = (f32[1,128,256]{2,1,0:T(8,128)S(1)}, f32[1,128,256]{2,1,0:T(8,128)S(1)}, u32[]{:S(2)}, u32[]{:S(2)}) collective-permute-start(f32[1,128,256]{2,1,0:T(8,128)S(1)} %collective-permute-done.12.refs_0_), channel_id=1, source_target_pairs={{0,8},{4,12},{8,0},{12,4},{16,24},{20,28},{24,16},{28,20},{1,9},{5... | collective-permute-start | bytes 393224 | tf_op jit(solution)/shard_map/ppermute | solution.py:15
  15.9 6.4 %collective-permute-start.13 = (f32[1,128,256]{2,1,0:T(8,128)S(1)}, f32[1,128,256]{2,1,0:T(8,128)S(1)}, u32[]{:S(2)}, u32[]{:S(2)}) collective-permute-start(f32[1,128,256]{2,1,0:T(8,128)S(1)} %collective-permute-done.12.refs_0_), channel_id=1, source_target_pairs={{0,4},{4,0},{8,12},{12,8},{16,20},{20,16},{24,28},{28,24},{1,5},{5... | collective-permute-start | bytes 393224 | tf_op jit(solution)/shard_map/ppermute | solution.py:15
  15.9 8.0 %collective-permute-start.10 = (f32[1,128,256]{2,1,0:T(8,128)S(1)}, f32[1,128,256]{2,1,0:T(8,128)S(1)}, u32[]{:S(2)}, u32[]{:S(2)}) collective-permute-start(f32[1,128,256]{2,1,0:T(8,128)S(1)} %collective-permute-done.4.refs_0_), channel_id=1, source_target_pairs={{0,24},{4,28},{8,16},{12,20},{16,8},{20,12},{24,0},{28,4},{1,25},{... | collective-permute-start | bytes 393224 | tf_op jit(solution)/shard_map/ppermute | solution.py:15
  17.6 8.2 %collective-permute-start.8 = (f32[1,128,256]{2,1,0:T(8,128)S(1)}, f32[1,128,256]{2,1,0:T(8,128)S(1)}, u32[]{:S(2)}, u32[]{:S(2)}) collective-permute-start(f32[1,128,256]{2,1,0:T(8,128)S(1)} %collective-permute-done.4.refs_0_), channel_id=1, source_target_pairs={{0,16},{4,20},{8,24},{12,28},{16,0},{20,4},{24,8},{28,12},{1,17},{... | collective-permute-start | bytes 393224 | tf_op jit(solution)/shard_map/ppermute | solution.py:15
  19.4 6.9 %collective-permute-start.6 = (f32[1,128,256]{2,1,0:T(8,128)S(1)}, f32[1,128,256]{2,1,0:T(8,128)S(1)}, u32[]{:S(2)}, u32[]{:S(2)}) collective-permute-start(f32[1,128,256]{2,1,0:T(8,128)S(1)} %collective-permute-done.4.refs_0_), channel_id=1, source_target_pairs={{0,8},{4,12},{8,0},{12,4},{16,24},{20,28},{24,16},{28,20},{1,9},{5... | collective-permute-start | bytes 393224 | tf_op jit(solution)/shard_map/ppermute | solution.py:15
  22.3 4.1 %collective-permute-start.5 = (f32[1,128,256]{2,1,0:T(8,128)S(1)}, f32[1,128,256]{2,1,0:T(8,128)S(1)}, u32[]{:S(2)}, u32[]{:S(2)}) collective-permute-start(f32[1,128,256]{2,1,0:T(8,128)S(1)} %collective-permute-done.4.refs_0_), channel_id=1, source_target_pairs={{0,4},{4,0},{8,12},{12,8},{16,20},{20,16},{24,28},{28,24},{1,5},{5... | collective-permute-start | bytes 393224 | tf_op jit(solution)/shard_map/ppermute | solution.py:15
  22.3 4.6 %collective-permute-start.19 = (f32[1,128,256]{2,1,0:T(8,128)S(1)}, f32[1,128,256]{2,1,0:T(8,128)S(1)}, u32[]{:S(2)}, u32[]{:S(2)}) collective-permute-start(f32[1,128,256]{2,1,0:T(8,128)S(1)} %collective-permute-done.18.refs_6_), channel_id=1, source_target_pairs={{0,4},{4,0},{8,12},{12,8},{16,20},{20,16},{24,28},{28,24},{1,5},{5... | collective-permute-start | bytes 393224 | tf_op jit(solution)/shard_map/ppermute | solution.py:15
  24.0 6.7 %collective-permute-start.17 = (f32[1,128,256]{2,1,0:T(8,128)S(1)}, f32[1,128,256]{2,1,0:T(8,128)S(1)}, u32[]{:S(2)}, u32[]{:S(2)}) collective-permute-start(f32[1,128,256]{2,1,0:T(8,128)S(1)} %collective-permute-done.16.refs_4_), channel_id=1, source_target_pairs={{0,4},{4,0},{8,12},{12,8},{16,20},{20,16},{24,28},{28,24},{1,5},{5... | collective-permute-start | bytes 393224 | tf_op jit(solution)/shard_map/ppermute | solution.py:15
  25.8 6.1 %collective-permute-start.15 = (f32[1,128,256]{2,1,0:T(8,128)S(1)}, f32[1,128,256]{2,1,0:T(8,128)S(1)}, u32[]{:S(2)}, u32[]{:S(2)}) collective-permute-start(f32[1,128,256]{2,1,0:T(8,128)S(1)} %collective-permute-done.14.refs_2_), channel_id=1, source_target_pairs={{0,4},{4,0},{8,12},{12,8},{16,20},{20,16},{24,28},{28,24},{1,5},{5... | collective-permute-start | bytes 393224 | tf_op jit(solution)/shard_map/ppermute | solution.py:15
  26.3 6.3 %collective-permute-start.11 = (f32[1,128,256]{2,1,0:T(8,128)S(1)}, f32[1,128,256]{2,1,0:T(8,128)S(1)}, u32[]{:S(2)}, u32[]{:S(2)}) collective-permute-start(f32[1,128,256]{2,1,0:T(8,128)S(1)} %collective-permute-done.10.refs_6_), channel_id=1, source_target_pairs={{0,4},{4,0},{8,12},{12,8},{16,20},{20,16},{24,28},{28,24},{1,5},{5... | collective-permute-start | bytes 393224 | tf_op jit(solution)/shard_map/ppermute | solution.py:15
  26.3 13.2 %collective-permute-start.9 = (f32[1,128,256]{2,1,0:T(8,128)S(1)}, f32[1,128,256]{2,1,0:T(8,128)S(1)}, u32[]{:S(2)}, u32[]{:S(2)}) collective-permute-start(f32[1,128,256]{2,1,0:T(8,128)S(1)} %collective-permute-done.8.refs_4_), channel_id=1, source_target_pairs={{0,4},{4,0},{8,12},{12,8},{16,20},{20,16},{24,28},{28,24},{1,5},{5... | collective-permute-start | bytes 393224 | tf_op jit(solution)/shard_map/ppermute | solution.py:15
  26.8 14.8 %collective-permute-start = (f32[2,128,256]{2,1,0:T(8,128)}, f32[2,128,256]{2,1,0:T(8,128)S(1)}, u32[]{:S(2)}, u32[]{:S(2)}) collective-permute-start(f32[2,128,256]{2,1,0:T(8,128)} %param.1), channel_id=1, source_target_pairs={{7,4},{9,8},{10,9},{13,12},{14,13},{15,14},{16,17},{17,18},{18,19}... | collective-permute-start | bytes 786440 | tf_op jit(solution)/shard_map/ppermute | solution.py:35
  30.6 25.3 %collective-permute-start.1 = (f32[2,128,256]{2,1,0:T(8,128)}, f32[2,128,256]{2,1,0:T(8,128)S(1)}, u32[]{:S(2)}, u32[]{:S(2)}) collective-permute-start(f32[2,128,256]{2,1,0:T(8,128)} %param.1), channel_id=1, source_target_pairs={{0,2},{1,3},{4,6},{5,7},{10,8},{11,9},{14,12},{15,13},{16,18},{17,... | collective-permute-start | bytes 786440 | tf_op jit(solution)/shard_map/ppermute | solution.py:35
  32.0 24.0 %collective-permute-start.3 = (f32[2,128,256]{2,1,0:T(8,128)}, f32[2,128,256]{2,1,0:T(8,128)S(1)}, u32[]{:S(2)}, u32[]{:S(2)}) collective-permute-start(f32[2,128,256]{2,1,0:T(8,128)} %param.1), channel_id=1, source_target_pairs={{6,4},{12,14},{19,17},{22,20},{25,27},{28,30}} | collective-permute-start | bytes 786440 | tf_op jit(solution)/shard_map/ppermute | solution.py:35
  32.7 23.3 %collective-permute-start.2 = (f32[2,128,256]{2,1,0:T(8,128)}, f32[2,128,256]{2,1,0:T(8,128)S(1)}, u32[]{:S(2)}, u32[]{:S(2)}) collective-permute-start(f32[2,128,256]{2,1,0:T(8,128)} %param.1), channel_id=1, source_target_pairs={{5,4},{8,9},{11,8},{12,13},{13,14},{15,12},{16,19},{18,17},{19,18}... | collective-permute-start | bytes 786440 | tf_op jit(solution)/shard_map/ppermute | solution.py:35
  39.6 1.4 %collective-permute-start.7 = (f32[1,128,256]{2,1,0:T(8,128)S(1)}, f32[1,128,256]{2,1,0:T(8,128)S(1)}, u32[]{:S(2)}, u32[]{:S(2)}) collective-permute-start(f32[1,128,256]{2,1,0:T(8,128)S(1)} %collective-permute-done.6.refs_2_), channel_id=1, source_target_pairs={{0,4},{4,0},{8,12},{12,8},{16,20},{20,16},{24,28},{28,24},{1,5},{5... | collective-permute-start | bytes 393224 | tf_op jit(solution)/shard_map/ppermute | solution.py:15

commit v7 on v6

--- a/solution.py
+++ b/solution.py
@@ -109,7 +109,29 @@
             ),
         )(position, *[pieces[distance] for distance in range(rows)])
 
-    split_parts = [columns(pieces) for pieces in held]
+    def split_row(position, distance, source, rows_of):
+        back = jnp.where(lax.rem(position[0], cols) < cols // 2, cols - distance, distance)
+        start = lax.rem(position[1] + back, cols) * depth
+        for panel in range(panels):
+            split(source(panel), rows_of, ROW_ORDER, panel // half, start, panel % half)
+
+    def second_columns(position, *refs):
+        split_row(position, 0, lambda panel: refs[panel // half][panel % half], refs[rows + 3])
+        split_columns(position, *refs[2 : rows + 3])
+
+    split_shape = jax.ShapeDtypeStruct((cycles, tile, len(COL_ORDER) * lanes), jnp.bfloat16)
+    rows_shape = jax.ShapeDtypeStruct((2, tile, len(ROW_ORDER) * lanes), jnp.bfloat16)
+    first_half = columns(held[0])
+    second_half, own_rows = pl.pallas_call(
+        second_columns,
+        out_shape=(split_shape, rows_shape),
+        in_specs=[smem] + [vmem] * (rows + 2),
+        out_specs=(vmem, vmem),
+        compiler_params=params,
+        cost_estimate=pl.CostEstimate(
+            flops=4 * cycles * tile * lanes, bytes_accessed=8 * cycles * tile * lanes, transcendentals=0
+        ),
+    )(position, *parts, *[held[1][distance] for distance in range(rows)])
 
     chunks = 2
     chunk = tile // chunks
@@ -120,9 +142,9 @@
         )
 
     def multiply(position, *refs):
-        own, blocks, refs = refs[:2], refs[2 : 2 + len(near)], refs[2 + len(near) :]
+        blocks, refs = refs[: len(near)], refs[len(near) :]
         columns_of = refs[:2]
-        out, rows_of, stage, sems = refs[2:]
+        out, rows_of, stage, sems = refs[3:]
         row, col = position[0], position[1]
         own_turn = row // cols
         diagonal = row - own_turn * cols == col
@@ -153,15 +175,15 @@
 
         @pl.when(jnp.logical_not(diagonal))
         def _():
-            ahead = lax.rem(row, cols) < cols // 2
-            for distance in range(cols):
-                back = jnp.where(ahead, cols - distance, distance)
-                start = lax.rem(col + back, cols) * depth
-                for panel in range(panels):
-                    source = blocks[distance - 1][panel] if distance else own[panel // half][panel % half]
+            for distance in range(1, cols):
+
+                def source(panel):
+                    value = blocks[distance - 1][panel]
                     if distance in halved:
-                        source += blocks[cols - 3 + distance][panel]
-                    split(source, rows_of, ROW_ORDER, panel // half, start, panel % half)
+                        value += blocks[cols - 3 + distance][panel]
+                    return value
+
+                split_row(position, distance, source, rows_of)
 
         for turn in range(cycles):
 
@@ -181,14 +203,13 @@
             for part in range(chunks):
                 copy(turn, part).wait()
 
-    half_rows = pltpu.VMEM((2, tile, len(ROW_ORDER) * lanes), jnp.bfloat16)
     return pl.pallas_call(
         multiply,
-        out_shape=jax.ShapeDtypeStruct((1, cycles, 1, tile, tile), jnp.float32),
-        in_specs=[smem] + [vmem] * (len(near) + 4),
-        out_specs=pl.BlockSpec(memory_space=pl.ANY),
+        out_shape=(jax.ShapeDtypeStruct((1, cycles, 1, tile, tile), jnp.float32), rows_shape),
+        in_specs=[smem] + [vmem] * (len(near) + 3),
+        out_specs=(pl.BlockSpec(memory_space=pl.ANY), vmem),
+        input_output_aliases={len(near) + 3: 1},
         scratch_shapes=[
-            half_rows,
             pltpu.VMEM((cycles, tile, tile), jnp.float32),
             pltpu.SemaphoreType.DMA((cycles, chunks)),
         ],
@@ -198,7 +219,7 @@
             bytes_accessed=8 * cycles * tile * tile,
             transcendentals=0,
         ),
-    )(position, *parts, *near, *split_parts)
+    )(position, *near, first_half, second_half, own_rows)[0]
 
 
 def solution(mesh):

time: 59.7 us -> 58.7 us (0.983)
  the two profiles are of different devices: /device:TPU:6 before, /device:TPU:15 now
where the time goes in v7:
time: 58.7 us; the launch traced here: 58.5 us
  waiting for transfers between devices  31.8 us (54%)
  starting transfers between devices  20.6 us (35%)
  Pallas kernels  4.89 us (8%)
  local copies, waits for them, and re-layouts  0.99 us (2%)
    ppermute x4, waiting for transfers between devices, shift(): return lax.ppermute(block, ('row', 'col'), route)  15.8 us
    ppermute x14, starting transfers between devices, swap(): return lax.ppermute(block, 'row', route)  10.8 us
    ppermute x2, waiting for transfers between devices, transpose(): return lax.ppermute(block, ('row', 'col'), route)  8.68 us
    ppermute x14, waiting for transfers between devices, swap(): return lax.ppermute(block, 'row', route)  7.35 us
    ppermute x4, starting transfers between devices, shift(): return lax.ppermute(block, ('row', 'col'), route)  7.25 us
    pallas_call x1, Pallas kernels, tiles(): pl.pallas_call(multiply, out_shape=(jax.ShapeDtypeStruct((1, cycles, 1, t...  3.52 us
    ppermute x2, starting transfers between devices, transpose(): return lax.ppermute(block, ('row', 'col'), route)  2.62 us
  transfers between devices with their start and end apart: 20, of which 9 were waited for; matrix products, arithmetic and copies ran while one was open for 0% of the time, Pallas kernels for 2%

profile of v7, /device:TPU:15, one launch (start us, length us, event | category | flops | bytes accessed | tf_op | source)
XLA Modules:
  0.0 58.5 jit_solution(1802645240725429888)
XLA Ops:
  0.0 1.0 %fusion = (f32[1,128,256]{2,1,0:T(8,128)S(1)}, f32[1,128,256]{2,1,0:T(8,128)S(1)}) fusion(f32[2,128,256]{2,1,0:T(8,128)} %param.1), kind=kLoop, calls=%fused_computation.1 | loop fusion | bytes 524288 | tf_op jit(solution)/shard_map/slice | solution.py:62
  1.0 2.4 %collective-permute-start.12 = (f32[1,128,256]{2,1,0:T(8,128)S(1)}, f32[1,128,256]{2,1,0:T(8,128)S(1)}, u32[]{:S(2)}, u32[]{:S(2)}) collective-permute-start(f32[1,128,256]{2,1,0:T(8,128)S(1)} %get-tuple-element.11.refs_1_), channel_id=1, source_target_pairs={{0,8},{1,12},{2,0},{3,4},{4,9},{5,13},{6,1},{7,5},{8,10},{9,14},{1... | collective-permute-start | bytes 393224 | tf_op jit(solution)/shard_map/ppermute | solution.py:45
  3.4 0.3 collective-permute-start.4
  3.6 8.7 %collective-permute-done.12.refs_2_ = f32[1,128,256]{2,1,0:T(8,128)S(1)} collective-permute-done((f32[1,128,256]{2,1,0:T(8,128)S(1)}, f32[1,128,256]{2,1,0:T(8,128)S(1)}, u32[]{:S(2)}, u32[]{:S(2)}) %collective-permute-start.12) | collective-permute-done | bytes 131104 | tf_op jit(solution)/shard_map/ppermute | solution.py:45
  12.3 0.2 collective-permute-start.16
  12.5 2.4 %collective-permute-start.14 = (f32[1,128,256]{2,1,0:T(8,128)S(1)}, f32[1,128,256]{2,1,0:T(8,128)S(1)}, u32[]{:S(2)}, u32[]{:S(2)}) collective-permute-start(f32[1,128,256]{2,1,0:T(8,128)S(1)} %collective-permute-done.12.refs_2_), channel_id=1, source_target_pairs={{0,8},{4,12},{8,0},{12,4},{16,24},{20,28},{24,16},{28,20},{1,9},{5... | collective-permute-start | bytes 393224 | tf_op jit(solution)/shard_map/ppermute | solution.py:15
  14.9 0.4 collective-permute-start.13
  15.3 1.4 %collective-permute-start.10 = (f32[1,128,256]{2,1,0:T(8,128)S(1)}, f32[1,128,256]{2,1,0:T(8,128)S(1)}, u32[]{:S(2)}, u32[]{:S(2)}) collective-permute-start(f32[1,128,256]{2,1,0:T(8,128)S(1)} %collective-permute-done.4.refs_0_), channel_id=1, source_target_pairs={{0,24},{4,28},{8,16},{12,20},{16,8},{20,12},{24,0},{28,4},{1,25},{... | collective-permute-start | bytes 393224 | tf_op jit(solution)/shard_map/ppermute | solution.py:15
  16.7 2.0 %collective-permute-done.18.refs_8_ = f32[1,128,256]{2,1,0:T(8,128)S(1)} collective-permute-done((f32[1,128,256]{2,1,0:T(8,128)S(1)}, f32[1,128,256]{2,1,0:T(8,128)S(1)}, u32[]{:S(2)}, u32[]{:S(2)}) %collective-permute-start.18) | collective-permute-done | bytes 131104 | tf_op jit(solution)/shard_map/ppermute | solution.py:15
  18.7 0.2 collective-permute-start.8
  18.9 0.7 %collective-permute-done.16.refs_6_ = f32[1,128,256]{2,1,0:T(8,128)S(1)} collective-permute-done((f32[1,128,256]{2,1,0:T(8,128)S(1)}, f32[1,128,256]{2,1,0:T(8,128)S(1)}, u32[]{:S(2)}, u32[]{:S(2)}) %collective-permute-start.16) | collective-permute-done | bytes 131104 | tf_op jit(solution)/shard_map/ppermute | solution.py:15
  19.6 0.7 %collective-permute-start.6 = (f32[1,128,256]{2,1,0:T(8,128)S(1)}, f32[1,128,256]{2,1,0:T(8,128)S(1)}, u32[]{:S(2)}, u32[]{:S(2)}) collective-permute-start(f32[1,128,256]{2,1,0:T(8,128)S(1)} %collective-permute-done.4.refs_0_), channel_id=1, source_target_pairs={{0,8},{4,12},{8,0},{12,4},{16,24},{20,28},{24,16},{28,20},{1,9},{5... | collective-permute-start | bytes 393224 | tf_op jit(solution)/shard_map/ppermute | solution.py:15
  20.3 0.1 collective-permute-done.14.refs_4_
  20.5 1.5 %collective-permute-start.5 = (f32[1,128,256]{2,1,0:T(8,128)S(1)}, f32[1,128,256]{2,1,0:T(8,128)S(1)}, u32[]{:S(2)}, u32[]{:S(2)}) collective-permute-start(f32[1,128,256]{2,1,0:T(8,128)S(1)} %collective-permute-done.4.refs_0_), channel_id=1, source_target_pairs={{0,4},{4,0},{8,12},{12,8},{16,20},{20,16},{24,28},{28,24},{1,5},{5... | collective-permute-start | bytes 393224 | tf_op jit(solution)/shard_map/ppermute | solution.py:15
  22.0 0.1 collective-permute-start.19
  22.1 2.3 %collective-permute-done.10.refs_6_ = f32[1,128,256]{2,1,0:T(8,128)S(1)} collective-permute-done((f32[1,128,256]{2,1,0:T(8,128)S(1)}, f32[1,128,256]{2,1,0:T(8,128)S(1)}, u32[]{:S(2)}, u32[]{:S(2)}) %collective-permute-start.10) | collective-permute-done | bytes 131104 | tf_op jit(solution)/shard_map/ppermute | solution.py:15
  24.4 0.5 collective-permute-start.17
  24.8 2.0 %collective-permute-done.8.refs_4_ = f32[1,128,256]{2,1,0:T(8,128)S(1)} collective-permute-done((f32[1,128,256]{2,1,0:T(8,128)S(1)}, f32[1,128,256]{2,1,0:T(8,128)S(1)}, u32[]{:S(2)}, u32[]{:S(2)}) %collective-permute-start.8) | collective-permute-done | bytes 131104 | tf_op jit(solution)/shard_map/ppermute | solution.py:15
  26.8 0.6 %collective-permute-start.11 = (f32[1,128,256]{2,1,0:T(8,128)S(1)}, f32[1,128,256]{2,1,0:T(8,128)S(1)}, u32[]{:S(2)}, u32[]{:S(2)}) collective-permute-start(f32[1,128,256]{2,1,0:T(8,128)S(1)} %collective-permute-done.10.refs_6_), channel_id=1, source_target_pairs={{0,4},{4,0},{8,12},{12,8},{16,20},{20,16},{24,28},{28,24},{1,5},{5... | collective-permute-start | bytes 393224 | tf_op jit(solution)/shard_map/ppermute | solution.py:15
  27.4 0.5 collective-permute-start.7
  27.9 1.9 %collective-permute-start.2 = (f32[2,128,256]{2,1,0:T(8,128)}, f32[2,128,256]{2,1,0:T(8,128)S(1)}, u32[]{:S(2)}, u32[]{:S(2)}) collective-permute-start(f32[2,128,256]{2,1,0:T(8,128)} %param.1), channel_id=1, source_target_pairs={{5,4},{8,9},{11,8},{12,13},{13,14},{15,12},{16,19},{18,17},{19,18}... | collective-permute-start | bytes 786440 | tf_op jit(solution)/shard_map/ppermute | solution.py:35
  29.9 1.3 %collective-permute-start.1 = (f32[2,128,256]{2,1,0:T(8,128)}, f32[2,128,256]{2,1,0:T(8,128)S(1)}, u32[]{:S(2)}, u32[]{:S(2)}) collective-permute-start(f32[2,128,256]{2,1,0:T(8,128)} %param.1), channel_id=1, source_target_pairs={{0,2},{1,3},{4,6},{5,7},{10,8},{11,9},{14,12},{15,13},{16,18},{17,... | collective-permute-start | bytes 786440 | tf_op jit(solution)/shard_map/ppermute | solution.py:35
  31.2 3.4 %collective-permute-start = (f32[2,128,256]{2,1,0:T(8,128)}, f32[2,128,256]{2,1,0:T(8,128)S(1)}, u32[]{:S(2)}, u32[]{:S(2)}) collective-permute-start(f32[2,128,256]{2,1,0:T(8,128)} %param.1), channel_id=1, source_target_pairs={{7,4},{9,8},{10,9},{13,12},{14,13},{15,14},{16,17},{17,18},{18,19}... | collective-permute-start | bytes 786440 | tf_op jit(solution)/shard_map/ppermute | solution.py:35
  34.6 0.7 %collective-permute-start.3 = (f32[2,128,256]{2,1,0:T(8,128)}, f32[2,128,256]{2,1,0:T(8,128)S(1)}, u32[]{:S(2)}, u32[]{:S(2)}) collective-permute-start(f32[2,128,256]{2,1,0:T(8,128)} %param.1), channel_id=1, source_target_pairs={{6,4},{12,14},{19,17},{22,20},{25,27},{28,30}} | collective-permute-start | bytes 786440 | tf_op jit(solution)/shard_map/ppermute | solution.py:35
  35.3 2.2 %collective-permute-start.15 = (f32[1,128,256]{2,1,0:T(8,128)S(1)}, f32[1,128,256]{2,1,0:T(8,128)S(1)}, u32[]{:S(2)}, u32[]{:S(2)}) collective-permute-start(f32[1,128,256]{2,1,0:T(8,128)S(1)} %collective-permute-done.14.refs_4_), channel_id=1, source_target_pairs={{0,4},{4,0},{8,12},{12,8},{16,20},{20,16},{24,28},{28,24},{1,5},{5... | collective-permute-start | bytes 393224 | tf_op jit(solution)/shard_map/ppermute | solution.py:15
  37.5 0.1 pad_add_fusion.position
  37.6 0.7 %shard_map.17.refs_4_ = bf16[2,512,512]{2,1,0:T(8,128)(2,1)S(1)} custom-call(s32[2]{0:T(128)S(1)} %pad_add_fusion.position, f32[1,128,256]{2,1,0:T(8,128)S(1)} %collective-permute-done.4.refs_0_, f32[1,128,256]{2,1,0:T(8,128)S(1)} %collective-permute-done.5.refs_1_, f32[1,128,256]{2,1,0:T(8,128)S(1)} %collective-permute-done.6.refs_2_, ...), custom_call_target="tpu_custom_call" | custom-call | flops 1048576 | bytes 2097152 | tf_op jit(solution)/shard_map/pallas_call | solution.py:101
  38.3 0.2 collective-permute-done.15.refs_5_
  38.5 0.7 %shard_map.18 = (bf16[2,512,512]{2,1,0:T(8,128)(2,1)S(1)}, bf16[2,512,512]{2,1,0:T(8,128)(2,1)S(1)}) custom-call(s32[2]{0:T(128)S(1)} %pad_add_fusion.position, f32[1,128,256]{2,1,0:T(8,128)S(1)} %get-tuple-element.12.refs_0_, f32[1,128,256]{2,1,0:T(8,128)S(1)} %get-tuple-element.11.refs_1_, f32[1,128,256]{2,1,0:T(8,128)S(1)} %collective-permute-done.12.refs_2_, ...), custom_call_target="tpu_custom_call" | custom-call | flops 1048576 | bytes 2097152 | tf_op jit(solution)/shard_map/pallas_call | solution.py:125
  39.2 3.7 %collective-permute-done.1.refs_1_ = f32[2,128,256]{2,1,0:T(8,128)S(1)} collective-permute-done((f32[2,128,256]{2,1,0:T(8,128)}, f32[2,128,256]{2,1,0:T(8,128)S(1)}, u32[]{:S(2)}, u32[]{:S(2)}) %collective-permute-start.1) | collective-permute-done | bytes 262176 | tf_op jit(solution)/shard_map/ppermute | solution.py:35
  42.9 12.1 %collective-permute-done.refs_0_ = f32[2,128,256]{2,1,0:T(8,128)S(1)} collective-permute-done((f32[2,128,256]{2,1,0:T(8,128)}, f32[2,128,256]{2,1,0:T(8,128)S(1)}, u32[]{:S(2)}, u32[]{:S(2)}) %collective-permute-start) | collective-permute-done | bytes 262176 | tf_op jit(solution)/shard_map/ppermute | solution.py:35
  55.0 3.5 %shard_map.19 = (f32[1,2,1,512,512]{4,3,2,1,0:T(8,128)}, bf16[2,512,512]{2,1,0:T(8,128)(2,1)S(1)}) custom-call(s32[2]{0:T(128)S(1)} %pad_add_fusion.position, f32[2,128,256]{2,1,0:T(8,128)S(1)} %collective-permute-done.refs_0_, f32[2,128,256]{2,1,0:T(8,128)S(1)} %collective-permute-done.1.refs_1_, ...), custom_call_target="tpu_custom_call", output_to_operand_aliasing={{1}: (7, {})} | custom-call | flops 1610612736 | bytes 4194304 | tf_op jit(solution)/shard_map/pallas_call | solution.py:206
  (13 shorter events, 0.0 us)
Async XLA Ops:
  1.0 11.3 %collective-permute-start.12 = (f32[1,128,256]{2,1,0:T(8,128)S(1)}, f32[1,128,256]{2,1,0:T(8,128)S(1)}, u32[]{:S(2)}, u32[]{:S(2)}) collective-permute-start(f32[1,128,256]{2,1,0:T(8,128)S(1)} %get-tuple-element.11.refs_1_), channel_id=1, source_target_pairs={{0,8},{1,12},{2,0},{3,4},{4,9},{5,13},{6,1},{7,5},{8,10},{9,14},{1... | collective-permute-start | bytes 393224 | tf_op jit(solution)/shard_map/ppermute | solution.py:45
  3.4 11.9 %collective-permute-start.4 = (f32[1,128,256]{2,1,0:T(8,128)S(1)}, f32[1,128,256]{2,1,0:T(8,128)S(1)}, u32[]{:S(2)}, u32[]{:S(2)}) collective-permute-start(f32[1,128,256]{2,1,0:T(8,128)S(1)} %get-tuple-element.12.refs_0_), channel_id=1, source_target_pairs={{0,8},{1,12},{2,0},{3,4},{4,9},{5,13},{6,1},{7,5},{8,10},{9,14},{1... | collective-permute-start | bytes 393224 | tf_op jit(solution)/shard_map/ppermute | solution.py:45
  12.3 6.4 %collective-permute-start.18 = (f32[1,128,256]{2,1,0:T(8,128)S(1)}, f32[1,128,256]{2,1,0:T(8,128)S(1)}, u32[]{:S(2)}, u32[]{:S(2)}) collective-permute-start(f32[1,128,256]{2,1,0:T(8,128)S(1)} %collective-permute-done.12.refs_2_), channel_id=1, source_target_pairs={{0,24},{4,28},{8,16},{12,20},{16,8},{20,12},{24,0},{28,4},{1,25},{... | collective-permute-start | bytes 393224 | tf_op jit(solution)/shard_map/ppermute | solution.py:15
  12.3 7.3 %collective-permute-start.16 = (f32[1,128,256]{2,1,0:T(8,128)S(1)}, f32[1,128,256]{2,1,0:T(8,128)S(1)}, u32[]{:S(2)}, u32[]{:S(2)}) collective-permute-start(f32[1,128,256]{2,1,0:T(8,128)S(1)} %collective-permute-done.12.refs_2_), channel_id=1, source_target_pairs={{0,16},{4,20},{8,24},{12,28},{16,0},{20,4},{24,8},{28,12},{1,17},{... | collective-permute-start | bytes 393224 | tf_op jit(solution)/shard_map/ppermute | solution.py:15
  12.5 8.0 %collective-permute-start.14 = (f32[1,128,256]{2,1,0:T(8,128)S(1)}, f32[1,128,256]{2,1,0:T(8,128)S(1)}, u32[]{:S(2)}, u32[]{:S(2)}) collective-permute-start(f32[1,128,256]{2,1,0:T(8,128)S(1)} %collective-permute-done.12.refs_2_), channel_id=1, source_target_pairs={{0,8},{4,12},{8,0},{12,4},{16,24},{20,28},{24,16},{28,20},{1,9},{5... | collective-permute-start | bytes 393224 | tf_op jit(solution)/shard_map/ppermute | solution.py:15
  14.9 7.1 %collective-permute-start.13 = (f32[1,128,256]{2,1,0:T(8,128)S(1)}, f32[1,128,256]{2,1,0:T(8,128)S(1)}, u32[]{:S(2)}, u32[]{:S(2)}) collective-permute-start(f32[1,128,256]{2,1,0:T(8,128)S(1)} %collective-permute-done.12.refs_2_), channel_id=1, source_target_pairs={{0,4},{4,0},{8,12},{12,8},{16,20},{20,16},{24,28},{28,24},{1,5},{5... | collective-permute-start | bytes 393224 | tf_op jit(solution)/shard_map/ppermute | solution.py:15
  15.3 9.1 %collective-permute-start.10 = (f32[1,128,256]{2,1,0:T(8,128)S(1)}, f32[1,128,256]{2,1,0:T(8,128)S(1)}, u32[]{:S(2)}, u32[]{:S(2)}) collective-permute-start(f32[1,128,256]{2,1,0:T(8,128)S(1)} %collective-permute-done.4.refs_0_), channel_id=1, source_target_pairs={{0,24},{4,28},{8,16},{12,20},{16,8},{20,12},{24,0},{28,4},{1,25},{... | collective-permute-start | bytes 393224 | tf_op jit(solution)/shard_map/ppermute | solution.py:15
  18.7 8.1 %collective-permute-start.8 = (f32[1,128,256]{2,1,0:T(8,128)S(1)}, f32[1,128,256]{2,1,0:T(8,128)S(1)}, u32[]{:S(2)}, u32[]{:S(2)}) collective-permute-start(f32[1,128,256]{2,1,0:T(8,128)S(1)} %collective-permute-done.4.refs_0_), channel_id=1, source_target_pairs={{0,16},{4,20},{8,24},{12,28},{16,0},{20,4},{24,8},{28,12},{1,17},{... | collective-permute-start | bytes 393224 | tf_op jit(solution)/shard_map/ppermute | solution.py:15
  19.6 7.8 %collective-permute-start.6 = (f32[1,128,256]{2,1,0:T(8,128)S(1)}, f32[1,128,256]{2,1,0:T(8,128)S(1)}, u32[]{:S(2)}, u32[]{:S(2)}) collective-permute-start(f32[1,128,256]{2,1,0:T(8,128)S(1)} %collective-permute-done.4.refs_0_), channel_id=1, source_target_pairs={{0,8},{4,12},{8,0},{12,4},{16,24},{20,28},{24,16},{28,20},{1,9},{5... | collective-permute-start | bytes 393224 | tf_op jit(solution)/shard_map/ppermute | solution.py:15
  20.5 7.0 %collective-permute-start.5 = (f32[1,128,256]{2,1,0:T(8,128)S(1)}, f32[1,128,256]{2,1,0:T(8,128)S(1)}, u32[]{:S(2)}, u32[]{:S(2)}) collective-permute-start(f32[1,128,256]{2,1,0:T(8,128)S(1)} %collective-permute-done.4.refs_0_), channel_id=1, source_target_pairs={{0,4},{4,0},{8,12},{12,8},{16,20},{20,16},{24,28},{28,24},{1,5},{5... | collective-permute-start | bytes 393224 | tf_op jit(solution)/shard_map/ppermute | solution.py:15
  22.0 5.9 %collective-permute-start.19 = (f32[1,128,256]{2,1,0:T(8,128)S(1)}, f32[1,128,256]{2,1,0:T(8,128)S(1)}, u32[]{:S(2)}, u32[]{:S(2)}) collective-permute-start(f32[1,128,256]{2,1,0:T(8,128)S(1)} %collective-permute-done.18.refs_8_), channel_id=1, source_target_pairs={{0,4},{4,0},{8,12},{12,8},{16,20},{20,16},{24,28},{28,24},{1,5},{5... | collective-permute-start | bytes 393224 | tf_op jit(solution)/shard_map/ppermute | solution.py:15
  24.4 5.5 %collective-permute-start.17 = (f32[1,128,256]{2,1,0:T(8,128)S(1)}, f32[1,128,256]{2,1,0:T(8,128)S(1)}, u32[]{:S(2)}, u32[]{:S(2)}) collective-permute-start(f32[1,128,256]{2,1,0:T(8,128)S(1)} %collective-permute-done.16.refs_6_), channel_id=1, source_target_pairs={{0,4},{4,0},{8,12},{12,8},{16,20},{20,16},{24,28},{28,24},{1,5},{5... | collective-permute-start | bytes 393224 | tf_op jit(solution)/shard_map/ppermute | solution.py:15
  26.8 4.4 %collective-permute-start.11 = (f32[1,128,256]{2,1,0:T(8,128)S(1)}, f32[1,128,256]{2,1,0:T(8,128)S(1)}, u32[]{:S(2)}, u32[]{:S(2)}) collective-permute-start(f32[1,128,256]{2,1,0:T(8,128)S(1)} %collective-permute-done.10.refs_6_), channel_id=1, source_target_pairs={{0,4},{4,0},{8,12},{12,8},{16,20},{20,16},{24,28},{28,24},{1,5},{5... | collective-permute-start | bytes 393224 | tf_op jit(solution)/shard_map/ppermute | solution.py:15
  27.4 7.1 %collective-permute-start.9 = (f32[1,128,256]{2,1,0:T(8,128)S(1)}, f32[1,128,256]{2,1,0:T(8,128)S(1)}, u32[]{:S(2)}, u32[]{:S(2)}) collective-permute-start(f32[1,128,256]{2,1,0:T(8,128)S(1)} %collective-permute-done.8.refs_4_), channel_id=1, source_target_pairs={{0,4},{4,0},{8,12},{12,8},{16,20},{20,16},{24,28},{28,24},{1,5},{5... | collective-permute-start | bytes 393224 | tf_op jit(solution)/shard_map/ppermute | solution.py:15
  27.4 7.8 %collective-permute-start.7 = (f32[1,128,256]{2,1,0:T(8,128)S(1)}, f32[1,128,256]{2,1,0:T(8,128)S(1)}, u32[]{:S(2)}, u32[]{:S(2)}) collective-permute-start(f32[1,128,256]{2,1,0:T(8,128)S(1)} %collective-permute-done.6.refs_2_), channel_id=1, source_target_pairs={{0,4},{4,0},{8,12},{12,8},{16,20},{20,16},{24,28},{28,24},{1,5},{5... | collective-permute-start | bytes 393224 | tf_op jit(solution)/shard_map/ppermute | solution.py:15
  27.9 11.2 %collective-permute-start.2 = (f32[2,128,256]{2,1,0:T(8,128)}, f32[2,128,256]{2,1,0:T(8,128)S(1)}, u32[]{:S(2)}, u32[]{:S(2)}) collective-permute-start(f32[2,128,256]{2,1,0:T(8,128)} %param.1), channel_id=1, source_target_pairs={{5,4},{8,9},{11,8},{12,13},{13,14},{15,12},{16,19},{18,17},{19,18}... | collective-permute-start | bytes 786440 | tf_op jit(solution)/shard_map/ppermute | solution.py:35
  29.9 13.1 %collective-permute-start.1 = (f32[2,128,256]{2,1,0:T(8,128)}, f32[2,128,256]{2,1,0:T(8,128)S(1)}, u32[]{:S(2)}, u32[]{:S(2)}) collective-permute-start(f32[2,128,256]{2,1,0:T(8,128)} %param.1), channel_id=1, source_target_pairs={{0,2},{1,3},{4,6},{5,7},{10,8},{11,9},{14,12},{15,13},{16,18},{17,... | collective-permute-start | bytes 786440 | tf_op jit(solution)/shard_map/ppermute | solution.py:35
  31.2 23.8 %collective-permute-start = (f32[2,128,256]{2,1,0:T(8,128)}, f32[2,128,256]{2,1,0:T(8,128)S(1)}, u32[]{:S(2)}, u32[]{:S(2)}) collective-permute-start(f32[2,128,256]{2,1,0:T(8,128)} %param.1), channel_id=1, source_target_pairs={{7,4},{9,8},{10,9},{13,12},{14,13},{15,14},{16,17},{17,18},{18,19}... | collective-permute-start | bytes 786440 | tf_op jit(solution)/shard_map/ppermute | solution.py:35
  34.6 20.4 %collective-permute-start.3 = (f32[2,128,256]{2,1,0:T(8,128)}, f32[2,128,256]{2,1,0:T(8,128)S(1)}, u32[]{:S(2)}, u32[]{:S(2)}) collective-permute-start(f32[2,128,256]{2,1,0:T(8,128)} %param.1), channel_id=1, source_target_pairs={{6,4},{12,14},{19,17},{22,20},{25,27},{28,30}} | collective-permute-start | bytes 786440 | tf_op jit(solution)/shard_map/ppermute | solution.py:35
  35.3 3.2 %collective-permute-start.15 = (f32[1,128,256]{2,1,0:T(8,128)S(1)}, f32[1,128,256]{2,1,0:T(8,128)S(1)}, u32[]{:S(2)}, u32[]{:S(2)}) collective-permute-start(f32[1,128,256]{2,1,0:T(8,128)S(1)} %collective-permute-done.14.refs_4_), channel_id=1, source_target_pairs={{0,4},{4,0},{8,12},{12,8},{16,20},{20,16},{24,28},{28,24},{1,5},{5... | collective-permute-start | bytes 393224 | tf_op jit(solution)/shard_map/ppermute | solution.py:15
